TPU v7x, 32 devices: a whole 2x2x4 slice. The times are simulated.
32 devices in a mesh: group: 8 (over z, core), helper: 4 (over y, x).
Axes of the slice: x: 2, y: 2, z: 4, core: 2. Of those that a mesh axis runs over, the one named last changes fastest.
Arguments:
- candidates: bfloat16 [64, 128, 1024], P(('group', 'helper')), may hold values from -36 to 36
- block_user: int32 [64], P(('group', 'helper')), may hold values from 0 to 3, as said below
- live_rows: int32 [64], P(('group', 'helper')), may hold values from 1 to 128
- prefix_keys: bfloat16 [32, 256, 1024], P(('group', 'helper')), may hold values from -6 to 6
- prefix_values: bfloat16 [32, 256, 1024], P(('group', 'helper')), may hold values from -6 to 6
- w_proj: bfloat16 [1024, 4096], P(('group', 'helper')), may hold values from -0.1875 to 0.1875
- w_out: bfloat16 [1024, 1024], P(('group', 'helper')), may hold values from -0.1875 to 0.1875
- gain_in: float32 [1024], replicated, may hold values from 0.1 to 1.9
- gain_mid: float32 [1024], replicated, may hold values from 0.1 to 1.9
- score_vec: float32 [1024], replicated, may hold values from -0.1875 to 0.1875
Outputs:
- embeddings: bfloat16 [64, 128, 1024], P(('group', 'helper'))
- scores: float32 [64, 128], P(('group', 'helper'))
Inputs may be any that keep to these rules, and one draw needn't show every extreme that they name: `block_user`: the 2 blocks of one device name different users; in every group some user is named by a block of every device of the group.
All inputs are finite; a program needn't handle non-finite values.
Results may differ from a plain program's by a relative error of at most 0.0045.
Values may be sent and summed in bfloat16 or wider, within the bound.
No kernel may reach another device: no remote copies, remote signals or barrier semaphores. Data moves between devices by JAX's collectives and lax.ppermute only.
A program may use at most 128 MiB of HBM per device.

v0:
```python
import jax
import jax.numpy as jnp
from jax import lax
from jax.sharding import PartitionSpec as P

HEADS = 8


epsilon = 1e-05


def layer_norm(values, gain):
    average = jnp.mean(values, axis=-1, keepdims=True)
    centred = values - average
    spread = jnp.mean(centred * centred, axis=-1, keepdims=True)
    return centred * lax.rsqrt(spread + epsilon) * gain


def shards(
    candidates,
    block_user,
    live_rows,
    prefix_keys,
    prefix_values,
    w_proj,
    w_out,
    gain_in,
    gain_mid,
    score_vec,
):
    helpers = lax.axis_size("helper")
    blocks, rows_block, features = candidates.shape
    head_dim = features // HEADS
    score_scale = head_dim ** (-0.5)
    proj_full, out_full = (
        lax.all_gather(w_proj, ("group", "helper"), axis=0, tiled=True),
        lax.all_gather(w_out, ("group", "helper"), axis=0, tiled=True),
    )
    cand_rows = candidates.reshape(blocks * rows_block, features).astype(jnp.float32)
    normed = layer_norm(cand_rows, gain_in).astype(jnp.bfloat16)
    projected = jax.nn.silu(jnp.dot(normed, proj_full, preferred_element_type=jnp.float32))
    gate_portion = projected[:, :features]
    value_part = projected[:, features : 2 * features]
    query_portion = projected[:, 2 * features : 3 * features]
    key_part = projected[:, 3 * features :]
    query_bf = lax.optimization_barrier(query_portion.astype(jnp.bfloat16))
    query_heads = query_bf.astype(jnp.float32).reshape(-1, HEADS, head_dim)
    own_weight = jax.nn.silu(
        score_scale * jnp.sum(query_heads * key_part.reshape(-1, HEADS, head_dim), axis=-1)
    )
    own_term = (own_weight[..., None] * value_part.reshape(-1, HEADS, head_dim)).reshape(
        -1, features
    )
    onehot = (block_user[None, :] == jnp.arange(helpers, dtype=jnp.int32)[:, None]).astype(
        jnp.bfloat16
    )
    outgoing = jnp.dot(
        onehot, query_bf.reshape(blocks, rows_block * features), preferred_element_type=jnp.float32
    )
    outgoing = outgoing.astype(jnp.bfloat16).reshape(helpers, rows_block, features)
    per_head_keys = prefix_keys[0].reshape(-1, HEADS, head_dim)
    per_head_values = prefix_values[0].reshape(-1, HEADS, head_dim)

    def attended_row_set(query_tile_group):
        raw_scores = jnp.einsum(
            "ocy,qcy->coq", query_tile_group, per_head_keys, preferred_element_type=jnp.float32
        )
        weight_brainfloat = jax.nn.silu(score_scale * raw_scores).astype(jnp.bfloat16)
        return jnp.einsum(
            "txw,wta->xta", weight_brainfloat, per_head_values, preferred_element_type=jnp.float32
        ).astype(jnp.bfloat16)

    arrived = lax.all_to_all(outgoing, "helper", split_axis=0, concat_axis=0, tiled=True)
    arrived_shape = arrived.shape
    count_rows = arrived_shape[0] * arrived_shape[1]
    flat_query = arrived.reshape(count_rows, HEADS, head_dim)
    if count_rows > 512 and count_rows % 512 == 0:
        mixed_heads = lax.map(
            attended_row_set, flat_query.reshape(count_rows // 512, 512, HEADS, head_dim)
        )
    else:
        mixed_heads = attended_row_set(flat_query)
    returned = lax.all_to_all(
        mixed_heads.reshape(arrived_shape), "helper", split_axis=0, concat_axis=0, tiled=True
    )
    prefix_mix = jnp.einsum(
        "jb,jf->bf",
        onehot,
        returned.reshape(helpers, rows_block * features),
        preferred_element_type=jnp.float32,
    )
    mixed = prefix_mix.reshape(-1, features) + own_term
    gated = (layer_norm(mixed, gain_mid) * gate_portion).astype(jnp.bfloat16)
    updated = cand_rows + jnp.dot(gated, out_full, preferred_element_type=jnp.float32)
    embeddings = updated.astype(jnp.bfloat16).reshape(blocks, rows_block, features)
    row_scores = jnp.sum(layer_norm(updated, 1.0) * score_vec, axis=-1).reshape(blocks, rows_block)
    live_mask = jnp.arange(rows_block, dtype=jnp.int32)[None, :] < live_rows[:, None]
    scores = jnp.where(live_mask, row_scores, jnp.zeros_like(row_scores))
    return (embeddings, scores)


def solution(mesh):
    placed = (
        P(("group", "helper"), None, None),
        P(("group", "helper")),
        P(("group", "helper")),
        P(("group", "helper"), None, None),
        P(("group", "helper"), None, None),
        P(("group", "helper"), None),
        P(("group", "helper"), None),
        P(),
        P(),
        P(),
    )
    return jax.shard_map(
        shards,
        mesh=mesh,
        in_specs=placed,
        out_specs=(P(("group", "helper"), None, None), P(("group", "helper"), None)),
        check_vma=False,
    )
```

profile of v0, /device:TPU:0, one launch (start us, length us, event | category | flops | bytes accessed | tf_op | source)
XLA Modules:
  0.0 164.2 jit_solution(251757091519188598)
XLA Ops:
  7.2 0.0 all-gather.3.cloned.1.call-start
  7.2 0.7 all-gather.3.cloned.1.call-update
  7.9 0.0 all-gather.5.cloned.1.call-start
  7.9 0.7 all-gather.5.cloned.1.call-update
  8.6 1.2 convert_reduce_fusion
  9.8 1.3 multiply_reduce_fusion.3
  11.2 1.3 fusion.8
  12.5 0.0 copy-start.6
  12.5 78.1 %all-gather.3.cloned.1.call-done = bf16[1024,4096]{1,0:T(8,128)(2,1)} async-done(((bf16[32,4096]{1,0:T(8,128)(2,1)}), bf16[1024,4096]{1,0:T(8,128)(2,1)}) %all-gather.3.cloned.1.call-update) | async-done | bytes 8388624 | tf_op jit(solution)/shard_map/all_gather | solution.py:36
  90.7 5.9 %divide_multiply_fusion = f32[256,4096]{1,0:T(8,128)S(1)} fusion(bf16[256,1024]{1,0:T(8,128)(2,1)S(1)} %fusion.8, bf16[1024,4096]{1,0:T(8,128)(2,1)} %all-gather.3.cloned.1.call-done), kind=kOutput, calls=%fused_computation.2 | convolution fusion | flops 2151677952 | bytes 13107200 | tf_op jit(solution)/shard_map/dot_general | solution.py:41
  96.5 0.0 copy-start.1
  96.5 1.9 %copy-done.1 = f32[256,4096]{1,0:T(8,128)} copy-done((f32[256,4096]{1,0:T(8,128)}, f32[256,4096]{1,0:T(8,128)S(1)}, u32[]{:S(2)}) %copy-start.1) | copy-done | bytes 4194328
  98.5 0.1 slice.30
  98.5 0.4 reshape.106
  98.9 0.0 copy-done.6
  98.9 0.0 copy-start.2
  98.9 0.0 copy-start.3
  99.0 0.7 convolution_convert_fusion
  99.7 1.3 copy.47
  100.9 3.5 %all-to-all-start = ((bf16[4,128,1024]{2,1,0:T(8,128)(2,1)}), bf16[4,128,1024]{2,1,0:T(8,128)(2,1)S(1)}, u32[]{:S(2)}, u32[]{:S(2)}) async-start(bf16[4,128,1024]{2,1,0:T(8,128)(2,1)} %bitcast.46), calls=%async_computation | async-start | bytes 2097152 | tf_op jit(solution)/shard_map/all_to_all | solution.py:73
  104.5 0.0 copy-done.2
  104.5 0.1 copy.31
  104.6 0.0 copy-done.3
  104.6 0.9 copy.32
  105.5 13.3 %all-to-all-done = bf16[4,128,1024]{2,1,0:T(8,128)(2,1)S(1)} async-done(((bf16[4,128,1024]{2,1,0:T(8,128)(2,1)}), bf16[4,128,1024]{2,1,0:T(8,128)(2,1)S(1)}, u32[]{:S(2)}, u32[]{:S(2)}) %all-to-all-start) | async-done | bytes 1048608 | tf_op jit(solution)/shard_map/all_to_all | solution.py:73
  118.8 0.3 copy.30
  119.0 3.8 %fusion.2 = bf16[512,8,128]{2,0,1:T(8,128)(2,1)} fusion(bf16[512,8,128]{2,1,0:T(8,128)(2,1)S(1)} %bitcast.53, bf16[256,8,128]{2,1,0:T(8,128)(2,1)} %bitcast.59, bf16[256,8,128]{2,1,0:T(8,128)(2,1)S(1)} %bitcast.58), kind=kOutput, calls=%fused_computation.5 | convolution fusion | flops 543686656 | bytes 3145728 | tf_op jit(solution)/shard_map/txw,wta->xta/dot_general | solution.py:69
  122.9 1.9 %copy.26 = bf16[512,8,128]{2,1,0:T(8,128)(2,1)S(1)} copy(bf16[512,8,128]{2,0,1:T(8,128)(2,1)} %fusion.2) | data formatting | bytes 2097152 | tf_op jit(solution)/shard_map/convert_element_type | solution.py:71
  124.8 1.3 reshape.109
  126.1 3.7 %all-to-all-start.1 = ((bf16[4,128,1024]{2,1,0:T(8,128)(2,1)}), bf16[4,128,1024]{2,1,0:T(8,128)(2,1)S(1)}, u32[]{:S(2)}, u32[]{:S(2)}) async-start(bf16[4,128,1024]{2,1,0:T(8,128)(2,1)} %reshape.109), calls=%async_computation.1 | async-start | bytes 2097152 | tf_op jit(solution)/shard_map/all_to_all | solution.py:83
  129.8 1.4 fusion.5
  131.2 0.2 copy.34
  131.4 0.3 reduce_sum.74
  131.7 0.1 copy.27
  131.8 0.1 copy.28
  131.9 14.8 %all-to-all-done.1 = bf16[4,128,1024]{2,1,0:T(8,128)(2,1)S(1)} async-done(((bf16[4,128,1024]{2,1,0:T(8,128)(2,1)}), bf16[4,128,1024]{2,1,0:T(8,128)(2,1)S(1)}, u32[]{:S(2)}, u32[]{:S(2)}) %all-to-all-start.1) | async-done | bytes 1048608 | tf_op jit(solution)/shard_map/all_to_all | solution.py:83
  146.7 0.8 copy.33
  147.5 1.1 fusion.18
  148.6 0.0 copy-start
  148.6 0.0 copy-start.4
  148.7 0.9 reshape.111
  149.6 0.3 mul.124
  149.9 1.6 fusion.24
  151.5 0.0 copy-start.5
  151.5 0.2 multiply_reduce_fusion.2
  151.8 0.9 all-gather.5.cloned.1.call-done
  152.6 0.0 copy-done
  152.6 0.0 copy-done.4
  152.6 0.0 copy-start.7
  152.6 2.8 %fusion.26 = (f32[256]{0:T(256)S(1)}, f32[256,1024]{1,0:T(8,128)S(1)}) fusion(bf16[1024,1024]{1,0:T(8,128)(2,1)} %all-gather.5.cloned.1.call-done, f32[256,4096]{1,0:T(8,128)} %copy-done.1, f32[256,1024]{1,0:T(8,128)S(1)} %get-tuple-element.3, f32[1024]{0:T(1024)S(1)} %copy-done.4, f32[256]{0:T(256)S(1)} %add_rsqrt_fusion.1, ...), kind=kOutput, calls=%fused_computation.46 | convolution fusion | flops 538967808 | bytes 5774336 | tf_op jit(solution)/shard_map/dot_general | solution.py:94
  155.4 0.3 multiply_reduce_fusion.1
  155.7 0.0 copy-done.5
  155.7 1.1 multiply_reduce_fusion
  156.8 0.0 copy-done.7
  156.8 0.6 compare_select_fusion
  (7 shorter events, 0.1 us)
Async XLA Ops:
  7.2 83.5 %all-gather.3.cloned.1.call-start = ((), (), s32[]{:S(2)}) async-start(), calls=%async_computation.2 | async-start | bytes 8650752 | tf_op jit(solution)/shard_map/all_gather | solution.py:36
  7.9 144.7 %all-gather.5.cloned.1.call-start = ((), (), s32[]{:S(2)}) async-start(), calls=%async_computation.3 | async-start | bytes 2162688 | tf_op jit(solution)/shard_map/all_gather | solution.py:37
  12.5 86.4 %copy-start.6 = (s32[2]{0:T(128)S(1)}, s32[2]{0:T(128)}, u32[]{:S(2)}) copy-start(s32[2]{0:T(128)} %param.11) | copy-start | bytes 28
  96.5 1.9 %copy-start.1 = (f32[256,4096]{1,0:T(8,128)}, f32[256,4096]{1,0:T(8,128)S(1)}, u32[]{:S(2)}) copy-start(f32[256,4096]{1,0:T(8,128)S(1)} %divide_multiply_fusion) | copy-start | bytes 12582916
  98.9 5.5 %copy-start.2 = (bf16[1,256,1024]{2,1,0:T(8,128)(2,1)S(1)}, bf16[1,256,1024]{2,1,0:T(8,128)(2,1)}, u32[]{:S(2)}) copy-start(bf16[1,256,1024]{2,1,0:T(8,128)(2,1)} %param.13) | copy-start | bytes 1572868
  98.9 5.6 %copy-start.3 = (bf16[1,256,1024]{2,1,0:T(8,128)(2,1)S(1)}, bf16[1,256,1024]{2,1,0:T(8,128)(2,1)}, u32[]{:S(2)}) copy-start(bf16[1,256,1024]{2,1,0:T(8,128)(2,1)} %param.14) | copy-start | bytes 1572868
  100.9 17.8 %all-to-all-start = ((bf16[4,128,1024]{2,1,0:T(8,128)(2,1)}), bf16[4,128,1024]{2,1,0:T(8,128)(2,1)S(1)}, u32[]{:S(2)}, u32[]{:S(2)}) async-start(bf16[4,128,1024]{2,1,0:T(8,128)(2,1)} %bitcast.46), calls=%async_computation | async-start | bytes 2097152 | tf_op jit(solution)/shard_map/all_to_all | solution.py:73
  126.1 20.6 %all-to-all-start.1 = ((bf16[4,128,1024]{2,1,0:T(8,128)(2,1)}), bf16[4,128,1024]{2,1,0:T(8,128)(2,1)S(1)}, u32[]{:S(2)}, u32[]{:S(2)}) async-start(bf16[4,128,1024]{2,1,0:T(8,128)(2,1)} %reshape.109), calls=%async_computation.1 | async-start | bytes 2097152 | tf_op jit(solution)/shard_map/all_to_all | solution.py:83
  148.6 4.0 %copy-start = (bf16[2,128,1024]{2,1,0:T(8,128)(2,1)S(1)}, bf16[2,128,1024]{2,1,0:T(8,128)(2,1)}, u32[]{:S(2)}) copy-start(bf16[2,128,1024]{2,1,0:T(8,128)(2,1)} %param.10) | copy-start | bytes 1572868
  148.6 4.0 %copy-start.4 = (f32[1024]{0:T(1024)S(1)}, f32[1024]{0:T(1024)}, u32[]{:S(2)}) copy-start(f32[1024]{0:T(1024)} %param.18) | copy-start | bytes 12292
  151.5 4.2 %copy-start.5 = (f32[1024]{0:T(1024)S(1)}, f32[1024]{0:T(1024)}, u32[]{:S(2)}) copy-start(f32[1024]{0:T(1024)} %param.19) | copy-start | bytes 12292
  152.6 4.1 %copy-start.7 = (s32[2]{0:T(128)S(1)}, s32[2]{0:T(128)}, u32[]{:S(2)}) copy-start(s32[2]{0:T(128)} %param.12) | copy-start | bytes 28
Sparse Core Ops, SparseCore 0:
  10.8 79.7 all-gather.2
  93.5 59.0 all-gather.4
where the time goes:
time: 165 us; the launch traced here: 164 us
  waiting for transfers between devices  108 us (65%)
  matrix products  14.3 us (9%)
  between operations  14.3 us (9%)
  local copies, waits for them, and re-layouts  10.6 us (6%)
  other arithmetic  9.38 us (6%)
  starting transfers between devices  7.29 us (4%)
    all_gather x1, waiting for transfers between devices, shards(): lax.all_gather(w_proj, ('group', 'helper'), axis=0, tiled=True)  78.1 us
    all_to_all x1, waiting for transfers between devices, shards(): lax.all_to_all(mixed_heads.reshape(arrived_shape), 'helper', split_axis=0...  14.8 us
    all_to_all x1, waiting for transfers between devices, shards(): lax.all_to_all(outgoing, 'helper', split_axis=0, concat_axis=0, tiled=True)  13.3 us
    dot_general x1, matrix products, shards(): jnp.dot(normed, proj_full, preferred_element_type=jnp.float32)  5.86 us
    unnamed x22, local copies, waits for them, and re-layouts  5.51 us
    dot_general x1, matrix products, attended_row_set(): jnp.einsum('txw,wta->xta', weight_brainfloat, per_head_values, preferred_...  3.85 us
    all_to_all x1, starting transfers between devices, shards(): lax.all_to_all(mixed_heads.reshape(arrived_shape), 'helper', split_axis=0...  3.7 us
    all_to_all x1, starting transfers between devices, shards(): lax.all_to_all(outgoing, 'helper', split_axis=0, concat_axis=0, tiled=True)  3.51 us
  transfers between devices with their start and end apart: 4, of which 4 were waited for; matrix products, arithmetic and copies ran while one was open for 17% of the time, Pallas kernels for 0%

commit v1 on v0

--- a/solution.py
+++ b/solution.py
@@ -1,9 +1,13 @@
 import jax
 import jax.numpy as jnp
 from jax import lax
+from jax.experimental import pallas as pl
+from jax.experimental.pallas import tpu as pltpu
 from jax.sharding import PartitionSpec as P
 
+
 HEADS = 8
+CORES = 2
 
 
 epsilon = 1e-05
@@ -99,7 +103,346 @@
     return (embeddings, scores)
 
 
+def silu(values):
+    half = 0.5 * values
+    return half + half * jnp.tanh(half)
+
+
+def kernel_call(body, out_shape, in_specs, scratch, out_specs=None, flops=0, vmem=16):
+    any_or_vmem = out_specs
+    if any_or_vmem is None:
+        any_or_vmem = jax.tree.map(lambda _: pl.BlockSpec(memory_space=pltpu.VMEM), out_shape)
+    return pl.pallas_call(
+        body,
+        out_shape=out_shape,
+        in_specs=in_specs,
+        out_specs=any_or_vmem,
+        scratch_shapes=scratch,
+        cost_estimate=pl.CostEstimate(flops=flops, transcendentals=0, bytes_accessed=1),
+        compiler_params=pltpu.CompilerParams(vmem_limit_bytes=vmem * 1024 * 1024),
+    )
+
+
+ANY = pl.BlockSpec(memory_space=pltpu.HBM)
+
+
+def in_hbm(arrays):
+    return [pltpu.with_memory_space_constraint(array, pltpu.HBM) for array in arrays]
+
+
+VMEM = pl.BlockSpec(memory_space=pltpu.VMEM)
+SMEM = pl.BlockSpec(memory_space=pltpu.SMEM)
+
+
+def columns_for_peers(array, parts, helpers):
+    lead, width = array.shape[:-1], array.shape[-1]
+    features = width // parts
+    feats = features // helpers
+
+    def body(in_ref, *outs):
+        mine = lax.axis_index("helper")
+        for rel in range(helpers):
+            start = pl.multiple_of((mine ^ rel) * feats, feats)
+            for part in range(parts):
+                outs[rel][..., pl.ds(part * feats, feats)] = in_ref[
+                    ..., pl.ds(part * features + start, feats)
+                ]
+
+    return kernel_call(body, [jax.ShapeDtypeStruct(lead + (parts * feats,), array.dtype)] * helpers, [VMEM], [])(array)
+
+
+def weight_copies(refs, scratch, sems, rows, helpers, planes):
+    group, mine = lax.axis_index("group"), lax.axis_index("helper")
+    plane, core = group // CORES, lax.rem(group, CORES)
+    copies = []
+    for at, ref in enumerate(refs):
+        turn, swap = at // CORES, at % CORES
+        source = lax.rem(plane + planes - turn, planes) * CORES + (core ^ swap)
+        for rel in range(helpers):
+            start = pl.multiple_of((source * helpers + (mine ^ rel)) * rows, rows)
+            copies.append(
+                pltpu.make_async_copy(
+                    ref.at[pl.ds(rel * rows, rows)], scratch.at[pl.ds(start, rows)], sems.at[len(copies)]
+                )
+            )
+    return copies
+
+
+def attend(cands, weights, prefixes, users, gain, rows, planes, rows_block):
+    helpers = len(prefixes)
+    (_, _, first), *_ = cands
+    count, features = first.shape
+    n_cands = len(cands)
+    width = weights[0].shape[1]
+    feats = width // 4
+    prefix = prefixes[0].shape[1]
+    head_dim = features // HEADS
+    heads = feats // head_dim
+    scale = head_dim ** (-0.5)
+    blocks = count // rows_block
+    n_weights = len(weights)
+
+    def body(users_ref, gain_ref, *rest):
+        cand_refs, rest = rest[:n_cands], rest[n_cands:]
+        weight_refs, rest = rest[:n_weights], rest[n_weights:]
+        prefix_refs, rest = rest[:helpers], rest[helpers:]
+        mixed_ref, gate_ref, stats_ref = rest[:3]
+        cand, normed, weight, keys, vals, proj, c_sems, w_sems, p_sems = rest[3:]
+        c_copies = [
+            pltpu.make_async_copy(ref, cand.at[rel, pl.ds(start, ref.shape[0])], c_sems.at[at])
+            for at, ((rel, start, _), ref) in enumerate(zip(cands, cand_refs))
+        ]
+        p_copies = [
+            pltpu.make_async_copy(
+                prefix_refs[rel].at[part], held.at[pl.ds(rel * prefix, prefix)], p_sems.at[2 * rel + part]
+            )
+            for rel in range(helpers)
+            for part, held in enumerate((keys, vals))
+        ]
+        w_copies = weight_copies(weight_refs, weight, w_sems, rows, helpers, planes)
+        for copy in c_copies + w_copies + p_copies:
+            copy.start()
+        for rel in range(helpers):
+            for (at, _, _), copy in zip(cands, c_copies):
+                if at == rel:
+                    copy.wait()
+            values = cand[rel].astype(jnp.float32)
+            average = jnp.mean(values, axis=-1, keepdims=True)
+            centred = values - average
+            spread = jnp.mean(centred * centred, axis=-1, keepdims=True)
+            normed[rel] = (centred * lax.rsqrt(spread + epsilon) * gain_ref[...]).astype(jnp.bfloat16)
+        for copy in w_copies:
+            copy.wait()
+        for copy in p_copies:
+            copy.wait()
+        lane = lax.broadcasted_iota(jnp.int32, (rows_block, 128), 1)
+        for rel in range(helpers):
+            proj[...] = silu(jnp.dot(normed[rel], weight[...], preferred_element_type=jnp.float32))
+            gate_ref[pl.ds(rel * count, count)] = proj[:, :feats]
+            for block in range(blocks):
+                user = pl.multiple_of(users_ref[rel * blocks + block] * prefix, prefix)
+                here = pl.ds(block * rows_block, rows_block)
+                out = []
+                for head in range(heads):
+                    low = head * head_dim
+                    val = proj[here, pl.ds(feats + low, head_dim)]
+                    query = proj[here, pl.ds(2 * feats + low, head_dim)].astype(jnp.bfloat16)
+                    key = proj[here, pl.ds(3 * feats + low, head_dim)]
+                    own = silu(
+                        scale * jnp.sum(query.astype(jnp.float32) * key, axis=-1, keepdims=True)
+                    ) * val
+                    raw = lax.dot_general(
+                        query,
+                        keys[pl.ds(user, prefix), pl.ds(low, head_dim)],
+                        (((1,), (1,)), ((), ())),
+                        preferred_element_type=jnp.float32,
+                    )
+                    share = silu(scale * raw).astype(jnp.bfloat16)
+                    mix = jnp.dot(
+                        share, vals[pl.ds(user, prefix), pl.ds(low, head_dim)], preferred_element_type=jnp.float32
+                    )
+                    out.append(mix.astype(jnp.bfloat16).astype(jnp.float32) + own)
+                total = jnp.sum(sum(out), axis=-1, keepdims=True)
+                average = total * (1.0 / feats)
+                off = sum(jnp.sum((piece - average) ** 2, axis=-1, keepdims=True) for piece in out)
+                both = jnp.where(lane == 0, average, jnp.where(lane == 1, off, 0.0))
+                stats_ref[rel * blocks + block] = both.T[:8]
+                for head in range(heads):
+                    mixed_ref[
+                        pl.ds(rel * count + block * rows_block, rows_block), pl.ds(head * head_dim, head_dim)
+                    ] = out[head]
+
+    total_rows = helpers * count
+    shapes = [
+        jax.ShapeDtypeStruct((total_rows, feats), jnp.float32),
+        jax.ShapeDtypeStruct((total_rows, feats), jnp.float32),
+        jax.ShapeDtypeStruct((helpers * blocks, 8, rows_block), jnp.float32),
+    ]
+    n_pieces = n_weights * helpers
+    scratch = [
+        pltpu.VMEM((helpers, count, features), jnp.bfloat16),
+        pltpu.VMEM((helpers, count, features), jnp.bfloat16),
+        pltpu.VMEM((features, width), jnp.bfloat16),
+        pltpu.VMEM((helpers * prefix, feats), jnp.bfloat16),
+        pltpu.VMEM((helpers * prefix, feats), jnp.bfloat16),
+        pltpu.VMEM((count, width), jnp.float32),
+        pltpu.SemaphoreType.DMA((n_cands,)),
+        pltpu.SemaphoreType.DMA((n_pieces,)),
+        pltpu.SemaphoreType.DMA((2 * helpers,)),
+    ]
+    arrays = in_hbm([array for _, _, array in cands] + list(weights) + list(prefixes))
+    return kernel_call(
+        body, shapes, [SMEM, VMEM] + [ANY] * len(arrays), scratch, flops=2 * total_rows * features * width
+    )(users, gain, *arrays)
+
+
+def gate(mixed, gates, stats, gain, helpers, rows_block):
+    total_rows, feats = mixed.shape
+    count = total_rows // helpers
+    blocks = count // rows_block
+    features = feats * helpers
+
+    def body(mixed_ref, gate_ref, gain_ref, *rest):
+        stats_refs, outs = rest[:helpers], rest[helpers:]
+        for rel in range(helpers):
+            for block in range(blocks):
+                parts = [stats_refs[peer][(rel ^ peer) * blocks + block] for peer in range(helpers)]
+                average = sum(part[0:1] for part in parts) * (1.0 / helpers)
+                off = sum(
+                    part[1:2] + feats * (part[0:1] - average) ** 2 for part in parts
+                )
+                level = lax.rsqrt(off * (1.0 / features) + epsilon)
+                row = lax.broadcasted_iota(jnp.int32, (128, rows_block), 0)
+                both = jnp.where(row == 0, average, jnp.where(row == 1, level, 0.0)).T
+                here = pl.ds(rel * count + block * rows_block, rows_block)
+                outs[rel][pl.ds(block * rows_block, rows_block)] = (
+                    (mixed_ref[here] - both[:, 0:1]) * both[:, 1:2] * gain_ref[...] * gate_ref[here]
+                ).astype(jnp.bfloat16)
+
+    return kernel_call(
+        body,
+        [jax.ShapeDtypeStruct((count, feats), jnp.bfloat16)] * helpers,
+        [VMEM] * (3 + helpers),
+        [],
+        flops=total_rows * feats * 8,
+    )(mixed, gates, gain, *stats)
+
+
+def project_out(gated, weights, cands, live, vec, rows, planes, rows_block):
+    helpers = len(gated)
+    count, features = cands.shape
+    feats = features // helpers
+    blocks = count // rows_block
+    n_weights = len(weights)
+
+    def body(live_ref, vec_ref, cand_ref, *rest):
+        gated_refs = rest[:helpers]
+        weight_refs = rest[helpers : helpers + n_weights]
+        emb_ref, score_ref, weight, w_sems = rest[helpers + n_weights :]
+        copies = weight_copies(weight_refs, weight, w_sems, rows, helpers, planes)
+        for copy in copies:
+            copy.start()
+        for copy in copies:
+            copy.wait()
+        mine = lax.axis_index("helper")
+        lane = lax.broadcasted_iota(jnp.int32, (1, rows_block), 1)
+        for block in range(blocks):
+            here = pl.ds(block * rows_block, rows_block)
+            updated = cand_ref[here].astype(jnp.float32)
+            moved = None
+            for rel in range(helpers):
+                start = pl.multiple_of((mine ^ rel) * feats, feats)
+                part = jnp.dot(
+                    gated_refs[rel][here], weight[pl.ds(start, feats)], preferred_element_type=jnp.float32
+                )
+                moved = part if moved is None else moved + part
+            updated = updated + moved
+            emb_ref[here] = updated.astype(jnp.bfloat16)
+            average = jnp.mean(updated, axis=-1, keepdims=True)
+            centred = updated - average
+            spread = jnp.mean(centred * centred, axis=-1, keepdims=True)
+            found = jnp.sum(centred * vec_ref[...], axis=-1, keepdims=True) * lax.rsqrt(spread + epsilon)
+            across = jnp.broadcast_to(found, (rows_block, 128)).T[0:1]
+            score_ref[pl.ds(block, 1)] = jnp.where(lane < live_ref[block], across, 0.0)
+
+    shapes = [
+        jax.ShapeDtypeStruct((count, features), jnp.bfloat16),
+        jax.ShapeDtypeStruct((blocks, rows_block), jnp.float32),
+    ]
+    scratch = [
+        pltpu.VMEM((features, features), jnp.bfloat16),
+        pltpu.SemaphoreType.DMA((n_weights * helpers,)),
+    ]
+    return kernel_call(
+        body,
+        shapes,
+        [SMEM] + [VMEM] * (2 + helpers) + [ANY] * n_weights,
+        scratch,
+        flops=2 * count * features * features,
+    )(live, vec, cands, *gated, *in_hbm(weights))
+
+
+def by_heads(
+    candidates,
+    block_user,
+    live_rows,
+    prefix_keys,
+    prefix_values,
+    w_proj,
+    w_out,
+    gain_in,
+    gain_mid,
+    score_vec,
+):
+    helpers, groups = lax.axis_size("helper"), lax.axis_size("group")
+    planes = groups // CORES
+    blocks, rows_block, features = candidates.shape
+    feats = features // helpers
+    rows = w_proj.shape[0]
+    mine = lax.axis_index("helper")
+
+    def sent(array, axis, pairs):
+        return lax.ppermute(array, axis, pairs)
+
+    def to_peers(pieces):
+        return [pieces[0]] + [
+            sent(pieces[rel], "helper", [(at, at ^ rel) for at in range(helpers)])
+            for rel in range(1, len(pieces))
+        ]
+
+    def everyone(rows_here):
+        if helpers != 4:
+            return [(rel, 0, part) for rel, part in enumerate(to_peers([rows_here] * helpers))]
+        near = to_peers([rows_here] * 3)
+        half = rows_here.shape[0] // 2
+        far = []
+        for at, (over, of) in enumerate(((2, 1), (1, 2))):
+            pairs = [(here, here ^ over) for here in range(helpers)]
+            far.append((3, at * half, sent(near[of][at * half : (at + 1) * half], "helper", pairs)))
+        return [(rel, 0, part) for rel, part in enumerate(near)] + far
+
+    def spread(pieces):
+        shard = jnp.concatenate(pieces, axis=0)
+        out = []
+        for turn in range(planes):
+            held = shard
+            if turn:
+                pairs = [(at, (at + CORES * turn) % groups) for at in range(groups)]
+                held = sent(shard, "group", pairs)
+            swap = [(at, at ^ 1) for at in range(groups)]
+            out += [held, sent(held, "group", swap)]
+        return out
+
+    cand_rows = candidates.reshape(blocks * rows_block, features)
+    w_pieces = columns_for_peers(w_proj, 4, helpers)
+    both = jnp.concatenate([prefix_keys, prefix_values], axis=0)
+    prefix_pieces = columns_for_peers(both, 1, helpers)
+    proj_shards = spread(to_peers(w_pieces))
+    cands = everyone(cand_rows)
+    prefixes = to_peers(prefix_pieces)
+    users = jnp.concatenate(to_peers([block_user] * helpers)) ^ mine
+    out_shards = spread(to_peers([w_out] * helpers))
+
+    mixed, gates, stats = attend(
+        cands, proj_shards, prefixes, users, gain_in.reshape(1, features), rows, planes, rows_block
+    )
+    all_stats = to_peers([stats] * helpers)
+    my_gain = lax.dynamic_slice_in_dim(gain_mid.reshape(1, features), mine * feats, feats, axis=1)
+    gated = gate(mixed, gates, all_stats, my_gain, helpers, rows_block)
+    arrived = to_peers(gated)
+    embeddings, scores = project_out(
+        arrived, out_shards, cand_rows, live_rows, score_vec.reshape(1, features), rows, planes, rows_block
+    )
+    return embeddings.reshape(candidates.shape), scores
+
+
+def whole(*arrays):
+    return by_heads(*arrays)
+
+
 def solution(mesh):
+    helpers, groups = mesh.shape["helper"], mesh.shape["group"]
+    split = HEADS % helpers == 0 and helpers & (helpers - 1) == 0 and groups % CORES == 0
     placed = (
         P(("group", "helper"), None, None),
         P(("group", "helper")),
@@ -113,7 +456,7 @@
         P(),
     )
     return jax.shard_map(
-        shards,
+        whole if split else shards,
         mesh=mesh,
         in_specs=placed,
         out_specs=(P(("group", "helper"), None, None), P(("group", "helper"), None)),

time: 165 us -> 128 us (0.78)
  the two profiles are of different devices: /device:TPU:0 before, /device:TPU:8 now
where the time goes in v1:
time: 128 us
  waiting for transfers between devices  74.2 us (58%)
  starting transfers between devices  36 us (28%)
  Pallas kernels  12.9 us (10%)
  local copies, waits for them, and re-layouts  2.53 us (2%)
  other arithmetic  1.38 us (1%)
    ppermute x36, waiting for transfers between devices, sent(): return lax.ppermute(array, axis, pairs)  74.2 us
    ppermute x36, starting transfers between devices, sent(): return lax.ppermute(array, axis, pairs)  36 us
    pallas_call x1, Pallas kernels, attend(): kernel_call(body, shapes, [SMEM, VMEM] + [ANY] * len(arrays), scratch, fl...  8.04 us
    pallas_call x1, Pallas kernels, project_out(): kernel_call(body, shapes, [SMEM] + [VMEM] * (2 + helpers) + [ANY] * n_wei...  4.06 us
  transfers between devices with their start and end apart: 36, of which 19 were waited for; matrix products, arithmetic and copies ran while one was open for 2% of the time, Pallas kernels for 7%

profile of v1, /device:TPU:8, one launch (start us, length us, event | category | flops | bytes accessed | tf_op | source)
XLA Modules:
  0.0 127.9 jit_solution(17790062594431870209)
XLA Ops:
  0.6 1.6 %collective-permute-start = (s32[2]{0:T(128)}, s32[2]{0:T(128)S(1)}, u32[]{:S(2)}, u32[]{:S(2)}) collective-permute-start(s32[2]{0:T(128)} %param.11), channel_id=1, source_target_pairs={{0,1},{1,0},{2,3},{3,2},{4,5},{5,4},{6,7},{7,6},{8,9},{9,8},{10,11... | collective-permute-start | bytes 32 | tf_op jit(solution)/shard_map/ppermute | solution.py:385
  2.2 1.5 %collective-permute-start.1 = (s32[2]{0:T(128)}, s32[2]{0:T(128)S(1)}, u32[]{:S(2)}, u32[]{:S(2)}) collective-permute-start(s32[2]{0:T(128)} %param.11), channel_id=1, source_target_pairs={{0,2},{1,3},{2,0},{3,1},{4,6},{5,7},{6,4},{7,5},{8,10},{9,11},{10,... | collective-permute-start | bytes 32 | tf_op jit(solution)/shard_map/ppermute | solution.py:385
  3.7 0.5 collective-permute-start.2
  4.2 0.9 copy-done.2
  5.2 1.6 %collective-permute-start.7 = (bf16[32,1024]{1,0:T(8,128)(2,1)S(1)}, bf16[32,1024]{1,0:T(8,128)(2,1)S(1)}, u32[]{:S(2)}, u32[]{:S(2)}) collective-permute-start(bf16[32,1024]{1,0:T(8,128)(2,1)S(1)} %get-tuple-element.20), channel_id=1, source_target_pairs={{0,1},{1,0},{2,3},{3,2},{4,5},{5,4},{6,7},{7,6},{8,9},{9,8},{10,11... | collective-permute-start | bytes 196616 | tf_op jit(solution)/shard_map/ppermute | solution.py:385
  6.7 0.7 collective-permute-start.26
  7.5 1.3 %pad_maximum_fusion.in_ref = bf16[2,256,1024]{2,1,0:T(8,128)(2,1)S(1)} fusion(bf16[1,256,1024]{2,1,0:T(8,128)(2,1)} %param.14, bf16[1,256,1024]{2,1,0:T(8,128)(2,1)} %param.13), kind=kLoop, calls=%fused_computation | loop fusion | flops 524288 | bytes 2097152 | tf_op jit(solution)/shard_map/concatenate | solution.py:418
  8.8 0.0 copy-start
  8.8 0.1 shard_map.114
  9.0 0.0 collective-permute-done
  9.0 1.6 %collective-permute-start.8 = (bf16[32,1024]{1,0:T(8,128)(2,1)S(1)}, bf16[32,1024]{1,0:T(8,128)(2,1)S(1)}, u32[]{:S(2)}, u32[]{:S(2)}) collective-permute-start(bf16[32,1024]{1,0:T(8,128)(2,1)S(1)} %get-tuple-element.21), channel_id=1, source_target_pairs={{0,2},{1,3},{2,0},{3,1},{4,6},{5,7},{6,4},{7,5},{8,10},{9,11},{10,... | collective-permute-start | bytes 196616 | tf_op jit(solution)/shard_map/ppermute | solution.py:385
  10.6 1.2 collective-permute-start.9
  11.8 0.0 collective-permute-done.2
  11.8 0.7 collective-permute-start.17
  12.5 1.5 %collective-permute-start.18 = (bf16[2,256,256]{2,1,0:T(8,128)(2,1)S(1)}, bf16[2,256,256]{2,1,0:T(8,128)(2,1)S(1)}, u32[]{:S(2)}, u32[]{:S(2)}) collective-permute-start(bf16[2,256,256]{2,1,0:T(8,128)(2,1)S(1)} %get-tuple-element.25), channel_id=1, source_target_pairs={{0,2},{1,3},{2,0},{3,1},{4,6},{5,7},{6,4},{7,5},{8,10},{9,11},{10,... | collective-permute-start | bytes 786440 | tf_op jit(solution)/shard_map/ppermute | solution.py:385
  14.1 0.5 collective-permute-done.8
  14.6 1.0 collective-permute-start.3
  15.6 0.8 collective-permute-done.9
  16.4 0.5 collective-permute-start.4
  16.9 1.5 %collective-permute-start.27 = (bf16[32,1024]{1,0:T(8,128)(2,1)S(1)}, bf16[32,1024]{1,0:T(8,128)(2,1)S(1)}, u32[]{:S(2)}, u32[]{:S(2)}) collective-permute-start(bf16[32,1024]{1,0:T(8,128)(2,1)S(1)} %copy-done.12), channel_id=1, source_target_pairs={{0,2},{1,3},{2,0},{3,1},{4,6},{5,7},{6,4},{7,5},{8,10},{9,11},{10,... | collective-permute-start | bytes 196616 | tf_op jit(solution)/shard_map/ppermute | solution.py:385
  18.5 14.4 %collective-permute-done.27 = bf16[32,1024]{1,0:T(8,128)(2,1)S(1)} collective-permute-done((bf16[32,1024]{1,0:T(8,128)(2,1)S(1)}, bf16[32,1024]{1,0:T(8,128)(2,1)S(1)}, u32[]{:S(2)}, u32[]{:S(2)}) %collective-permute-start.27) | collective-permute-done | bytes 65568 | tf_op jit(solution)/shard_map/ppermute | solution.py:385
  32.9 1.7 %collective-permute-start.28 = (bf16[32,1024]{1,0:T(8,128)(2,1)S(1)}, bf16[32,1024]{1,0:T(8,128)(2,1)S(1)}, u32[]{:S(2)}, u32[]{:S(2)}) collective-permute-start(bf16[32,1024]{1,0:T(8,128)(2,1)S(1)} %copy-done.12), channel_id=1, source_target_pairs={{0,3},{1,2},{2,1},{3,0},{4,7},{5,6},{6,5},{7,4},{8,11},{9,10},{10,... | collective-permute-start | bytes 196616 | tf_op jit(solution)/shard_map/ppermute | solution.py:385
  34.5 3.5 %collective-permute-done.28 = bf16[32,1024]{1,0:T(8,128)(2,1)S(1)} collective-permute-done((bf16[32,1024]{1,0:T(8,128)(2,1)S(1)}, bf16[32,1024]{1,0:T(8,128)(2,1)S(1)}, u32[]{:S(2)}, u32[]{:S(2)}) %collective-permute-start.28) | collective-permute-done | bytes 65568 | tf_op jit(solution)/shard_map/ppermute | solution.py:385
  38.0 1.7 %collective-permute-start.19 = (bf16[2,256,256]{2,1,0:T(8,128)(2,1)S(1)}, bf16[2,256,256]{2,1,0:T(8,128)(2,1)S(1)}, u32[]{:S(2)}, u32[]{:S(2)}) collective-permute-start(bf16[2,256,256]{2,1,0:T(8,128)(2,1)S(1)} %get-tuple-element.26), channel_id=1, source_target_pairs={{0,3},{1,2},{2,1},{3,0},{4,7},{5,6},{6,5},{7,4},{8,11},{9,10},{10,... | collective-permute-start | bytes 786440 | tf_op jit(solution)/shard_map/ppermute | solution.py:385
  39.7 1.6 %collective-permute-start.11 = (bf16[128,1024]{1,0:T(8,128)(2,1)S(1)}, bf16[128,1024]{1,0:T(8,128)(2,1)}, u32[]{:S(2)}, u32[]{:S(2)}) collective-permute-start(bf16[128,1024]{1,0:T(8,128)(2,1)S(1)} %constant_dynamic-update-slice_fusion.rest_5_), channel_id=1, source_target_pairs={{0,8},{4,12},{8,16},{12,20},{16,24},{20,28},{24,0},{28,4},{1,9},{5... | collective-permute-start | bytes 786440 | tf_op jit(solution)/shard_map/ppermute | solution.py:385
  41.3 1.2 collective-permute-start.13
  42.5 2.7 %collective-permute-done.19.rest_16_ = bf16[2,256,256]{2,1,0:T(8,128)(2,1)S(1)} collective-permute-done((bf16[2,256,256]{2,1,0:T(8,128)(2,1)S(1)}, bf16[2,256,256]{2,1,0:T(8,128)(2,1)S(1)}, u32[]{:S(2)}, u32[]{:S(2)}) %collective-permute-start.19) | collective-permute-done | bytes 262176 | tf_op jit(solution)/shard_map/ppermute | solution.py:385
  45.3 0.4 collective-permute-start.15
  45.7 11.9 %collective-permute-done.11.rest_7_ = bf16[128,1024]{1,0:T(8,128)(2,1)} collective-permute-done((bf16[128,1024]{1,0:T(8,128)(2,1)S(1)}, bf16[128,1024]{1,0:T(8,128)(2,1)}, u32[]{:S(2)}, u32[]{:S(2)}) %collective-permute-start.11) | collective-permute-done | bytes 262176 | tf_op jit(solution)/shard_map/ppermute | solution.py:385
  57.6 2.8 %collective-permute-done.13.rest_9_ = bf16[128,1024]{1,0:T(8,128)(2,1)} collective-permute-done((bf16[128,1024]{1,0:T(8,128)(2,1)S(1)}, bf16[128,1024]{1,0:T(8,128)(2,1)}, u32[]{:S(2)}, u32[]{:S(2)}) %collective-permute-start.13) | collective-permute-done | bytes 262176 | tf_op jit(solution)/shard_map/ppermute | solution.py:385
  60.4 3.6 %collective-permute-start.32 = (bf16[128,1024]{1,0:T(8,128)(2,1)S(1)}, bf16[128,1024]{1,0:T(8,128)(2,1)S(1)}, u32[]{:S(2)}, u32[]{:S(2)}) collective-permute-start(bf16[128,1024]{1,0:T(8,128)(2,1)S(1)} %constant_dynamic-update-slice_fusion.4.rest_4_), channel_id=1, source_target_pairs={{0,16},{4,20},{8,24},{12,28},{16,0},{20,4},{24,8},{28,12},{1,17},{... | collective-permute-start | bytes 786440 | tf_op jit(solution)/shard_map/ppermute | solution.py:385
  64.0 2.0 %collective-permute-start.34 = (bf16[128,1024]{1,0:T(8,128)(2,1)S(1)}, bf16[128,1024]{1,0:T(8,128)(2,1)}, u32[]{:S(2)}, u32[]{:S(2)}) collective-permute-start(bf16[128,1024]{1,0:T(8,128)(2,1)S(1)} %constant_dynamic-update-slice_fusion.4.rest_4_), channel_id=1, source_target_pairs={{0,24},{4,28},{8,0},{12,4},{16,8},{20,12},{24,16},{28,20},{1,25},{... | collective-permute-start | bytes 786440 | tf_op jit(solution)/shard_map/ppermute | solution.py:385
  66.0 0.0 copy-start.14
  66.0 4.5 %collective-permute-done.15.rest_11_ = bf16[128,1024]{1,0:T(8,128)(2,1)S(1)} collective-permute-done((bf16[128,1024]{1,0:T(8,128)(2,1)S(1)}, bf16[128,1024]{1,0:T(8,128)(2,1)S(1)}, u32[]{:S(2)}, u32[]{:S(2)}) %collective-permute-start.15) | collective-permute-done | bytes 262176 | tf_op jit(solution)/shard_map/ppermute | solution.py:385
  70.5 0.5 collective-permute-start.14
  71.0 7.3 %collective-permute-done.30.rest_6_ = bf16[128,1024]{1,0:T(8,128)(2,1)S(1)} collective-permute-done((bf16[128,1024]{1,0:T(8,128)(2,1)S(1)}, bf16[128,1024]{1,0:T(8,128)(2,1)S(1)}, u32[]{:S(2)}, u32[]{:S(2)}) %collective-permute-start.30) | collective-permute-done | bytes 262176 | tf_op jit(solution)/shard_map/ppermute | solution.py:385
  78.4 4.9 %collective-permute-done.32.rest_8_ = bf16[128,1024]{1,0:T(8,128)(2,1)S(1)} collective-permute-done((bf16[128,1024]{1,0:T(8,128)(2,1)S(1)}, bf16[128,1024]{1,0:T(8,128)(2,1)S(1)}, u32[]{:S(2)}, u32[]{:S(2)}) %collective-permute-start.32) | collective-permute-done | bytes 262176 | tf_op jit(solution)/shard_map/ppermute | solution.py:385
  83.3 1.0 collective-permute-start.5
  84.3 0.6 collective-permute-done.34.rest_10_
  84.8 0.7 collective-permute-start.6
  85.6 0.1 add_xor_fusion.users_ref
  85.7 0.1 collective-permute-start.29
  85.8 0.5 collective-permute-start.31
  86.3 0.1 collective-permute-start.33
  86.4 4.6 %collective-permute-done.5.rest_3_ = bf16[128,1024]{1,0:T(8,128)(2,1)S(1)} collective-permute-done((bf16[128,1024]{1,0:T(8,128)(2,1)S(1)}, bf16[128,1024]{1,0:T(8,128)(2,1)S(1)}, u32[]{:S(2)}, u32[]{:S(2)}) %collective-permute-start.5) | collective-permute-done | bytes 262176 | tf_op jit(solution)/shard_map/ppermute | solution.py:385
  90.9 2.2 %collective-permute-done.6.rest_4_ = bf16[128,1024]{1,0:T(8,128)(2,1)} collective-permute-done((bf16[128,1024]{1,0:T(8,128)(2,1)S(1)}, bf16[128,1024]{1,0:T(8,128)(2,1)}, u32[]{:S(2)}, u32[]{:S(2)}) %collective-permute-start.6) | collective-permute-done | bytes 262176 | tf_op jit(solution)/shard_map/ppermute | solution.py:385
  93.2 8.0 %shard_map.115 = (f32[1024,256]{1,0:T(8,128)S(1)}, f32[1024,256]{1,0:T(8,128)S(1)}, f32[8,8,128]{2,1,0:T(8,128)S(1)}) custom-call(s32[8]{0:T(128)S(1)} %add_xor_fusion.users_ref, f32[1,1024]{1,0:T(1,128)S(1)} %bitcast.11, bf16[256,1024]{1,0:T(8,128)(2,1)} %bitcast.5, bf16[256,1024]{1,0:T(8,128)(2,1)} %copy-done.10, bf16[256,1024]{1,0:T(8,128)(2,1)} %copy-done.11, ...), custom_call_target="tpu_custom_call" | custom-call | flops 2147483648 | bytes 1 | tf_op jit(solution)/shard_map/pallas_call | solution.py:274
  101.3 0.8 collective-permute-start.20
  102.1 3.2 %collective-permute-done.20.rest_1_ = f32[8,8,128]{2,1,0:T(8,128)S(1)} collective-permute-done((f32[8,8,128]{2,1,0:T(8,128)S(1)}, f32[8,8,128]{2,1,0:T(8,128)S(1)}, u32[]{:S(2)}, u32[]{:S(2)}) %collective-permute-start.20) | collective-permute-done | bytes 32800 | tf_op jit(solution)/shard_map/ppermute | solution.py:385
  105.3 1.0 collective-permute-start.21
  106.3 2.9 %collective-permute-done.21.rest_2_ = f32[8,8,128]{2,1,0:T(8,128)S(1)} collective-permute-done((f32[8,8,128]{2,1,0:T(8,128)S(1)}, f32[8,8,128]{2,1,0:T(8,128)S(1)}, u32[]{:S(2)}, u32[]{:S(2)}) %collective-permute-start.21) | collective-permute-done | bytes 32800 | tf_op jit(solution)/shard_map/ppermute | solution.py:385
  109.2 1.7 %collective-permute-start.22 = (f32[8,8,128]{2,1,0:T(8,128)S(1)}, f32[8,8,128]{2,1,0:T(8,128)S(1)}, u32[]{:S(2)}, u32[]{:S(2)}) collective-permute-start(f32[8,8,128]{2,1,0:T(8,128)S(1)} %get-tuple-element.29.rest_0_), channel_id=1, source_target_pairs={{0,3},{1,2},{2,1},{3,0},{4,7},{5,6},{6,5},{7,4},{8,11},{9,10},{10,... | collective-permute-start | bytes 98312 | tf_op jit(solution)/shard_map/ppermute | solution.py:385
  110.9 0.8 dynamic-slice.3
  111.7 2.7 %collective-permute-done.22.rest_3_ = f32[8,8,128]{2,1,0:T(8,128)S(1)} collective-permute-done((f32[8,8,128]{2,1,0:T(8,128)S(1)}, f32[8,8,128]{2,1,0:T(8,128)S(1)}, u32[]{:S(2)}, u32[]{:S(2)}) %collective-permute-start.22) | collective-permute-done | bytes 32800 | tf_op jit(solution)/shard_map/ppermute | solution.py:385
  114.4 0.6 shard_map.116
  115.0 0.0 copy-start.3
  115.0 0.5 collective-permute-start.23
  115.5 1.9 %collective-permute-start.24 = (bf16[256,256]{1,0:T(8,128)(2,1)S(1)}, bf16[256,256]{1,0:T(8,128)(2,1)S(1)}, u32[]{:S(2)}, u32[]{:S(2)}) collective-permute-start(bf16[256,256]{1,0:T(8,128)(2,1)S(1)} %get-tuple-element.32), channel_id=1, source_target_pairs={{0,2},{1,3},{2,0},{3,1},{4,6},{5,7},{6,4},{7,5},{8,10},{9,11},{10,... | collective-permute-start | bytes 393224 | tf_op jit(solution)/shard_map/ppermute | solution.py:385
  117.3 1.2 collective-permute-start.25
  118.6 1.5 %collective-permute-done.23.rest_1_ = bf16[256,256]{1,0:T(8,128)(2,1)S(1)} collective-permute-done((bf16[256,256]{1,0:T(8,128)(2,1)S(1)}, bf16[256,256]{1,0:T(8,128)(2,1)S(1)}, u32[]{:S(2)}, u32[]{:S(2)}) %collective-permute-start.23) | collective-permute-done | bytes 131104 | tf_op jit(solution)/shard_map/ppermute | solution.py:385
  120.0 1.2 collective-permute-done.24.rest_2_
  121.3 1.9 %collective-permute-done.25.rest_3_ = bf16[256,256]{1,0:T(8,128)(2,1)S(1)} collective-permute-done((bf16[256,256]{1,0:T(8,128)(2,1)S(1)}, bf16[256,256]{1,0:T(8,128)(2,1)S(1)}, u32[]{:S(2)}, u32[]{:S(2)}) %collective-permute-start.25) | collective-permute-done | bytes 131104 | tf_op jit(solution)/shard_map/ppermute | solution.py:385
  123.2 0.6 copy-done.4
  123.9 4.1 %shard_map.117 = (bf16[256,1024]{1,0:T(8,128)(2,1)}, f32[2,128]{1,0:T(2,128)}) custom-call(s32[2]{0:T(128)S(1)} %copy-done.4, f32[1,1024]{1,0:T(1,128)S(1)} %bitcast.9, bf16[256,1024]{1,0:T(8,128)(2,1)S(1)} %bitcast.8, bf16[256,256]{1,0:T(8,128)(2,1)S(1)} %get-tuple-element.30.rest_0_, bf16[256,256]{1,0:T(8,128)(2,1)S(1)} %collective-permute-done.23.rest_1_, ...), custom_call_target="tpu_custom_call" | custom-call | flops 536870912 | bytes 1 | tf_op jit(solution)/shard_map/pallas_call | solution.py:356
  (74 shorter events, 0.3 us)
Async XLA Ops:
  0.6 8.3 %collective-permute-start = (s32[2]{0:T(128)}, s32[2]{0:T(128)S(1)}, u32[]{:S(2)}, u32[]{:S(2)}) collective-permute-start(s32[2]{0:T(128)} %param.11), channel_id=1, source_target_pairs={{0,1},{1,0},{2,3},{3,2},{4,5},{5,4},{6,7},{7,6},{8,9},{9,8},{10,11... | collective-permute-start | bytes 32 | tf_op jit(solution)/shard_map/ppermute | solution.py:385
  2.2 8.4 %collective-permute-start.1 = (s32[2]{0:T(128)}, s32[2]{0:T(128)S(1)}, u32[]{:S(2)}, u32[]{:S(2)}) collective-permute-start(s32[2]{0:T(128)} %param.11), channel_id=1, source_target_pairs={{0,2},{1,3},{2,0},{3,1},{4,6},{5,7},{6,4},{7,5},{8,10},{9,11},{10,... | collective-permute-start | bytes 32 | tf_op jit(solution)/shard_map/ppermute | solution.py:385
  3.7 8.1 %collective-permute-start.2 = (s32[2]{0:T(128)}, s32[2]{0:T(128)S(1)}, u32[]{:S(2)}, u32[]{:S(2)}) collective-permute-start(s32[2]{0:T(128)} %param.11), channel_id=1, source_target_pairs={{0,3},{1,2},{2,1},{3,0},{4,7},{5,6},{6,5},{7,4},{8,11},{9,10},{10,... | collective-permute-start | bytes 32 | tf_op jit(solution)/shard_map/ppermute | solution.py:385
  4.2 0.9 copy-start.2
  5.1 1.6 %copy-start.12 = (bf16[32,1024]{1,0:T(8,128)(2,1)S(1)}, bf16[32,1024]{1,0:T(8,128)(2,1)}, u32[]{:S(2)}) copy-start(bf16[32,1024]{1,0:T(8,128)(2,1)} %param.16) | copy-start | bytes 196612
  5.2 7.4 %collective-permute-start.7 = (bf16[32,1024]{1,0:T(8,128)(2,1)S(1)}, bf16[32,1024]{1,0:T(8,128)(2,1)S(1)}, u32[]{:S(2)}, u32[]{:S(2)}) collective-permute-start(bf16[32,1024]{1,0:T(8,128)(2,1)S(1)} %get-tuple-element.20), channel_id=1, source_target_pairs={{0,1},{1,0},{2,3},{3,2},{4,5},{5,4},{6,7},{7,6},{8,9},{9,8},{10,11... | collective-permute-start | bytes 196616 | tf_op jit(solution)/shard_map/ppermute | solution.py:385
  6.7 10.2 %collective-permute-start.26 = (bf16[32,1024]{1,0:T(8,128)(2,1)S(1)}, bf16[32,1024]{1,0:T(8,128)(2,1)S(1)}, u32[]{:S(2)}, u32[]{:S(2)}) collective-permute-start(bf16[32,1024]{1,0:T(8,128)(2,1)S(1)} %copy-done.12), channel_id=1, source_target_pairs={{0,1},{1,0},{2,3},{3,2},{4,5},{5,4},{6,7},{7,6},{8,9},{9,8},{10,11... | collective-permute-start | bytes 196616 | tf_op jit(solution)/shard_map/ppermute | solution.py:385
  8.8 5.8 %copy-start = (bf16[2,128,1024]{2,1,0:T(8,128)(2,1)S(1)}, bf16[2,128,1024]{2,1,0:T(8,128)(2,1)}, u32[]{:S(2)}) copy-start(bf16[2,128,1024]{2,1,0:T(8,128)(2,1)} %param.10) | copy-start | bytes 1572868
  8.9 25.6 %copy-start.5 = (bf16[2,256,256]{2,1,0:T(8,128)(2,1)}, bf16[2,256,256]{2,1,0:T(8,128)(2,1)S(1)}, u32[]{:S(2)}) copy-start(bf16[2,256,256]{2,1,0:T(8,128)(2,1)S(1)} %get-tuple-element.23.rest_13_) | copy-start | bytes 786436
  9.0 5.6 %collective-permute-start.8 = (bf16[32,1024]{1,0:T(8,128)(2,1)S(1)}, bf16[32,1024]{1,0:T(8,128)(2,1)S(1)}, u32[]{:S(2)}, u32[]{:S(2)}) collective-permute-start(bf16[32,1024]{1,0:T(8,128)(2,1)S(1)} %get-tuple-element.21), channel_id=1, source_target_pairs={{0,2},{1,3},{2,0},{3,1},{4,6},{5,7},{6,4},{7,5},{8,10},{9,11},{10,... | collective-permute-start | bytes 196616 | tf_op jit(solution)/shard_map/ppermute | solution.py:385
  10.6 5.9 %collective-permute-start.9 = (bf16[32,1024]{1,0:T(8,128)(2,1)S(1)}, bf16[32,1024]{1,0:T(8,128)(2,1)S(1)}, u32[]{:S(2)}, u32[]{:S(2)}) collective-permute-start(bf16[32,1024]{1,0:T(8,128)(2,1)S(1)} %get-tuple-element.22), channel_id=1, source_target_pairs={{0,3},{1,2},{2,1},{3,0},{4,7},{5,6},{6,5},{7,4},{8,11},{9,10},{10,... | collective-permute-start | bytes 196616 | tf_op jit(solution)/shard_map/ppermute | solution.py:385
  11.8 27.9 %collective-permute-start.17 = (bf16[2,256,256]{2,1,0:T(8,128)(2,1)S(1)}, bf16[2,256,256]{2,1,0:T(8,128)(2,1)S(1)}, u32[]{:S(2)}, u32[]{:S(2)}) collective-permute-start(bf16[2,256,256]{2,1,0:T(8,128)(2,1)S(1)} %get-tuple-element.24), channel_id=1, source_target_pairs={{0,1},{1,0},{2,3},{3,2},{4,5},{5,4},{6,7},{7,6},{8,9},{9,8},{10,11... | collective-permute-start | bytes 786440 | tf_op jit(solution)/shard_map/ppermute | solution.py:385
  12.5 28.7 %collective-permute-start.18 = (bf16[2,256,256]{2,1,0:T(8,128)(2,1)S(1)}, bf16[2,256,256]{2,1,0:T(8,128)(2,1)S(1)}, u32[]{:S(2)}, u32[]{:S(2)}) collective-permute-start(bf16[2,256,256]{2,1,0:T(8,128)(2,1)S(1)} %get-tuple-element.25), channel_id=1, source_target_pairs={{0,2},{1,3},{2,0},{3,1},{4,6},{5,7},{6,4},{7,5},{8,10},{9,11},{10,... | collective-permute-start | bytes 786440 | tf_op jit(solution)/shard_map/ppermute | solution.py:385
  14.6 45.9 %collective-permute-start.3 = (bf16[256,1024]{1,0:T(8,128)(2,1)S(1)}, bf16[256,1024]{1,0:T(8,128)(2,1)S(1)}, u32[]{:S(2)}, u32[]{:S(2)}) collective-permute-start(bf16[256,1024]{1,0:T(8,128)(2,1)S(1)} %bitcast.6), channel_id=1, source_target_pairs={{0,1},{1,0},{2,3},{3,2},{4,5},{5,4},{6,7},{7,6},{8,9},{9,8},{10,11... | collective-permute-start | bytes 1572872 | tf_op jit(solution)/shard_map/ppermute | solution.py:385
  16.4 47.6 %collective-permute-start.4 = (bf16[256,1024]{1,0:T(8,128)(2,1)S(1)}, bf16[256,1024]{1,0:T(8,128)(2,1)S(1)}, u32[]{:S(2)}, u32[]{:S(2)}) collective-permute-start(bf16[256,1024]{1,0:T(8,128)(2,1)S(1)} %bitcast.7), channel_id=1, source_target_pairs={{0,2},{1,3},{2,0},{3,1},{4,6},{5,7},{6,4},{7,5},{8,10},{9,11},{10,... | collective-permute-start | bytes 1572872 | tf_op jit(solution)/shard_map/ppermute | solution.py:385
  16.9 15.9 %collective-permute-start.27 = (bf16[32,1024]{1,0:T(8,128)(2,1)S(1)}, bf16[32,1024]{1,0:T(8,128)(2,1)S(1)}, u32[]{:S(2)}, u32[]{:S(2)}) collective-permute-start(bf16[32,1024]{1,0:T(8,128)(2,1)S(1)} %copy-done.12), channel_id=1, source_target_pairs={{0,2},{1,3},{2,0},{3,1},{4,6},{5,7},{6,4},{7,5},{8,10},{9,11},{10,... | collective-permute-start | bytes 196616 | tf_op jit(solution)/shard_map/ppermute | solution.py:385
  32.9 5.2 %collective-permute-start.28 = (bf16[32,1024]{1,0:T(8,128)(2,1)S(1)}, bf16[32,1024]{1,0:T(8,128)(2,1)S(1)}, u32[]{:S(2)}, u32[]{:S(2)}) collective-permute-start(bf16[32,1024]{1,0:T(8,128)(2,1)S(1)} %copy-done.12), channel_id=1, source_target_pairs={{0,3},{1,2},{2,1},{3,0},{4,7},{5,6},{6,5},{7,4},{8,11},{9,10},{10,... | collective-permute-start | bytes 196616 | tf_op jit(solution)/shard_map/ppermute | solution.py:385
  34.5 31.5 %copy-start.13 = (bf16[128,1024]{1,0:T(8,128)(2,1)}, bf16[128,1024]{1,0:T(8,128)(2,1)S(1)}, u32[]{:S(2)}) copy-start(bf16[128,1024]{1,0:T(8,128)(2,1)S(1)} %constant_dynamic-update-slice_fusion.rest_5_) | copy-start | bytes 786436
  38.0 7.3 %collective-permute-start.19 = (bf16[2,256,256]{2,1,0:T(8,128)(2,1)S(1)}, bf16[2,256,256]{2,1,0:T(8,128)(2,1)S(1)}, u32[]{:S(2)}, u32[]{:S(2)}) collective-permute-start(bf16[2,256,256]{2,1,0:T(8,128)(2,1)S(1)} %get-tuple-element.26), channel_id=1, source_target_pairs={{0,3},{1,2},{2,1},{3,0},{4,7},{5,6},{6,5},{7,4},{8,11},{9,10},{10,... | collective-permute-start | bytes 786440 | tf_op jit(solution)/shard_map/ppermute | solution.py:385
  39.7 26.3 %copy-start.15 = (bf16[2,256,256]{2,1,0:T(8,128)(2,1)}, bf16[2,256,256]{2,1,0:T(8,128)(2,1)S(1)}, u32[]{:S(2)}) copy-start(bf16[2,256,256]{2,1,0:T(8,128)(2,1)S(1)} %collective-permute-done.17.rest_14_) | copy-start | bytes 786436
  39.7 17.9 %collective-permute-start.11 = (bf16[128,1024]{1,0:T(8,128)(2,1)S(1)}, bf16[128,1024]{1,0:T(8,128)(2,1)}, u32[]{:S(2)}, u32[]{:S(2)}) collective-permute-start(bf16[128,1024]{1,0:T(8,128)(2,1)S(1)} %constant_dynamic-update-slice_fusion.rest_5_), channel_id=1, source_target_pairs={{0,8},{4,12},{8,16},{12,20},{16,24},{20,28},{24,0},{28,4},{1,9},{5... | collective-permute-start | bytes 786440 | tf_op jit(solution)/shard_map/ppermute | solution.py:385
  41.3 44.3 %copy-start.16 = (bf16[2,256,256]{2,1,0:T(8,128)(2,1)}, bf16[2,256,256]{2,1,0:T(8,128)(2,1)S(1)}, u32[]{:S(2)}) copy-start(bf16[2,256,256]{2,1,0:T(8,128)(2,1)S(1)} %collective-permute-done.18.rest_15_) | copy-start | bytes 786436
  41.3 19.2 %collective-permute-start.13 = (bf16[128,1024]{1,0:T(8,128)(2,1)S(1)}, bf16[128,1024]{1,0:T(8,128)(2,1)}, u32[]{:S(2)}, u32[]{:S(2)}) collective-permute-start(bf16[128,1024]{1,0:T(8,128)(2,1)S(1)} %constant_dynamic-update-slice_fusion.rest_5_), channel_id=1, source_target_pairs={{0,16},{4,20},{8,24},{12,28},{16,0},{20,4},{24,8},{28,12},{1,17},{... | collective-permute-start | bytes 786440 | tf_op jit(solution)/shard_map/ppermute | solution.py:385
  42.5 43.2 %copy-start.7 = (bf16[128,1024]{1,0:T(8,128)(2,1)}, bf16[128,1024]{1,0:T(8,128)(2,1)S(1)}, u32[]{:S(2)}) copy-start(bf16[128,1024]{1,0:T(8,128)(2,1)S(1)} %constant_dynamic-update-slice_fusion.4.rest_4_) | copy-start | bytes 786436
  45.3 40.3 %copy-start.17 = (bf16[2,256,256]{2,1,0:T(8,128)(2,1)}, bf16[2,256,256]{2,1,0:T(8,128)(2,1)S(1)}, u32[]{:S(2)}) copy-start(bf16[2,256,256]{2,1,0:T(8,128)(2,1)S(1)} %collective-permute-done.19.rest_16_) | copy-start | bytes 786436
  45.3 25.2 %collective-permute-start.15 = (bf16[128,1024]{1,0:T(8,128)(2,1)S(1)}, bf16[128,1024]{1,0:T(8,128)(2,1)S(1)}, u32[]{:S(2)}, u32[]{:S(2)}) collective-permute-start(bf16[128,1024]{1,0:T(8,128)(2,1)S(1)} %constant_dynamic-update-slice_fusion.rest_5_), channel_id=1, source_target_pairs={{0,24},{4,28},{8,0},{12,4},{16,8},{20,12},{24,16},{28,20},{1,25},{... | collective-permute-start | bytes 786440 | tf_op jit(solution)/shard_map/ppermute | solution.py:385
  57.6 12.9 %collective-permute-start.10 = (bf16[128,1024]{1,0:T(8,128)(2,1)S(1)}, bf16[128,1024]{1,0:T(8,128)(2,1)S(1)}, u32[]{:S(2)}, u32[]{:S(2)}) collective-permute-start(bf16[128,1024]{1,0:T(8,128)(2,1)S(1)} %constant_dynamic-update-slice_fusion.rest_5_), channel_id=1, source_target_pairs={{0,4},{4,0},{8,12},{12,8},{16,20},{20,16},{24,28},{28,24},{1,5},{5... | collective-permute-start | bytes 786440 | tf_op jit(solution)/shard_map/ppermute | solution.py:385
  60.4 17.9 %collective-permute-start.30 = (bf16[128,1024]{1,0:T(8,128)(2,1)S(1)}, bf16[128,1024]{1,0:T(8,128)(2,1)S(1)}, u32[]{:S(2)}, u32[]{:S(2)}) collective-permute-start(bf16[128,1024]{1,0:T(8,128)(2,1)S(1)} %constant_dynamic-update-slice_fusion.4.rest_4_), channel_id=1, source_target_pairs={{0,8},{4,12},{8,16},{12,20},{16,24},{20,28},{24,0},{28,4},{1,9},{5... | collective-permute-start | bytes 786440 | tf_op jit(solution)/shard_map/ppermute | solution.py:385
  60.4 5.6 %copy-start.10 = (bf16[256,1024]{1,0:T(8,128)(2,1)}, bf16[256,1024]{1,0:T(8,128)(2,1)S(1)}, u32[]{:S(2)}) copy-start(bf16[256,1024]{1,0:T(8,128)(2,1)S(1)} %collective-permute-done.3.rest_1_) | copy-start | bytes 1572868
  60.4 22.9 %collective-permute-start.32 = (bf16[128,1024]{1,0:T(8,128)(2,1)S(1)}, bf16[128,1024]{1,0:T(8,128)(2,1)S(1)}, u32[]{:S(2)}, u32[]{:S(2)}) collective-permute-start(bf16[128,1024]{1,0:T(8,128)(2,1)S(1)} %constant_dynamic-update-slice_fusion.4.rest_4_), channel_id=1, source_target_pairs={{0,16},{4,20},{8,24},{12,28},{16,0},{20,4},{24,8},{28,12},{1,17},{... | collective-permute-start | bytes 786440 | tf_op jit(solution)/shard_map/ppermute | solution.py:385
  64.0 29.2 %copy-start.11 = (bf16[256,1024]{1,0:T(8,128)(2,1)}, bf16[256,1024]{1,0:T(8,128)(2,1)S(1)}, u32[]{:S(2)}) copy-start(bf16[256,1024]{1,0:T(8,128)(2,1)S(1)} %collective-permute-done.4.rest_2_) | copy-start | bytes 1572868
  64.0 20.9 %collective-permute-start.34 = (bf16[128,1024]{1,0:T(8,128)(2,1)S(1)}, bf16[128,1024]{1,0:T(8,128)(2,1)}, u32[]{:S(2)}, u32[]{:S(2)}) collective-permute-start(bf16[128,1024]{1,0:T(8,128)(2,1)S(1)} %constant_dynamic-update-slice_fusion.4.rest_4_), channel_id=1, source_target_pairs={{0,24},{4,28},{8,0},{12,4},{16,8},{20,12},{24,16},{28,20},{1,25},{... | collective-permute-start | bytes 786440 | tf_op jit(solution)/shard_map/ppermute | solution.py:385
  66.0 19.6 %copy-start.14 = (s32[2]{0:T(128)S(1)}, s32[2]{0:T(128)}, u32[]{:S(2)}) copy-start(s32[2]{0:T(128)} %param.11) | copy-start | bytes 28
  70.5 22.7 %copy-start.18 = (bf16[128,1024]{1,0:T(8,128)(2,1)}, bf16[128,1024]{1,0:T(8,128)(2,1)S(1)}, u32[]{:S(2)}) copy-start(bf16[128,1024]{1,0:T(8,128)(2,1)S(1)} %collective-permute-done.15.rest_11_) | copy-start | bytes 786436
  70.5 15.2 %collective-permute-start.12 = (bf16[128,1024]{1,0:T(8,128)(2,1)}, bf16[128,1024]{1,0:T(8,128)(2,1)S(1)}, u32[]{:S(2)}, u32[]{:S(2)}) collective-permute-start(bf16[128,1024]{1,0:T(8,128)(2,1)} %collective-permute-done.11.rest_7_), channel_id=1, source_target_pairs={{0,4},{4,0},{8,12},{12,8},{16,20},{20,16},{24,28},{28,24},{1,5},{5... | collective-permute-start | bytes 786440 | tf_op jit(solution)/shard_map/ppermute | solution.py:385
  70.5 15.1 %copy-start.19 = (bf16[128,1024]{1,0:T(8,128)(2,1)}, bf16[128,1024]{1,0:T(8,128)(2,1)S(1)}, u32[]{:S(2)}) copy-start(bf16[128,1024]{1,0:T(8,128)(2,1)S(1)} %collective-permute-done.10.rest_6_) | copy-start | bytes 786436
  70.5 15.2 %collective-permute-start.14 = (bf16[128,1024]{1,0:T(8,128)(2,1)}, bf16[128,1024]{1,0:T(8,128)(2,1)S(1)}, u32[]{:S(2)}, u32[]{:S(2)}) collective-permute-start(bf16[128,1024]{1,0:T(8,128)(2,1)} %collective-permute-done.13.rest_9_), channel_id=1, source_target_pairs={{0,4},{4,0},{8,12},{12,8},{16,20},{20,16},{24,28},{28,24},{1,5},{5... | collective-permute-start | bytes 786440 | tf_op jit(solution)/shard_map/ppermute | solution.py:385
  78.4 22.9 %copy-start.8 = (bf16[128,1024]{1,0:T(8,128)(2,1)}, bf16[128,1024]{1,0:T(8,128)(2,1)S(1)}, u32[]{:S(2)}) copy-start(bf16[128,1024]{1,0:T(8,128)(2,1)S(1)} %collective-permute-done.30.rest_6_) | copy-start | bytes 786436
  78.4 7.9 %collective-permute-start.16 = (bf16[128,1024]{1,0:T(8,128)(2,1)S(1)}, bf16[128,1024]{1,0:T(8,128)(2,1)S(1)}, u32[]{:S(2)}, u32[]{:S(2)}) collective-permute-start(bf16[128,1024]{1,0:T(8,128)(2,1)S(1)} %collective-permute-done.15.rest_11_), channel_id=1, source_target_pairs={{0,4},{4,0},{8,12},{12,8},{16,20},{20,16},{24,28},{28,24},{1,5},{5... | collective-permute-start | bytes 786440 | tf_op jit(solution)/shard_map/ppermute | solution.py:385
  83.3 18.0 %copy-start.9 = (bf16[128,1024]{1,0:T(8,128)(2,1)}, bf16[128,1024]{1,0:T(8,128)(2,1)S(1)}, u32[]{:S(2)}) copy-start(bf16[128,1024]{1,0:T(8,128)(2,1)S(1)} %collective-permute-done.32.rest_8_) | copy-start | bytes 786436
  83.3 7.6 %collective-permute-start.5 = (bf16[128,1024]{1,0:T(8,128)(2,1)S(1)}, bf16[128,1024]{1,0:T(8,128)(2,1)S(1)}, u32[]{:S(2)}, u32[]{:S(2)}) collective-permute-start(bf16[128,1024]{1,0:T(8,128)(2,1)S(1)} %slice.8), channel_id=1, source_target_pairs={{0,2},{1,3},{2,0},{3,1},{4,6},{5,7},{6,4},{7,5},{8,10},{9,11},{10,... | collective-permute-start | bytes 786440 | tf_op jit(solution)/shard_map/ppermute | solution.py:385
  84.8 8.3 %collective-permute-start.6 = (bf16[128,1024]{1,0:T(8,128)(2,1)S(1)}, bf16[128,1024]{1,0:T(8,128)(2,1)}, u32[]{:S(2)}, u32[]{:S(2)}) collective-permute-start(bf16[128,1024]{1,0:T(8,128)(2,1)S(1)} %slice.9), channel_id=1, source_target_pairs={{0,1},{1,0},{2,3},{3,2},{4,5},{5,4},{6,7},{7,6},{8,9},{9,8},{10,11... | collective-permute-start | bytes 786440 | tf_op jit(solution)/shard_map/ppermute | solution.py:385
  85.6 7.6 %copy-start.6 = (f32[1024]{0:T(1024)S(1)}, f32[1024]{0:T(1024)}, u32[]{:S(2)}) copy-start(f32[1024]{0:T(1024)} %param.17) | copy-start | bytes 12292
  85.7 7.5 %copy-start.20 = (bf16[128,1024]{1,0:T(8,128)(2,1)}, bf16[128,1024]{1,0:T(8,128)(2,1)S(1)}, u32[]{:S(2)}) copy-start(bf16[128,1024]{1,0:T(8,128)(2,1)S(1)} %collective-permute-done.12.rest_8_) | copy-start | bytes 786436
  85.7 29.8 %collective-permute-start.29 = (bf16[128,1024]{1,0:T(8,128)(2,1)S(1)}, bf16[128,1024]{1,0:T(8,128)(2,1)}, u32[]{:S(2)}, u32[]{:S(2)}) collective-permute-start(bf16[128,1024]{1,0:T(8,128)(2,1)S(1)} %constant_dynamic-update-slice_fusion.4.rest_4_), channel_id=1, source_target_pairs={{0,4},{4,0},{8,12},{12,8},{16,20},{20,16},{24,28},{28,24},{1,5},{5... | collective-permute-start | bytes 786440 | tf_op jit(solution)/shard_map/ppermute | solution.py:385
  85.8 7.4 %copy-start.21 = (bf16[128,1024]{1,0:T(8,128)(2,1)}, bf16[128,1024]{1,0:T(8,128)(2,1)S(1)}, u32[]{:S(2)}) copy-start(bf16[128,1024]{1,0:T(8,128)(2,1)S(1)} %collective-permute-done.14.rest_10_) | copy-start | bytes 786436
  85.8 31.6 %collective-permute-start.31 = (bf16[128,1024]{1,0:T(8,128)(2,1)S(1)}, bf16[128,1024]{1,0:T(8,128)(2,1)}, u32[]{:S(2)}, u32[]{:S(2)}) collective-permute-start(bf16[128,1024]{1,0:T(8,128)(2,1)S(1)} %collective-permute-done.30.rest_6_), channel_id=1, source_target_pairs={{0,4},{4,0},{8,12},{12,8},{16,20},{20,16},{24,28},{28,24},{1,5},{5... | collective-permute-start | bytes 786440 | tf_op jit(solution)/shard_map/ppermute | solution.py:385
  86.3 6.9 %copy-start.22 = (bf16[128,1024]{1,0:T(8,128)(2,1)}, bf16[128,1024]{1,0:T(8,128)(2,1)S(1)}, u32[]{:S(2)}) copy-start(bf16[128,1024]{1,0:T(8,128)(2,1)S(1)} %collective-permute-done.16.rest_12_) | copy-start | bytes 786436
  86.3 32.3 %collective-permute-start.33 = (bf16[128,1024]{1,0:T(8,128)(2,1)S(1)}, bf16[128,1024]{1,0:T(8,128)(2,1)}, u32[]{:S(2)}, u32[]{:S(2)}) collective-permute-start(bf16[128,1024]{1,0:T(8,128)(2,1)S(1)} %collective-permute-done.32.rest_8_), channel_id=1, source_target_pairs={{0,4},{4,0},{8,12},{12,8},{16,20},{20,16},{24,28},{28,24},{1,5},{5... | collective-permute-start | bytes 786440 | tf_op jit(solution)/shard_map/ppermute | solution.py:385
  90.9 2.3 %copy-start.23 = (bf16[128,1024]{1,0:T(8,128)(2,1)}, bf16[128,1024]{1,0:T(8,128)(2,1)S(1)}, u32[]{:S(2)}) copy-start(bf16[128,1024]{1,0:T(8,128)(2,1)S(1)} %collective-permute-done.5.rest_3_) | copy-start | bytes 786436
  90.9 27.7 %collective-permute-start.35 = (bf16[128,1024]{1,0:T(8,128)(2,1)}, bf16[128,1024]{1,0:T(8,128)(2,1)}, u32[]{:S(2)}, u32[]{:S(2)}) collective-permute-start(bf16[128,1024]{1,0:T(8,128)(2,1)} %collective-permute-done.34.rest_10_), channel_id=1, source_target_pairs={{0,4},{4,0},{8,12},{12,8},{16,20},{20,16},{24,28},{28,24},{1,5},{5... | collective-permute-start | bytes 786440 | tf_op jit(solution)/shard_map/ppermute | solution.py:385
  101.3 4.0 %collective-permute-start.20 = (f32[8,8,128]{2,1,0:T(8,128)S(1)}, f32[8,8,128]{2,1,0:T(8,128)S(1)}, u32[]{:S(2)}, u32[]{:S(2)}) collective-permute-start(f32[8,8,128]{2,1,0:T(8,128)S(1)} %get-tuple-element.29.rest_0_), channel_id=1, source_target_pairs={{0,1},{1,0},{2,3},{3,2},{4,5},{5,4},{6,7},{7,6},{8,9},{9,8},{10,11... | collective-permute-start | bytes 98312 | tf_op jit(solution)/shard_map/ppermute | solution.py:385
  105.3 3.9 %collective-permute-start.21 = (f32[8,8,128]{2,1,0:T(8,128)S(1)}, f32[8,8,128]{2,1,0:T(8,128)S(1)}, u32[]{:S(2)}, u32[]{:S(2)}) collective-permute-start(f32[8,8,128]{2,1,0:T(8,128)S(1)} %get-tuple-element.29.rest_0_), channel_id=1, source_target_pairs={{0,2},{1,3},{2,0},{3,1},{4,6},{5,7},{6,4},{7,5},{8,10},{9,11},{10,... | collective-permute-start | bytes 98312 | tf_op jit(solution)/shard_map/ppermute | solution.py:385
  109.2 5.2 %collective-permute-start.22 = (f32[8,8,128]{2,1,0:T(8,128)S(1)}, f32[8,8,128]{2,1,0:T(8,128)S(1)}, u32[]{:S(2)}, u32[]{:S(2)}) collective-permute-start(f32[8,8,128]{2,1,0:T(8,128)S(1)} %get-tuple-element.29.rest_0_), channel_id=1, source_target_pairs={{0,3},{1,2},{2,1},{3,0},{4,7},{5,6},{6,5},{7,4},{8,11},{9,10},{10,... | collective-permute-start | bytes 98312 | tf_op jit(solution)/shard_map/ppermute | solution.py:385
  114.4 8.9 %copy-start.1 = (bf16[2,128,1024]{2,1,0:T(8,128)(2,1)S(1)}, bf16[2,128,1024]{2,1,0:T(8,128)(2,1)}, u32[]{:S(2)}) copy-start(bf16[2,128,1024]{2,1,0:T(8,128)(2,1)} %param.10) | copy-start | bytes 1572868
  115.0 8.2 %copy-start.3 = (f32[1024]{0:T(1024)S(1)}, f32[1024]{0:T(1024)}, u32[]{:S(2)}) copy-start(f32[1024]{0:T(1024)} %param.19) | copy-start | bytes 12292
  115.0 5.0 %collective-permute-start.23 = (bf16[256,256]{1,0:T(8,128)(2,1)S(1)}, bf16[256,256]{1,0:T(8,128)(2,1)S(1)}, u32[]{:S(2)}, u32[]{:S(2)}) collective-permute-start(bf16[256,256]{1,0:T(8,128)(2,1)S(1)} %get-tuple-element.31), channel_id=1, source_target_pairs={{0,1},{1,0},{2,3},{3,2},{4,5},{5,4},{6,7},{7,6},{8,9},{9,8},{10,11... | collective-permute-start | bytes 393224 | tf_op jit(solution)/shard_map/ppermute | solution.py:385
  115.5 5.8 %collective-permute-start.24 = (bf16[256,256]{1,0:T(8,128)(2,1)S(1)}, bf16[256,256]{1,0:T(8,128)(2,1)S(1)}, u32[]{:S(2)}, u32[]{:S(2)}) collective-permute-start(bf16[256,256]{1,0:T(8,128)(2,1)S(1)} %get-tuple-element.32), channel_id=1, source_target_pairs={{0,2},{1,3},{2,0},{3,1},{4,6},{5,7},{6,4},{7,5},{8,10},{9,11},{10,... | collective-permute-start | bytes 393224 | tf_op jit(solution)/shard_map/ppermute | solution.py:385
  117.3 5.9 %collective-permute-start.25 = (bf16[256,256]{1,0:T(8,128)(2,1)S(1)}, bf16[256,256]{1,0:T(8,128)(2,1)S(1)}, u32[]{:S(2)}, u32[]{:S(2)}) collective-permute-start(bf16[256,256]{1,0:T(8,128)(2,1)S(1)} %get-tuple-element.33), channel_id=1, source_target_pairs={{0,3},{1,2},{2,1},{3,0},{4,7},{5,6},{6,5},{7,4},{8,11},{9,10},{10,... | collective-permute-start | bytes 393224 | tf_op jit(solution)/shard_map/ppermute | solution.py:385
  123.2 0.7 copy-start.4

commit v2 on v1

--- a/solution.py
+++ b/solution.py
@@ -8,6 +8,7 @@
 
 HEADS = 8
 CORES = 2
+TAG_ROWS = 16
 
 
 epsilon = 1e-05
@@ -109,14 +110,13 @@
 
 
 def kernel_call(body, out_shape, in_specs, scratch, out_specs=None, flops=0, vmem=16):
-    any_or_vmem = out_specs
-    if any_or_vmem is None:
-        any_or_vmem = jax.tree.map(lambda _: pl.BlockSpec(memory_space=pltpu.VMEM), out_shape)
+    if out_specs is None:
+        out_specs = jax.tree.map(lambda _: pl.BlockSpec(memory_space=pltpu.VMEM), out_shape)
     return pl.pallas_call(
         body,
         out_shape=out_shape,
         in_specs=in_specs,
-        out_specs=any_or_vmem,
+        out_specs=out_specs,
         scratch_shapes=scratch,
         cost_estimate=pl.CostEstimate(flops=flops, transcendentals=0, bytes_accessed=1),
         compiler_params=pltpu.CompilerParams(vmem_limit_bytes=vmem * 1024 * 1024),
@@ -134,93 +134,162 @@
 SMEM = pl.BlockSpec(memory_space=pltpu.SMEM)
 
 
-def columns_for_peers(array, parts, helpers):
-    lead, width = array.shape[:-1], array.shape[-1]
+def columns_for_peers(arrays, parts, helpers):
+    rows, width = arrays[0].shape[-2:]
     features = width // parts
     feats = features // helpers
 
-    def body(in_ref, *outs):
+    def body(*refs):
+        in_refs, outs = refs[: len(arrays)], refs[len(arrays) :]
         mine = lax.axis_index("helper")
         for rel in range(helpers):
             start = pl.multiple_of((mine ^ rel) * feats, feats)
-            for part in range(parts):
-                outs[rel][..., pl.ds(part * feats, feats)] = in_ref[
-                    ..., pl.ds(part * features + start, feats)
-                ]
-
-    return kernel_call(body, [jax.ShapeDtypeStruct(lead + (parts * feats,), array.dtype)] * helpers, [VMEM], [])(array)
-
-
-def weight_copies(refs, scratch, sems, rows, helpers, planes):
+            for at, ref in enumerate(in_refs):
+                for part in range(parts):
+                    outs[rel][at, :, pl.ds(part * feats, feats)] = ref[:, pl.ds(part * features + start, feats)]
+
+    return kernel_call(
+        body,
+        [jax.ShapeDtypeStruct((len(arrays), rows, parts * feats), arrays[0].dtype)] * helpers,
+        [VMEM] * len(arrays),
+        [],
+    )(*arrays)
+
+
+def prefix_for_peers(keys, values, users, helpers):
+    prefix, features = keys.shape
+    feats = features // helpers
+    blocks = users.shape[0]
+
+    def body(users_ref, k_ref, v_ref, *outs):
+        mine = lax.axis_index("helper")
+        row = lax.broadcasted_iota(jnp.int32, (TAG_ROWS, feats), 0)
+        tags = jnp.zeros((TAG_ROWS, feats), jnp.int32)
+        for block in range(blocks):
+            tags = jnp.where(row == block, users_ref[block], tags)
+        for rel in range(helpers):
+            columns = pl.ds(pl.multiple_of((mine ^ rel) * feats, feats), feats)
+            outs[rel][pl.ds(0, prefix)] = k_ref[:, columns]
+            outs[rel][pl.ds(prefix, prefix)] = v_ref[:, columns]
+            outs[rel][pl.ds(2 * prefix, TAG_ROWS)] = tags.astype(jnp.float32).astype(jnp.bfloat16)
+
+    shape = (2 * prefix + TAG_ROWS, feats)
+    return kernel_call(
+        body,
+        [pltpu.HBM(shape, keys.dtype)] + [jax.ShapeDtypeStruct(shape, keys.dtype)] * (helpers - 1),
+        [SMEM, VMEM, VMEM],
+        [],
+        [VMEM] * helpers,
+    )(*in_hbm([users, keys, values]))
+
+
+def normalise(values, gain):
+    average = jnp.mean(values, axis=-1, keepdims=True)
+    centred = values - average
+    spread = jnp.mean(centred * centred, axis=-1, keepdims=True)
+    return (centred * lax.rsqrt(spread + epsilon) * gain).astype(jnp.bfloat16)
+
+
+def norm_rows(arrays, gain, halves):
+    def body(gain_ref, *refs):
+        outs = list(refs[len(arrays) :])
+        for ref in refs[: len(arrays)]:
+            step = ref.shape[0] // halves
+            for first in range(0, ref.shape[0], step):
+                out = outs.pop(0)
+                for at in range(0, step, 128):
+                    out[pl.ds(at, 128)] = normalise(
+                        ref[pl.ds(first + at, 128)].astype(jnp.float32), gain_ref[...]
+                    )
+
+    shapes = [
+        pltpu.HBM((array.shape[0] // halves, array.shape[1]), jnp.bfloat16)
+        for array in arrays
+        for _ in range(halves)
+    ]
+    specs = [VMEM] * len(shapes)
+    return kernel_call(body, shapes, [VMEM] * (1 + len(arrays)), [], specs)(*in_hbm([gain]), *arrays)
+
+
+def weight_copies(refs, scratch, sems, rows, helpers, planes, by_plane):
     group, mine = lax.axis_index("group"), lax.axis_index("helper")
     plane, core = group // CORES, lax.rem(group, CORES)
     copies = []
     for at, ref in enumerate(refs):
-        turn, swap = at // CORES, at % CORES
-        source = lax.rem(plane + planes - turn, planes) * CORES + (core ^ swap)
-        for rel in range(helpers):
-            start = pl.multiple_of((source * helpers + (mine ^ rel)) * rows, rows)
+        outer, swap = at // CORES, at % CORES
+        for inner in range(helpers if by_plane else planes):
+            turn, rel = (outer, inner) if by_plane else (inner, outer)
+            source = ((plane ^ turn) * CORES + (core ^ swap)) * helpers + (mine ^ rel)
             copies.append(
                 pltpu.make_async_copy(
-                    ref.at[pl.ds(rel * rows, rows)], scratch.at[pl.ds(start, rows)], sems.at[len(copies)]
+                    ref.at[pl.ds(inner * rows, rows)],
+                    scratch.at[pl.ds(pl.multiple_of(source * rows, rows), rows)],
+                    sems.at[len(copies)],
                 )
             )
     return copies
 
 
-def attend(cands, weights, prefixes, users, gain, rows, planes, rows_block):
+def attend(cands, weights, prefixes, rows, planes, rows_block):
     helpers = len(prefixes)
-    (_, _, first), *_ = cands
-    count, features = first.shape
+    count, features = sum(array.shape[0] for rel, _, array in cands if rel == 0), cands[0][2].shape[1]
     n_cands = len(cands)
     width = weights[0].shape[1]
     feats = width // 4
-    prefix = prefixes[0].shape[1]
+    prefix = (prefixes[0].shape[0] - TAG_ROWS) // 2
     head_dim = features // HEADS
     heads = feats // head_dim
     scale = head_dim ** (-0.5)
     blocks = count // rows_block
     n_weights = len(weights)
 
-    def body(users_ref, gain_ref, *rest):
+    def body(*rest):
         cand_refs, rest = rest[:n_cands], rest[n_cands:]
         weight_refs, rest = rest[:n_weights], rest[n_weights:]
         prefix_refs, rest = rest[:helpers], rest[helpers:]
         mixed_ref, gate_ref, stats_ref = rest[:3]
-        cand, normed, weight, keys, vals, proj, c_sems, w_sems, p_sems = rest[3:]
+        normed, weight, keys, vals, tags, proj, c_sems, w_sems, p_sems, t_sems = rest[3:]
         c_copies = [
-            pltpu.make_async_copy(ref, cand.at[rel, pl.ds(start, ref.shape[0])], c_sems.at[at])
+            pltpu.make_async_copy(ref, normed.at[rel, pl.ds(start, ref.shape[0])], c_sems.at[at])
             for at, ((rel, start, _), ref) in enumerate(zip(cands, cand_refs))
         ]
         p_copies = [
             pltpu.make_async_copy(
-                prefix_refs[rel].at[part], held.at[pl.ds(rel * prefix, prefix)], p_sems.at[2 * rel + part]
+                prefix_refs[rel].at[pl.ds(part * prefix, prefix)],
+                held.at[pl.ds(rel * prefix, prefix)],
+                p_sems.at[2 * rel + part],
             )
             for rel in range(helpers)
             for part, held in enumerate((keys, vals))
         ]
-        w_copies = weight_copies(weight_refs, weight, w_sems, rows, helpers, planes)
-        for copy in c_copies + w_copies + p_copies:
+        w_copies = weight_copies(weight_refs, weight, w_sems, rows, helpers, planes, True)
+        t_copies = [
+            pltpu.make_async_copy(
+                prefix_refs[rel].at[pl.ds(2 * prefix, TAG_ROWS)], tags.at[rel], t_sems.at[rel]
+            )
+            for rel in range(helpers)
+        ]
+        for copy in t_copies + w_copies + c_copies + p_copies:
             copy.start()
-        for rel in range(helpers):
-            for (at, _, _), copy in zip(cands, c_copies):
-                if at == rel:
-                    copy.wait()
-            values = cand[rel].astype(jnp.float32)
-            average = jnp.mean(values, axis=-1, keepdims=True)
-            centred = values - average
-            spread = jnp.mean(centred * centred, axis=-1, keepdims=True)
-            normed[rel] = (centred * lax.rsqrt(spread + epsilon) * gain_ref[...]).astype(jnp.bfloat16)
-        for copy in w_copies:
+        for copy in t_copies:
             copy.wait()
-        for copy in p_copies:
+        mine = lax.axis_index("helper")
+        owners = [
+            jnp.max(tags[rel, pl.ds(block, 1), :128].astype(jnp.float32)).astype(jnp.int32) ^ mine
+            for rel in range(helpers)
+            for block in range(blocks)
+        ]
+        for copy in w_copies + c_copies:
             copy.wait()
         lane = lax.broadcasted_iota(jnp.int32, (rows_block, 128), 1)
         for rel in range(helpers):
             proj[...] = silu(jnp.dot(normed[rel], weight[...], preferred_element_type=jnp.float32))
             gate_ref[pl.ds(rel * count, count)] = proj[:, :feats]
+            if rel == 0:
+                for copy in p_copies:
+                    copy.wait()
             for block in range(blocks):
-                user = pl.multiple_of(users_ref[rel * blocks + block] * prefix, prefix)
+                user = pl.multiple_of(owners[rel * blocks + block] * prefix, prefix)
                 here = pl.ds(block * rows_block, rows_block)
                 out = []
                 for head in range(heads):
@@ -261,19 +330,18 @@
     n_pieces = n_weights * helpers
     scratch = [
         pltpu.VMEM((helpers, count, features), jnp.bfloat16),
-        pltpu.VMEM((helpers, count, features), jnp.bfloat16),
         pltpu.VMEM((features, width), jnp.bfloat16),
         pltpu.VMEM((helpers * prefix, feats), jnp.bfloat16),
         pltpu.VMEM((helpers * prefix, feats), jnp.bfloat16),
+        pltpu.VMEM((helpers, TAG_ROWS, feats), jnp.bfloat16),
         pltpu.VMEM((count, width), jnp.float32),
         pltpu.SemaphoreType.DMA((n_cands,)),
         pltpu.SemaphoreType.DMA((n_pieces,)),
         pltpu.SemaphoreType.DMA((2 * helpers,)),
+        pltpu.SemaphoreType.DMA((helpers,)),
     ]
     arrays = in_hbm([array for _, _, array in cands] + list(weights) + list(prefixes))
-    return kernel_call(
-        body, shapes, [SMEM, VMEM] + [ANY] * len(arrays), scratch, flops=2 * total_rows * features * width
-    )(users, gain, *arrays)
+    return kernel_call(body, shapes, [ANY] * len(arrays), scratch, flops=2 * total_rows * features * width)(*arrays)
 
 
 def gate(mixed, gates, stats, gain, helpers, rows_block):
@@ -284,6 +352,8 @@
 
     def body(mixed_ref, gate_ref, gain_ref, *rest):
         stats_refs, outs = rest[:helpers], rest[helpers:]
+        mine = lax.axis_index("helper")
+        my_gain = gain_ref[:, pl.ds(pl.multiple_of(mine * feats, feats), feats)]
         for rel in range(helpers):
             for block in range(blocks):
                 parts = [stats_refs[peer][(rel ^ peer) * blocks + block] for peer in range(helpers)]
@@ -296,7 +366,7 @@
                 both = jnp.where(row == 0, average, jnp.where(row == 1, level, 0.0)).T
                 here = pl.ds(rel * count + block * rows_block, rows_block)
                 outs[rel][pl.ds(block * rows_block, rows_block)] = (
-                    (mixed_ref[here] - both[:, 0:1]) * both[:, 1:2] * gain_ref[...] * gate_ref[here]
+                    (mixed_ref[here] - both[:, 0:1]) * both[:, 1:2] * my_gain * gate_ref[here]
                 ).astype(jnp.bfloat16)
 
     return kernel_call(
@@ -308,22 +378,36 @@
     )(mixed, gates, gain, *stats)
 
 
-def project_out(gated, weights, cands, live, vec, rows, planes, rows_block):
+def assemble(weights, rows, helpers, planes):
+    n_weights = len(weights)
+    width = weights[0].shape[1]
+    features = CORES * planes * helpers * rows
+
+    def body(*refs):
+        weight_refs, out, sems = refs[:n_weights], refs[n_weights], refs[n_weights + 1]
+        copies = weight_copies(weight_refs, out, sems, rows, helpers, planes, False)
+        for copy in copies:
+            copy.start()
+        for copy in copies:
+            copy.wait()
+
+    return kernel_call(
+        body,
+        jax.ShapeDtypeStruct((features, width), weights[0].dtype),
+        [ANY] * n_weights,
+        [pltpu.SemaphoreType.DMA((n_weights * planes,))],
+    )(*in_hbm(weights))
+
+
+def project_out(gated, weight, cands, live, vec, rows_block):
     helpers = len(gated)
     count, features = cands.shape
     feats = features // helpers
     blocks = count // rows_block
-    n_weights = len(weights)
-
-    def body(live_ref, vec_ref, cand_ref, *rest):
+
+    def body(live_ref, vec_ref, cand_ref, weight, *rest):
         gated_refs = rest[:helpers]
-        weight_refs = rest[helpers : helpers + n_weights]
-        emb_ref, score_ref, weight, w_sems = rest[helpers + n_weights :]
-        copies = weight_copies(weight_refs, weight, w_sems, rows, helpers, planes)
-        for copy in copies:
-            copy.start()
-        for copy in copies:
-            copy.wait()
+        emb_ref, score_ref = rest[helpers:]
         mine = lax.axis_index("helper")
         lane = lax.broadcasted_iota(jnp.int32, (1, rows_block), 1)
         for block in range(blocks):
@@ -349,17 +433,9 @@
         jax.ShapeDtypeStruct((count, features), jnp.bfloat16),
         jax.ShapeDtypeStruct((blocks, rows_block), jnp.float32),
     ]
-    scratch = [
-        pltpu.VMEM((features, features), jnp.bfloat16),
-        pltpu.SemaphoreType.DMA((n_weights * helpers,)),
-    ]
     return kernel_call(
-        body,
-        shapes,
-        [SMEM] + [VMEM] * (2 + helpers) + [ANY] * n_weights,
-        scratch,
-        flops=2 * count * features * features,
-    )(live, vec, cands, *gated, *in_hbm(weights))
+        body, shapes, [SMEM] + [VMEM] * (3 + helpers), [], flops=2 * count * features * features
+    )(live, vec, cands, weight, *gated)
 
 
 def by_heads(
@@ -377,61 +453,66 @@
     helpers, groups = lax.axis_size("helper"), lax.axis_size("group")
     planes = groups // CORES
     blocks, rows_block, features = candidates.shape
-    feats = features // helpers
     rows = w_proj.shape[0]
-    mine = lax.axis_index("helper")
-
-    def sent(array, axis, pairs):
-        return lax.ppermute(array, axis, pairs)
 
     def to_peers(pieces):
         return [pieces[0]] + [
-            sent(pieces[rel], "helper", [(at, at ^ rel) for at in range(helpers)])
+            lax.ppermute(pieces[rel], "helper", [(at, at ^ rel) for at in range(helpers)])
             for rel in range(1, len(pieces))
         ]
 
-    def everyone(rows_here):
-        if helpers != 4:
-            return [(rel, 0, part) for rel, part in enumerate(to_peers([rows_here] * helpers))]
-        near = to_peers([rows_here] * 3)
+    def everyone(rows_here, gain):
+        near = to_peers([rows_here] * (3 if helpers == 4 else helpers))
+        normed = norm_rows(near, gain, 2)
         half = rows_here.shape[0] // 2
-        far = []
-        for at, (over, of) in enumerate(((2, 1), (1, 2))):
-            pairs = [(here, here ^ over) for here in range(helpers)]
-            far.append((3, at * half, sent(near[of][at * half : (at + 1) * half], "helper", pairs)))
-        return [(rel, 0, part) for rel, part in enumerate(near)] + far
-
-    def spread(pieces):
-        shard = jnp.concatenate(pieces, axis=0)
-        out = []
-        for turn in range(planes):
-            held = shard
-            if turn:
-                pairs = [(at, (at + CORES * turn) % groups) for at in range(groups)]
-                held = sent(shard, "group", pairs)
-            swap = [(at, at ^ 1) for at in range(groups)]
-            out += [held, sent(held, "group", swap)]
+        out = [(at // 2, at % 2 * half, part) for at, part in enumerate(normed)]
+        if helpers == 4:
+            for at, (over, part) in enumerate(((2, normed[2]), (1, normed[5]))):
+                pairs = [(here, here ^ over) for here in range(helpers)]
+                out.append((3, at * half, lax.ppermute(part, "helper", pairs)))
         return out
 
+    def to_plane(array, turn):
+        return lax.ppermute(array, "group", [(at, at ^ (CORES * turn)) for at in range(groups)])
+
+    def to_core(array):
+        return lax.ppermute(array, "group", [(here, here ^ 1) for here in range(groups)])
+
+    def to_planes(shard):
+        if planes != 4:
+            return [shard] + [to_plane(shard, turn) for turn in range(1, planes)]
+        near, across = to_plane(shard, 1), to_plane(shard, 2)
+        inner = [CORES + core for core in range(CORES)]
+        pairs = [(at, at ^ (3 * CORES)) for here in inner for at in (here, here + CORES)]
+        middle = lax.ppermute(shard, "group", pairs)
+        pairs = [(at, at ^ CORES) for here in inner for at in (here, here + CORES)]
+        ends = lax.ppermute(across, "group", pairs)
+        plane = lax.axis_index("group") // CORES
+        return [shard, near, across, jnp.where((plane == 0) | (plane == 3), ends, middle)]
+
+    def with_swaps(shards):
+        return [part for shard in shards for part in (shard, to_core(shard))]
+
     cand_rows = candidates.reshape(blocks * rows_block, features)
-    w_pieces = columns_for_peers(w_proj, 4, helpers)
-    both = jnp.concatenate([prefix_keys, prefix_values], axis=0)
-    prefix_pieces = columns_for_peers(both, 1, helpers)
-    proj_shards = spread(to_peers(w_pieces))
-    cands = everyone(cand_rows)
+    gain = gain_in.reshape(1, features)
+    w_pieces = columns_for_peers(in_hbm([w_proj]), 4, helpers)
+    prefix_pieces = prefix_for_peers(prefix_keys[0], prefix_values[0], block_user, helpers)
+    w_shard = jnp.concatenate(to_peers([piece[0] for piece in w_pieces]), axis=0)
+    proj_shards = with_swaps(to_planes(w_shard))
+    cands = everyone(cand_rows, gain)
     prefixes = to_peers(prefix_pieces)
-    users = jnp.concatenate(to_peers([block_user] * helpers)) ^ mine
-    out_shards = spread(to_peers([w_out] * helpers))
+    o_shard = jnp.concatenate([w_out] + [to_plane(w_out, turn) for turn in range(1, planes)], axis=0)
+    out_shards = with_swaps(to_peers([o_shard] * helpers))
 
     mixed, gates, stats = attend(
-        cands, proj_shards, prefixes, users, gain_in.reshape(1, features), rows, planes, rows_block
+        cands, proj_shards, prefixes, rows, planes, rows_block
     )
     all_stats = to_peers([stats] * helpers)
-    my_gain = lax.dynamic_slice_in_dim(gain_mid.reshape(1, features), mine * feats, feats, axis=1)
-    gated = gate(mixed, gates, all_stats, my_gain, helpers, rows_block)
+    gated = gate(mixed, gates, all_stats, gain_mid.reshape(1, features), helpers, rows_block)
     arrived = to_peers(gated)
+    out_full = assemble(out_shards, rows, helpers, planes)
     embeddings, scores = project_out(
-        arrived, out_shards, cand_rows, live_rows, score_vec.reshape(1, features), rows, planes, rows_block
+        arrived, out_full, cand_rows, live_rows, score_vec.reshape(1, features), rows_block
     )
     return embeddings.reshape(candidates.shape), scores
 
@@ -442,7 +523,8 @@
 
 def solution(mesh):
     helpers, groups = mesh.shape["helper"], mesh.shape["group"]
-    split = HEADS % helpers == 0 and helpers & (helpers - 1) == 0 and groups % CORES == 0
+    split = HEADS % helpers == 0 and helpers > 1 and groups % CORES == 0
+    split = split and helpers & (helpers - 1) == 0 and groups & (groups - 1) == 0
     placed = (
         P(("group", "helper"), None, None),
         P(("group", "helper")),

time: 128 us -> 105 us (0.82)
  the two profiles are of different devices: /device:TPU:8 before, /device:TPU:0 now
where the time goes in v2:
time: 105 us; the launch traced here: 104 us
  starting transfers between devices  42 us (40%)
  waiting for transfers between devices  40.7 us (39%)
  Pallas kernels  17.5 us (17%)
  local copies, waits for them, and re-layouts  3.02 us (3%)
    ppermute x17, waiting for transfers between devices, to_peers(): lax.ppermute(pieces[rel], 'helper', [(at, at ^ rel) for at in range(helpe...  25.7 us
    ppermute x17, starting transfers between devices, to_peers(): lax.ppermute(pieces[rel], 'helper', [(at, at ^ rel) for at in range(helpe...  25.6 us
    ppermute x5, waiting for transfers between devices, to_plane(): lax.ppermute(array, 'group', [(at, at ^ CORES * turn) for at in range(gro...  11.1 us
    ppermute x5, starting transfers between devices, to_plane(): lax.ppermute(array, 'group', [(at, at ^ CORES * turn) for at in range(gro...  8.47 us
    pallas_call x1, Pallas kernels, attend(): kernel_call(body, shapes, [ANY] * len(arrays), scratch, flops=2 * total_r...  7 us
    ppermute x2, starting transfers between devices, everyone(): out.append((3, at * half, lax.ppermute(part, 'helper', pairs)))  4.36 us
    ppermute x2, waiting for transfers between devices, everyone(): out.append((3, at * half, lax.ppermute(part, 'helper', pairs)))  3.95 us
    unnamed x51, local copies, waits for them, and re-layouts  3.01 us
  transfers between devices with their start and end apart: 34, of which 12 were waited for; matrix products, arithmetic and copies ran while one was open for 1% of the time, Pallas kernels for 14%

profile of v2, /device:TPU:0, one launch (start us, length us, event | category | flops | bytes accessed | tf_op | source)
XLA Modules:
  0.0 104.2 jit_solution(12466222182785453544)
XLA Ops:
  0.6 0.0 copy-start
  0.6 1.0 %shard_map.115 = (bf16[1,32,1024]{2,1,0:T(8,128)(2,1)S(1)}, bf16[1,32,1024]{2,1,0:T(8,128)(2,1)S(1)}, bf16[1,32,1024]{2,1,0:T(8,128)(2,1)S(1)}, bf16[1,32,1024]{2,1,0:T(8,128)(2,1)S(1)}) custom-call(bf16[32,4096]{1,0:T(8,128)(2,1)} %refs_0_.1), custom_call_target="tpu_custom_call" | custom-call | bytes 1 | tf_op jit(solution)/shard_map/pallas_call | solution.py:151
  1.7 3.0 %collective-permute-start.14 = (bf16[32,1024]{1,0:T(8,128)(2,1)S(1)}, bf16[32,1024]{1,0:T(8,128)(2,1)S(1)}, u32[]{:S(2)}, u32[]{:S(2)}) collective-permute-start(bf16[32,1024]{1,0:T(8,128)(2,1)S(1)} %bitcast.20), channel_id=1, source_target_pairs={{0,1},{1,0},{2,3},{3,2},{4,5},{5,4},{6,7},{7,6},{8,9},{9,8},{10,11... | collective-permute-start | bytes 196616 | tf_op jit(solution)/shard_map/ppermute | solution.py:460
  4.7 1.5 %collective-permute-start.15 = (bf16[32,1024]{1,0:T(8,128)(2,1)S(1)}, bf16[32,1024]{1,0:T(8,128)(2,1)S(1)}, u32[]{:S(2)}, u32[]{:S(2)}) collective-permute-start(bf16[32,1024]{1,0:T(8,128)(2,1)S(1)} %bitcast.19), channel_id=1, source_target_pairs={{0,2},{1,3},{2,0},{3,1},{4,6},{5,7},{6,4},{7,5},{8,10},{9,11},{10,... | collective-permute-start | bytes 196616 | tf_op jit(solution)/shard_map/ppermute | solution.py:460
  6.2 0.0 collective-permute-start.16
  6.3 2.1 %shard_map.116 = (bf16[528,256]{1,0:T(8,128)(2,1)}, bf16[528,256]{1,0:T(8,128)(2,1)S(1)}, bf16[528,256]{1,0:T(8,128)(2,1)S(1)}, bf16[528,256]{1,0:T(8,128)(2,1)S(1)}) custom-call(s32[2]{0:T(128)} %users_ref.1, bf16[256,1024]{1,0:T(8,128)(2,1)} %bitcast.21, bf16[256,1024]{1,0:T(8,128)(2,1)} %bitcast.22), custom_call_target="tpu_custom_call" | custom-call | bytes 1 | tf_op jit(solution)/shard_map/pallas_call | solution.py:177
  8.3 1.9 %collective-permute-start.25 = (bf16[528,256]{1,0:T(8,128)(2,1)S(1)}, bf16[528,256]{1,0:T(8,128)(2,1)S(1)}, u32[]{:S(2)}, u32[]{:S(2)}) collective-permute-start(bf16[528,256]{1,0:T(8,128)(2,1)S(1)} %get-tuple-element.36), channel_id=1, source_target_pairs={{0,1},{1,0},{2,3},{3,2},{4,5},{5,4},{6,7},{7,6},{8,9},{9,8},{10,11... | collective-permute-start | bytes 811016 | tf_op jit(solution)/shard_map/ppermute | solution.py:460
  10.3 1.5 %collective-permute-start.26 = (bf16[528,256]{1,0:T(8,128)(2,1)S(1)}, bf16[528,256]{1,0:T(8,128)(2,1)S(1)}, u32[]{:S(2)}, u32[]{:S(2)}) collective-permute-start(bf16[528,256]{1,0:T(8,128)(2,1)S(1)} %get-tuple-element.37), channel_id=1, source_target_pairs={{0,2},{1,3},{2,0},{3,1},{4,6},{5,7},{6,4},{7,5},{8,10},{9,11},{10,... | collective-permute-start | bytes 811016 | tf_op jit(solution)/shard_map/ppermute | solution.py:460
  11.8 1.6 %collective-permute-start = (bf16[32,1024]{1,0:T(8,128)(2,1)}, bf16[32,1024]{1,0:T(8,128)(2,1)S(1)}, u32[]{:S(2)}, u32[]{:S(2)}) collective-permute-start(bf16[32,1024]{1,0:T(8,128)(2,1)} %param.16), channel_id=1, source_target_pairs={{0,8},{4,12},{8,0},{12,4},{16,24},{20,28},{24,16},{28,20},{1,9},{5... | collective-permute-start | bytes 196616 | tf_op jit(solution)/shard_map/ppermute | solution.py:476
  13.4 2.7 %collective-permute-start.20 = (bf16[128,1024]{1,0:T(8,128)(2,1)S(1)}, bf16[128,1024]{1,0:T(8,128)(2,1)S(1)}, u32[]{:S(2)}, u32[]{:S(2)}) collective-permute-start(bf16[128,1024]{1,0:T(8,128)(2,1)S(1)} %pad_maximum_fusion.rest_8_), channel_id=1, source_target_pairs={{0,16},{4,20},{8,24},{12,28},{16,0},{20,4},{24,8},{28,12},{1,17},{... | collective-permute-start | bytes 786440 | tf_op jit(solution)/shard_map/ppermute | solution.py:476
  16.1 0.3 collective-permute-start.1
  16.4 0.2 collective-permute-done
  16.6 3.9 %collective-permute-start.2 = (bf16[32,1024]{1,0:T(8,128)(2,1)}, bf16[32,1024]{1,0:T(8,128)(2,1)S(1)}, u32[]{:S(2)}, u32[]{:S(2)}) collective-permute-start(bf16[32,1024]{1,0:T(8,128)(2,1)} %param.16), channel_id=1, source_target_pairs={{0,24},{4,28},{8,16},{12,20},{16,8},{20,12},{24,0},{28,4},{1,25},{... | collective-permute-start | bytes 196616 | tf_op jit(solution)/shard_map/ppermute | solution.py:476
  20.5 10.8 %collective-permute-done.1 = bf16[32,1024]{1,0:T(8,128)(2,1)S(1)} collective-permute-done((bf16[32,1024]{1,0:T(8,128)(2,1)}, bf16[32,1024]{1,0:T(8,128)(2,1)S(1)}, u32[]{:S(2)}, u32[]{:S(2)}) %collective-permute-start.1) | collective-permute-done | bytes 65568 | tf_op jit(solution)/shard_map/ppermute | solution.py:476
  31.3 0.5 collective-permute-start.10
  31.8 0.5 collective-permute-start.11
  32.3 0.8 constant_dynamic-update-slice_fusion.3
  33.2 0.0 collective-permute-done.25.rest_17_
  33.2 2.5 %collective-permute-start.27 = (bf16[528,256]{1,0:T(8,128)(2,1)S(1)}, bf16[528,256]{1,0:T(8,128)(2,1)S(1)}, u32[]{:S(2)}, u32[]{:S(2)}) collective-permute-start(bf16[528,256]{1,0:T(8,128)(2,1)S(1)} %get-tuple-element.38), channel_id=1, source_target_pairs={{0,3},{1,2},{2,1},{3,0},{4,7},{5,6},{6,5},{7,4},{8,11},{9,10},{10,... | collective-permute-start | bytes 811016 | tf_op jit(solution)/shard_map/ppermute | solution.py:460
  35.7 0.0 collective-permute-done.26.rest_18_
  35.7 0.7 collective-permute-start.23
  36.4 0.0 collective-permute-done.20.rest_12_
  36.4 1.3 %collective-permute-start.22 = (bf16[128,1024]{1,0:T(8,128)(2,1)S(1)}, bf16[128,1024]{1,0:T(8,128)(2,1)S(1)}, u32[]{:S(2)}, u32[]{:S(2)}) collective-permute-start(bf16[128,1024]{1,0:T(8,128)(2,1)S(1)} %collective-permute-done.20.rest_12_), channel_id=1, source_target_pairs={{8,0},{16,24},{12,4},{20,28},{9,1},{17,25},{13,5},{21,29},{10,2},{... | collective-permute-start | bytes 786440 | tf_op jit(solution)/shard_map/ppermute | solution.py:489
  37.7 12.0 %collective-permute-done.27.rest_19_ = bf16[528,256]{1,0:T(8,128)(2,1)S(1)} collective-permute-done((bf16[528,256]{1,0:T(8,128)(2,1)S(1)}, bf16[528,256]{1,0:T(8,128)(2,1)S(1)}, u32[]{:S(2)}, u32[]{:S(2)}) %collective-permute-start.27) | collective-permute-done | bytes 270368 | tf_op jit(solution)/shard_map/ppermute | solution.py:460
  49.7 0.0 collective-permute-start.18
  49.7 0.0 collective-permute-done.23
  49.7 0.1 collective-permute-start.17
  49.8 0.6 collective-permute-start.4
  50.4 1.5 %collective-permute-start.6 = (bf16[128,1024]{1,0:T(8,128)(2,1)S(1)}, bf16[128,1024]{1,0:T(8,128)(2,1)S(1)}, u32[]{:S(2)}, u32[]{:S(2)}) collective-permute-start(bf16[128,1024]{1,0:T(8,128)(2,1)S(1)} %constant_dynamic-update-slice_fusion.refs_0_), channel_id=1, source_target_pairs={{0,2},{1,3},{2,0},{3,1},{4,6},{5,7},{6,4},{7,5},{8,10},{9,11},{10,... | collective-permute-start | bytes 786440 | tf_op jit(solution)/shard_map/ppermute | solution.py:460
  51.9 1.4 %collective-permute-start.8 = (bf16[128,1024]{1,0:T(8,128)(2,1)S(1)}, bf16[128,1024]{1,0:T(8,128)(2,1)S(1)}, u32[]{:S(2)}, u32[]{:S(2)}) collective-permute-start(bf16[128,1024]{1,0:T(8,128)(2,1)S(1)} %constant_dynamic-update-slice_fusion.refs_0_), channel_id=1, source_target_pairs={{0,3},{1,2},{2,1},{3,0},{4,7},{5,6},{6,5},{7,4},{8,11},{9,10},{10,... | collective-permute-start | bytes 786440 | tf_op jit(solution)/shard_map/ppermute | solution.py:460
  53.4 2.6 %shard_map.114 = (bf16[128,1024]{1,0:T(8,128)(2,1)}, bf16[128,1024]{1,0:T(8,128)(2,1)}, bf16[128,1024]{1,0:T(8,128)(2,1)}, bf16[128,1024]{1,0:T(8,128)(2,1)}, bf...) custom-call(f32[1,1024]{1,0:T(1,128)} %bitcast.23, bf16[256,1024]{1,0:T(8,128)(2,1)S(1)} %bitcast.13, ...), custom_call_target="tpu_custom_call" | custom-call | bytes 1 | tf_op jit(solution)/shard_map/pallas_call | solution.py:211
  56.1 0.1 collective-permute-done.18.rest_10_
  56.2 0.5 collective-permute-start.19
  56.7 2.3 %collective-permute-done.4.refs_2_ = bf16[128,1024]{1,0:T(8,128)(2,1)S(1)} collective-permute-done((bf16[128,1024]{1,0:T(8,128)(2,1)S(1)}, bf16[128,1024]{1,0:T(8,128)(2,1)S(1)}, u32[]{:S(2)}, u32[]{:S(2)}) %collective-permute-start.4) | collective-permute-done | bytes 262176 | tf_op jit(solution)/shard_map/ppermute | solution.py:460
  59.0 1.4 %collective-permute-start.12 = (bf16[128,1024]{1,0:T(8,128)(2,1)}, bf16[128,1024]{1,0:T(8,128)(2,1)S(1)}, u32[]{:S(2)}, u32[]{:S(2)}) collective-permute-start(bf16[128,1024]{1,0:T(8,128)(2,1)} %get-tuple-element.27.rest_2_), channel_id=1, source_target_pairs={{0,2},{1,3},{2,0},{3,1},{4,6},{5,7},{6,4},{7,5},{8,10},{9,11},{10,... | collective-permute-start | bytes 786440 | tf_op jit(solution)/shard_map/ppermute | solution.py:472
  60.5 2.6 %collective-permute-done.6.refs_4_ = bf16[128,1024]{1,0:T(8,128)(2,1)S(1)} collective-permute-done((bf16[128,1024]{1,0:T(8,128)(2,1)S(1)}, bf16[128,1024]{1,0:T(8,128)(2,1)S(1)}, u32[]{:S(2)}, u32[]{:S(2)}) %collective-permute-start.6) | collective-permute-done | bytes 262176 | tf_op jit(solution)/shard_map/ppermute | solution.py:460
  63.1 2.9 %collective-permute-start.13 = (bf16[128,1024]{1,0:T(8,128)(2,1)}, bf16[128,1024]{1,0:T(8,128)(2,1)S(1)}, u32[]{:S(2)}, u32[]{:S(2)}) collective-permute-start(bf16[128,1024]{1,0:T(8,128)(2,1)} %get-tuple-element.30.rest_5_), channel_id=1, source_target_pairs={{0,1},{1,0},{2,3},{3,2},{4,5},{5,4},{6,7},{7,6},{8,9},{9,8},{10,11... | collective-permute-start | bytes 786440 | tf_op jit(solution)/shard_map/ppermute | solution.py:472
  66.0 0.0 collective-permute-done.8.refs_6_
  66.1 0.5 collective-permute-start.3
  66.6 0.1 collective-permute-start.5
  66.6 3.9 %collective-permute-done.12.rest_6_ = bf16[128,1024]{1,0:T(8,128)(2,1)S(1)} collective-permute-done((bf16[128,1024]{1,0:T(8,128)(2,1)}, bf16[128,1024]{1,0:T(8,128)(2,1)S(1)}, u32[]{:S(2)}, u32[]{:S(2)}) %collective-permute-start.12) | collective-permute-done | bytes 262176 | tf_op jit(solution)/shard_map/ppermute | solution.py:472
  70.6 0.0 collective-permute-start.7
  70.6 0.5 collective-permute-start.9
  71.1 0.2 copy-done.21
  71.3 0.1 copy-done.22
  71.4 0.4 copy-done.23
  71.8 7.0 %shard_map.117 = (f32[1024,256]{1,0:T(8,128)S(1)}, f32[1024,256]{1,0:T(8,128)S(1)}, f32[8,8,128]{2,1,0:T(8,128)S(1)}) custom-call(bf16[128,1024]{1,0:T(8,128)(2,1)} %get-tuple-element.25.rest_0_, bf16[128,1024]{1,0:T(8,128)(2,1)} %get-tuple-element.26.rest_1_, bf16[128,1024]{1,0:T(8,128)(2,1)} %get-tuple-element.27.rest_2_, ...), custom_call_target="tpu_custom_call" | custom-call | flops 2147483648 | bytes 1 | tf_op jit(solution)/shard_map/pallas_call | solution.py:344
  78.9 1.7 %collective-permute-start.28 = (f32[8,8,128]{2,1,0:T(8,128)S(1)}, f32[8,8,128]{2,1,0:T(8,128)S(1)}, u32[]{:S(2)}, u32[]{:S(2)}) collective-permute-start(f32[8,8,128]{2,1,0:T(8,128)S(1)} %get-tuple-element.41.rest_0_), channel_id=1, source_target_pairs={{0,1},{1,0},{2,3},{3,2},{4,5},{5,4},{6,7},{7,6},{8,9},{9,8},{10,11... | collective-permute-start | bytes 98312 | tf_op jit(solution)/shard_map/ppermute | solution.py:460
  80.5 2.3 %collective-permute-done.28.rest_1_ = f32[8,8,128]{2,1,0:T(8,128)S(1)} collective-permute-done((f32[8,8,128]{2,1,0:T(8,128)S(1)}, f32[8,8,128]{2,1,0:T(8,128)S(1)}, u32[]{:S(2)}, u32[]{:S(2)}) %collective-permute-start.28) | collective-permute-done | bytes 32800 | tf_op jit(solution)/shard_map/ppermute | solution.py:460
  82.9 2.0 %collective-permute-start.29 = (f32[8,8,128]{2,1,0:T(8,128)S(1)}, f32[8,8,128]{2,1,0:T(8,128)S(1)}, u32[]{:S(2)}, u32[]{:S(2)}) collective-permute-start(f32[8,8,128]{2,1,0:T(8,128)S(1)} %get-tuple-element.41.rest_0_), channel_id=1, source_target_pairs={{0,2},{1,3},{2,0},{3,1},{4,6},{5,7},{6,4},{7,5},{8,10},{9,11},{10,... | collective-permute-start | bytes 98312 | tf_op jit(solution)/shard_map/ppermute | solution.py:460
  84.9 1.9 %collective-permute-done.29.rest_2_ = f32[8,8,128]{2,1,0:T(8,128)S(1)} collective-permute-done((f32[8,8,128]{2,1,0:T(8,128)S(1)}, f32[8,8,128]{2,1,0:T(8,128)S(1)}, u32[]{:S(2)}, u32[]{:S(2)}) %collective-permute-start.29) | collective-permute-done | bytes 32800 | tf_op jit(solution)/shard_map/ppermute | solution.py:460
  86.8 3.2 %collective-permute-start.30 = (f32[8,8,128]{2,1,0:T(8,128)S(1)}, f32[8,8,128]{2,1,0:T(8,128)S(1)}, u32[]{:S(2)}, u32[]{:S(2)}) collective-permute-start(f32[8,8,128]{2,1,0:T(8,128)S(1)} %get-tuple-element.41.rest_0_), channel_id=1, source_target_pairs={{0,3},{1,2},{2,1},{3,0},{4,7},{5,6},{6,5},{7,4},{8,11},{9,10},{10,... | collective-permute-start | bytes 98312 | tf_op jit(solution)/shard_map/ppermute | solution.py:460
  89.9 1.9 %collective-permute-done.30.rest_3_ = f32[8,8,128]{2,1,0:T(8,128)S(1)} collective-permute-done((f32[8,8,128]{2,1,0:T(8,128)S(1)}, f32[8,8,128]{2,1,0:T(8,128)S(1)}, u32[]{:S(2)}, u32[]{:S(2)}) %collective-permute-start.30) | collective-permute-done | bytes 32800 | tf_op jit(solution)/shard_map/ppermute | solution.py:460
  91.8 0.6 shard_map.118
  92.5 1.5 %collective-permute-start.31 = (bf16[256,256]{1,0:T(8,128)(2,1)S(1)}, bf16[256,256]{1,0:T(8,128)(2,1)S(1)}, u32[]{:S(2)}, u32[]{:S(2)}) collective-permute-start(bf16[256,256]{1,0:T(8,128)(2,1)S(1)} %get-tuple-element.43), channel_id=1, source_target_pairs={{0,1},{1,0},{2,3},{3,2},{4,5},{5,4},{6,7},{7,6},{8,9},{9,8},{10,11... | collective-permute-start | bytes 393224 | tf_op jit(solution)/shard_map/ppermute | solution.py:460
  94.0 2.0 %collective-permute-start.32 = (bf16[256,256]{1,0:T(8,128)(2,1)S(1)}, bf16[256,256]{1,0:T(8,128)(2,1)S(1)}, u32[]{:S(2)}, u32[]{:S(2)}) collective-permute-start(bf16[256,256]{1,0:T(8,128)(2,1)S(1)} %get-tuple-element.44), channel_id=1, source_target_pairs={{0,2},{1,3},{2,0},{3,1},{4,6},{5,7},{6,4},{7,5},{8,10},{9,11},{10,... | collective-permute-start | bytes 393224 | tf_op jit(solution)/shard_map/ppermute | solution.py:460
  96.1 0.1 collective-permute-start.33
  96.2 0.6 copy-done.9
  96.8 0.1 copy-done.10
  96.9 0.7 copy-done.11
  97.6 1.8 %shard_map.113.weight = bf16[1024,1024]{1,0:T(8,128)(2,1)S(1)} custom-call(bf16[128,1024]{1,0:T(8,128)(2,1)} %copy-done.4, bf16[128,1024]{1,0:T(8,128)(2,1)} %copy-done.8, bf16[128,1024]{1,0:T(8,128)(2,1)} %copy-done.5, bf16[128,1024]{1,0:T(8,128)(2,1)} %copy-done.9, bf16[128,1024]{1,0:T(8,128)(2,1)} %copy-done.6, bf16[128,1024]{1,0:T(8,128)(2,1)} %copy-done.10, ...), custom_call_target="tpu_custom_call" | custom-call | bytes 1 | tf_op jit(solution)/shard_map/pallas_call | solution.py:394
  99.4 0.5 collective-permute-done.32.rest_2_
  100.0 2.0 %collective-permute-done.33.rest_3_ = bf16[256,256]{1,0:T(8,128)(2,1)S(1)} collective-permute-done((bf16[256,256]{1,0:T(8,128)(2,1)S(1)}, bf16[256,256]{1,0:T(8,128)(2,1)S(1)}, u32[]{:S(2)}, u32[]{:S(2)}) %collective-permute-start.33) | collective-permute-done | bytes 131104 | tf_op jit(solution)/shard_map/ppermute | solution.py:460
  102.0 2.3 %shard_map.119 = (bf16[256,1024]{1,0:T(8,128)(2,1)}, f32[2,128]{1,0:T(2,128)}) custom-call(s32[2]{0:T(128)S(1)} %copy-done.3, f32[1,1024]{1,0:T(1,128)S(1)} %bitcast.17, bf16[256,1024]{1,0:T(8,128)(2,1)S(1)} %bitcast.14, bf16[1024,1024]{1,0:T(8,128)(2,1)S(1)} %shard_map.113.weight, bf16[256,256]{1,0:T(8,128)(2,1)S(1)} %get-tuple-element.42.rest_0_, ...), custom_call_target="tpu_custom_call" | custom-call | flops 536870912 | bytes 1 | tf_op jit(solution)/shard_map/pallas_call | solution.py:436
  (65 shorter events, 0.2 us)
Async XLA Ops:
  0.6 52.8 %copy-start = (bf16[2,128,1024]{2,1,0:T(8,128)(2,1)S(1)}, bf16[2,128,1024]{2,1,0:T(8,128)(2,1)}, u32[]{:S(2)}) copy-start(bf16[2,128,1024]{2,1,0:T(8,128)(2,1)} %param.10) | copy-start | bytes 1572868
  1.7 10.1 %collective-permute-start.14 = (bf16[32,1024]{1,0:T(8,128)(2,1)S(1)}, bf16[32,1024]{1,0:T(8,128)(2,1)S(1)}, u32[]{:S(2)}, u32[]{:S(2)}) collective-permute-start(bf16[32,1024]{1,0:T(8,128)(2,1)S(1)} %bitcast.20), channel_id=1, source_target_pairs={{0,1},{1,0},{2,3},{3,2},{4,5},{5,4},{6,7},{7,6},{8,9},{9,8},{10,11... | collective-permute-start | bytes 196616 | tf_op jit(solution)/shard_map/ppermute | solution.py:460
  4.7 8.7 %collective-permute-start.15 = (bf16[32,1024]{1,0:T(8,128)(2,1)S(1)}, bf16[32,1024]{1,0:T(8,128)(2,1)S(1)}, u32[]{:S(2)}, u32[]{:S(2)}) collective-permute-start(bf16[32,1024]{1,0:T(8,128)(2,1)S(1)} %bitcast.19), channel_id=1, source_target_pairs={{0,2},{1,3},{2,0},{3,1},{4,6},{5,7},{6,4},{7,5},{8,10},{9,11},{10,... | collective-permute-start | bytes 196616 | tf_op jit(solution)/shard_map/ppermute | solution.py:460
  6.2 7.1 %collective-permute-start.16 = (bf16[32,1024]{1,0:T(8,128)(2,1)S(1)}, bf16[32,1024]{1,0:T(8,128)(2,1)S(1)}, u32[]{:S(2)}, u32[]{:S(2)}) collective-permute-start(bf16[32,1024]{1,0:T(8,128)(2,1)S(1)} %bitcast.18), channel_id=1, source_target_pairs={{0,3},{1,2},{2,1},{3,0},{4,7},{5,6},{6,5},{7,4},{8,11},{9,10},{10,... | collective-permute-start | bytes 196616 | tf_op jit(solution)/shard_map/ppermute | solution.py:460
  8.3 24.8 %collective-permute-start.25 = (bf16[528,256]{1,0:T(8,128)(2,1)S(1)}, bf16[528,256]{1,0:T(8,128)(2,1)S(1)}, u32[]{:S(2)}, u32[]{:S(2)}) collective-permute-start(bf16[528,256]{1,0:T(8,128)(2,1)S(1)} %get-tuple-element.36), channel_id=1, source_target_pairs={{0,1},{1,0},{2,3},{3,2},{4,5},{5,4},{6,7},{7,6},{8,9},{9,8},{10,11... | collective-permute-start | bytes 811016 | tf_op jit(solution)/shard_map/ppermute | solution.py:460
  10.3 25.4 %collective-permute-start.26 = (bf16[528,256]{1,0:T(8,128)(2,1)S(1)}, bf16[528,256]{1,0:T(8,128)(2,1)S(1)}, u32[]{:S(2)}, u32[]{:S(2)}) collective-permute-start(bf16[528,256]{1,0:T(8,128)(2,1)S(1)} %get-tuple-element.37), channel_id=1, source_target_pairs={{0,2},{1,3},{2,0},{3,1},{4,6},{5,7},{6,4},{7,5},{8,10},{9,11},{10,... | collective-permute-start | bytes 811016 | tf_op jit(solution)/shard_map/ppermute | solution.py:460
  11.8 4.8 %collective-permute-start = (bf16[32,1024]{1,0:T(8,128)(2,1)}, bf16[32,1024]{1,0:T(8,128)(2,1)S(1)}, u32[]{:S(2)}, u32[]{:S(2)}) collective-permute-start(bf16[32,1024]{1,0:T(8,128)(2,1)} %param.16), channel_id=1, source_target_pairs={{0,8},{4,12},{8,0},{12,4},{16,24},{20,28},{24,16},{28,20},{1,9},{5... | collective-permute-start | bytes 196616 | tf_op jit(solution)/shard_map/ppermute | solution.py:476
  13.4 57.7 %copy-start.12 = (bf16[128,1024]{1,0:T(8,128)(2,1)}, bf16[128,1024]{1,0:T(8,128)(2,1)S(1)}, u32[]{:S(2)}) copy-start(bf16[128,1024]{1,0:T(8,128)(2,1)S(1)} %pad_maximum_fusion.rest_8_) | copy-start | bytes 786436
  13.4 23.0 %collective-permute-start.20 = (bf16[128,1024]{1,0:T(8,128)(2,1)S(1)}, bf16[128,1024]{1,0:T(8,128)(2,1)S(1)}, u32[]{:S(2)}, u32[]{:S(2)}) collective-permute-start(bf16[128,1024]{1,0:T(8,128)(2,1)S(1)} %pad_maximum_fusion.rest_8_), channel_id=1, source_target_pairs={{0,16},{4,20},{8,24},{12,28},{16,0},{20,4},{24,8},{28,12},{1,17},{... | collective-permute-start | bytes 786440 | tf_op jit(solution)/shard_map/ppermute | solution.py:476
  16.1 15.2 %collective-permute-start.1 = (bf16[32,1024]{1,0:T(8,128)(2,1)}, bf16[32,1024]{1,0:T(8,128)(2,1)S(1)}, u32[]{:S(2)}, u32[]{:S(2)}) collective-permute-start(bf16[32,1024]{1,0:T(8,128)(2,1)} %param.16), channel_id=1, source_target_pairs={{0,16},{4,20},{8,24},{12,28},{16,0},{20,4},{24,8},{28,12},{1,17},{... | collective-permute-start | bytes 196616 | tf_op jit(solution)/shard_map/ppermute | solution.py:476
  16.6 15.2 %collective-permute-start.2 = (bf16[32,1024]{1,0:T(8,128)(2,1)}, bf16[32,1024]{1,0:T(8,128)(2,1)S(1)}, u32[]{:S(2)}, u32[]{:S(2)}) collective-permute-start(bf16[32,1024]{1,0:T(8,128)(2,1)} %param.16), channel_id=1, source_target_pairs={{0,24},{4,28},{8,16},{12,20},{16,8},{20,12},{24,0},{28,4},{1,25},{... | collective-permute-start | bytes 196616 | tf_op jit(solution)/shard_map/ppermute | solution.py:476
  31.3 18.5 %collective-permute-start.10 = (bf16[256,1024]{1,0:T(8,128)(2,1)}, bf16[256,1024]{1,0:T(8,128)(2,1)S(1)}, u32[]{:S(2)}, u32[]{:S(2)}) collective-permute-start(bf16[256,1024]{1,0:T(8,128)(2,1)} %bitcast.11), channel_id=1, source_target_pairs={{0,1},{1,0},{2,3},{3,2},{4,5},{5,4},{6,7},{7,6},{8,9},{9,8},{10,11... | collective-permute-start | bytes 1572872 | tf_op jit(solution)/shard_map/ppermute | solution.py:460
  31.8 18.6 %collective-permute-start.11 = (bf16[256,1024]{1,0:T(8,128)(2,1)}, bf16[256,1024]{1,0:T(8,128)(2,1)S(1)}, u32[]{:S(2)}, u32[]{:S(2)}) collective-permute-start(bf16[256,1024]{1,0:T(8,128)(2,1)} %bitcast.12), channel_id=1, source_target_pairs={{0,2},{1,3},{2,0},{3,1},{4,6},{5,7},{6,4},{7,5},{8,10},{9,11},{10,... | collective-permute-start | bytes 1572872 | tf_op jit(solution)/shard_map/ppermute | solution.py:460
  33.2 17.2 %copy-start.14 = (bf16[528,256]{1,0:T(8,128)(2,1)}, bf16[528,256]{1,0:T(8,128)(2,1)S(1)}, u32[]{:S(2)}) copy-start(bf16[528,256]{1,0:T(8,128)(2,1)S(1)} %collective-permute-done.25.rest_17_) | copy-start | bytes 811012
  33.2 16.5 %collective-permute-start.27 = (bf16[528,256]{1,0:T(8,128)(2,1)S(1)}, bf16[528,256]{1,0:T(8,128)(2,1)S(1)}, u32[]{:S(2)}, u32[]{:S(2)}) collective-permute-start(bf16[528,256]{1,0:T(8,128)(2,1)S(1)} %get-tuple-element.38), channel_id=1, source_target_pairs={{0,3},{1,2},{2,1},{3,0},{4,7},{5,6},{6,5},{7,4},{8,11},{9,10},{10,... | collective-permute-start | bytes 811016 | tf_op jit(solution)/shard_map/ppermute | solution.py:460
  35.7 16.2 %copy-start.15 = (bf16[528,256]{1,0:T(8,128)(2,1)}, bf16[528,256]{1,0:T(8,128)(2,1)S(1)}, u32[]{:S(2)}) copy-start(bf16[528,256]{1,0:T(8,128)(2,1)S(1)} %collective-permute-done.26.rest_18_) | copy-start | bytes 811012
  35.7 14.0 %collective-permute-start.23 = (bf16[128,1024]{1,0:T(8,128)(2,1)S(1)}, bf16[128,1024]{1,0:T(8,128)(2,1)S(1)}, u32[]{:S(2)}, u32[]{:S(2)}) collective-permute-start(bf16[128,1024]{1,0:T(8,128)(2,1)S(1)} %pad_maximum_fusion.rest_8_), channel_id=1, source_target_pairs={{8,16},{16,8},{12,20},{20,12},{9,17},{17,9},{13,21},{21,13},{10,18... | collective-permute-start | bytes 786440 | tf_op jit(solution)/shard_map/ppermute | solution.py:487
  36.4 17.0 %copy-start.17 = (bf16[128,1024]{1,0:T(8,128)(2,1)}, bf16[128,1024]{1,0:T(8,128)(2,1)S(1)}, u32[]{:S(2)}) copy-start(bf16[128,1024]{1,0:T(8,128)(2,1)S(1)} %collective-permute-done.20.rest_12_) | copy-start | bytes 786436
  36.4 15.5 %collective-permute-start.22 = (bf16[128,1024]{1,0:T(8,128)(2,1)S(1)}, bf16[128,1024]{1,0:T(8,128)(2,1)S(1)}, u32[]{:S(2)}, u32[]{:S(2)}) collective-permute-start(bf16[128,1024]{1,0:T(8,128)(2,1)S(1)} %collective-permute-done.20.rest_12_), channel_id=1, source_target_pairs={{8,0},{16,24},{12,4},{20,28},{9,1},{17,25},{13,5},{21,29},{10,2},{... | collective-permute-start | bytes 786440 | tf_op jit(solution)/shard_map/ppermute | solution.py:489
  37.7 41.1 %copy-start.4 = (bf16[128,1024]{1,0:T(8,128)(2,1)}, bf16[128,1024]{1,0:T(8,128)(2,1)S(1)}, u32[]{:S(2)}) copy-start(bf16[128,1024]{1,0:T(8,128)(2,1)S(1)} %constant_dynamic-update-slice_fusion.refs_0_) | copy-start | bytes 786436
  49.7 3.7 %copy-start.16 = (bf16[528,256]{1,0:T(8,128)(2,1)}, bf16[528,256]{1,0:T(8,128)(2,1)S(1)}, u32[]{:S(2)}) copy-start(bf16[528,256]{1,0:T(8,128)(2,1)S(1)} %collective-permute-done.27.rest_19_) | copy-start | bytes 811012
  49.7 6.5 %collective-permute-start.18 = (bf16[128,1024]{1,0:T(8,128)(2,1)S(1)}, bf16[128,1024]{1,0:T(8,128)(2,1)}, u32[]{:S(2)}, u32[]{:S(2)}) collective-permute-start(bf16[128,1024]{1,0:T(8,128)(2,1)S(1)} %pad_maximum_fusion.rest_8_), channel_id=1, source_target_pairs={{0,8},{4,12},{8,0},{12,4},{16,24},{20,28},{24,16},{28,20},{1,9},{5... | collective-permute-start | bytes 786440 | tf_op jit(solution)/shard_map/ppermute | solution.py:476
  49.7 6.5 %collective-permute-start.17 = (bf16[128,1024]{1,0:T(8,128)(2,1)S(1)}, bf16[128,1024]{1,0:T(8,128)(2,1)}, u32[]{:S(2)}, u32[]{:S(2)}) collective-permute-start(bf16[128,1024]{1,0:T(8,128)(2,1)S(1)} %pad_maximum_fusion.rest_8_), channel_id=1, source_target_pairs={{0,4},{4,0},{8,12},{12,8},{16,20},{20,16},{24,28},{28,24},{1,5},{5... | collective-permute-start | bytes 786440 | tf_op jit(solution)/shard_map/ppermute | solution.py:479
  49.8 9.2 %collective-permute-start.4 = (bf16[128,1024]{1,0:T(8,128)(2,1)S(1)}, bf16[128,1024]{1,0:T(8,128)(2,1)S(1)}, u32[]{:S(2)}, u32[]{:S(2)}) collective-permute-start(bf16[128,1024]{1,0:T(8,128)(2,1)S(1)} %constant_dynamic-update-slice_fusion.refs_0_), channel_id=1, source_target_pairs={{0,1},{1,0},{2,3},{3,2},{4,5},{5,4},{6,7},{7,6},{8,9},{9,8},{10,11... | collective-permute-start | bytes 786440 | tf_op jit(solution)/shard_map/ppermute | solution.py:460
  50.4 12.7 %collective-permute-start.6 = (bf16[128,1024]{1,0:T(8,128)(2,1)S(1)}, bf16[128,1024]{1,0:T(8,128)(2,1)S(1)}, u32[]{:S(2)}, u32[]{:S(2)}) collective-permute-start(bf16[128,1024]{1,0:T(8,128)(2,1)S(1)} %constant_dynamic-update-slice_fusion.refs_0_), channel_id=1, source_target_pairs={{0,2},{1,3},{2,0},{3,1},{4,6},{5,7},{6,4},{7,5},{8,10},{9,11},{10,... | collective-permute-start | bytes 786440 | tf_op jit(solution)/shard_map/ppermute | solution.py:460
  51.9 14.1 %collective-permute-start.8 = (bf16[128,1024]{1,0:T(8,128)(2,1)S(1)}, bf16[128,1024]{1,0:T(8,128)(2,1)S(1)}, u32[]{:S(2)}, u32[]{:S(2)}) collective-permute-start(bf16[128,1024]{1,0:T(8,128)(2,1)S(1)} %constant_dynamic-update-slice_fusion.refs_0_), channel_id=1, source_target_pairs={{0,3},{1,2},{2,1},{3,0},{4,7},{5,6},{6,5},{7,4},{8,11},{9,10},{10,... | collective-permute-start | bytes 786440 | tf_op jit(solution)/shard_map/ppermute | solution.py:460
  53.4 2.8 %copy-start.18 = (bf16[128,1024]{1,0:T(8,128)(2,1)S(1)}, bf16[128,1024]{1,0:T(8,128)(2,1)}, u32[]{:S(2)}) copy-start(bf16[128,1024]{1,0:T(8,128)(2,1)} %copy-done.17) | copy-start | bytes 786436
  56.0 15.1 %copy-start.13 = (bf16[128,1024]{1,0:T(8,128)(2,1)}, bf16[128,1024]{1,0:T(8,128)(2,1)S(1)}, u32[]{:S(2)}) copy-start(bf16[128,1024]{1,0:T(8,128)(2,1)S(1)} %broadcast_select_fusion.rest_14_) | copy-start | bytes 786436
  56.2 9.9 %collective-permute-start.21 = (bf16[128,1024]{1,0:T(8,128)(2,1)S(1)}, bf16[128,1024]{1,0:T(8,128)(2,1)S(1)}, u32[]{:S(2)}, u32[]{:S(2)}) collective-permute-start(bf16[128,1024]{1,0:T(8,128)(2,1)S(1)} %copy-done.18), channel_id=1, source_target_pairs={{0,4},{4,0},{8,12},{12,8},{16,20},{20,16},{24,28},{28,24},{1,5},{5... | collective-permute-start | bytes 786440 | tf_op jit(solution)/shard_map/ppermute | solution.py:479
  56.2 10.4 %collective-permute-start.19 = (bf16[128,1024]{1,0:T(8,128)(2,1)}, bf16[128,1024]{1,0:T(8,128)(2,1)S(1)}, u32[]{:S(2)}, u32[]{:S(2)}) collective-permute-start(bf16[128,1024]{1,0:T(8,128)(2,1)} %collective-permute-done.18.rest_10_), channel_id=1, source_target_pairs={{0,4},{4,0},{8,12},{12,8},{16,20},{20,16},{24,28},{28,24},{1,5},{5... | collective-permute-start | bytes 786440 | tf_op jit(solution)/shard_map/ppermute | solution.py:479
  59.0 19.8 %copy-start.5 = (bf16[128,1024]{1,0:T(8,128)(2,1)}, bf16[128,1024]{1,0:T(8,128)(2,1)S(1)}, u32[]{:S(2)}) copy-start(bf16[128,1024]{1,0:T(8,128)(2,1)S(1)} %collective-permute-done.4.refs_2_) | copy-start | bytes 786436
  59.0 11.5 %collective-permute-start.12 = (bf16[128,1024]{1,0:T(8,128)(2,1)}, bf16[128,1024]{1,0:T(8,128)(2,1)S(1)}, u32[]{:S(2)}, u32[]{:S(2)}) collective-permute-start(bf16[128,1024]{1,0:T(8,128)(2,1)} %get-tuple-element.27.rest_2_), channel_id=1, source_target_pairs={{0,2},{1,3},{2,0},{3,1},{4,6},{5,7},{6,4},{7,5},{8,10},{9,11},{10,... | collective-permute-start | bytes 786440 | tf_op jit(solution)/shard_map/ppermute | solution.py:472
  63.1 15.8 %copy-start.6 = (bf16[128,1024]{1,0:T(8,128)(2,1)}, bf16[128,1024]{1,0:T(8,128)(2,1)S(1)}, u32[]{:S(2)}) copy-start(bf16[128,1024]{1,0:T(8,128)(2,1)S(1)} %collective-permute-done.6.refs_4_) | copy-start | bytes 786436
  63.1 7.5 %collective-permute-start.13 = (bf16[128,1024]{1,0:T(8,128)(2,1)}, bf16[128,1024]{1,0:T(8,128)(2,1)S(1)}, u32[]{:S(2)}, u32[]{:S(2)}) collective-permute-start(bf16[128,1024]{1,0:T(8,128)(2,1)} %get-tuple-element.30.rest_5_), channel_id=1, source_target_pairs={{0,1},{1,0},{2,3},{3,2},{4,5},{5,4},{6,7},{7,6},{8,9},{9,8},{10,11... | collective-permute-start | bytes 786440 | tf_op jit(solution)/shard_map/ppermute | solution.py:472
  66.0 12.8 %copy-start.7 = (bf16[128,1024]{1,0:T(8,128)(2,1)}, bf16[128,1024]{1,0:T(8,128)(2,1)S(1)}, u32[]{:S(2)}) copy-start(bf16[128,1024]{1,0:T(8,128)(2,1)S(1)} %collective-permute-done.8.refs_6_) | copy-start | bytes 786436
  66.0 5.1 %collective-permute-start.24 = (bf16[128,1024]{1,0:T(8,128)(2,1)S(1)}, bf16[128,1024]{1,0:T(8,128)(2,1)S(1)}, u32[]{:S(2)}, u32[]{:S(2)}) collective-permute-start(bf16[128,1024]{1,0:T(8,128)(2,1)S(1)} %broadcast_select_fusion.rest_14_), channel_id=1, source_target_pairs={{0,4},{4,0},{8,12},{12,8},{16,20},{20,16},{24,28},{28,24},{1,5},{5... | collective-permute-start | bytes 786440 | tf_op jit(solution)/shard_map/ppermute | solution.py:479
  66.1 5.1 %copy-start.19 = (bf16[128,1024]{1,0:T(8,128)(2,1)}, bf16[128,1024]{1,0:T(8,128)(2,1)S(1)}, u32[]{:S(2)}) copy-start(bf16[128,1024]{1,0:T(8,128)(2,1)S(1)} %collective-permute-done.21.rest_13_) | copy-start | bytes 786436
  66.1 27.9 %collective-permute-start.3 = (bf16[128,1024]{1,0:T(8,128)(2,1)S(1)}, bf16[128,1024]{1,0:T(8,128)(2,1)S(1)}, u32[]{:S(2)}, u32[]{:S(2)}) collective-permute-start(bf16[128,1024]{1,0:T(8,128)(2,1)S(1)} %constant_dynamic-update-slice_fusion.refs_0_), channel_id=1, source_target_pairs={{0,4},{4,0},{8,12},{12,8},{16,20},{20,16},{24,28},{28,24},{1,5},{5... | collective-permute-start | bytes 786440 | tf_op jit(solution)/shard_map/ppermute | solution.py:479
  66.6 4.6 %copy-start.20 = (bf16[128,1024]{1,0:T(8,128)(2,1)}, bf16[128,1024]{1,0:T(8,128)(2,1)S(1)}, u32[]{:S(2)}) copy-start(bf16[128,1024]{1,0:T(8,128)(2,1)S(1)} %collective-permute-done.19.rest_11_) | copy-start | bytes 786436
  66.6 29.5 %collective-permute-start.5 = (bf16[128,1024]{1,0:T(8,128)(2,1)S(1)}, bf16[128,1024]{1,0:T(8,128)(2,1)S(1)}, u32[]{:S(2)}, u32[]{:S(2)}) collective-permute-start(bf16[128,1024]{1,0:T(8,128)(2,1)S(1)} %collective-permute-done.4.refs_2_), channel_id=1, source_target_pairs={{0,4},{4,0},{8,12},{12,8},{16,20},{20,16},{24,28},{28,24},{1,5},{5... | collective-permute-start | bytes 786440 | tf_op jit(solution)/shard_map/ppermute | solution.py:479
  70.6 0.7 copy-start.21
  70.6 25.5 %collective-permute-start.7 = (bf16[128,1024]{1,0:T(8,128)(2,1)S(1)}, bf16[128,1024]{1,0:T(8,128)(2,1)S(1)}, u32[]{:S(2)}, u32[]{:S(2)}) collective-permute-start(bf16[128,1024]{1,0:T(8,128)(2,1)S(1)} %collective-permute-done.6.refs_4_), channel_id=1, source_target_pairs={{0,4},{4,0},{8,12},{12,8},{16,20},{20,16},{24,28},{28,24},{1,5},{5... | collective-permute-start | bytes 786440 | tf_op jit(solution)/shard_map/ppermute | solution.py:479
  70.6 0.8 copy-start.22
  70.6 25.5 %collective-permute-start.9 = (bf16[128,1024]{1,0:T(8,128)(2,1)S(1)}, bf16[128,1024]{1,0:T(8,128)(2,1)S(1)}, u32[]{:S(2)}, u32[]{:S(2)}) collective-permute-start(bf16[128,1024]{1,0:T(8,128)(2,1)S(1)} %collective-permute-done.8.refs_6_), channel_id=1, source_target_pairs={{0,4},{4,0},{8,12},{12,8},{16,20},{20,16},{24,28},{28,24},{1,5},{5... | collective-permute-start | bytes 786440 | tf_op jit(solution)/shard_map/ppermute | solution.py:479
  71.1 0.7 copy-start.23
  71.8 20.0 %copy-start.1 = (f32[1024]{0:T(1024)S(1)}, f32[1024]{0:T(1024)}, u32[]{:S(2)}) copy-start(f32[1024]{0:T(1024)} %param.18) | copy-start | bytes 12292
  78.9 4.0 %collective-permute-start.28 = (f32[8,8,128]{2,1,0:T(8,128)S(1)}, f32[8,8,128]{2,1,0:T(8,128)S(1)}, u32[]{:S(2)}, u32[]{:S(2)}) collective-permute-start(f32[8,8,128]{2,1,0:T(8,128)S(1)} %get-tuple-element.41.rest_0_), channel_id=1, source_target_pairs={{0,1},{1,0},{2,3},{3,2},{4,5},{5,4},{6,7},{7,6},{8,9},{9,8},{10,11... | collective-permute-start | bytes 98312 | tf_op jit(solution)/shard_map/ppermute | solution.py:460
  82.9 3.9 %collective-permute-start.29 = (f32[8,8,128]{2,1,0:T(8,128)S(1)}, f32[8,8,128]{2,1,0:T(8,128)S(1)}, u32[]{:S(2)}, u32[]{:S(2)}) collective-permute-start(f32[8,8,128]{2,1,0:T(8,128)S(1)} %get-tuple-element.41.rest_0_), channel_id=1, source_target_pairs={{0,2},{1,3},{2,0},{3,1},{4,6},{5,7},{6,4},{7,5},{8,10},{9,11},{10,... | collective-permute-start | bytes 98312 | tf_op jit(solution)/shard_map/ppermute | solution.py:460
  86.8 5.1 %collective-permute-start.30 = (f32[8,8,128]{2,1,0:T(8,128)S(1)}, f32[8,8,128]{2,1,0:T(8,128)S(1)}, u32[]{:S(2)}, u32[]{:S(2)}) collective-permute-start(f32[8,8,128]{2,1,0:T(8,128)S(1)} %get-tuple-element.41.rest_0_), channel_id=1, source_target_pairs={{0,3},{1,2},{2,1},{3,0},{4,7},{5,6},{6,5},{7,4},{8,11},{9,10},{10,... | collective-permute-start | bytes 98312 | tf_op jit(solution)/shard_map/ppermute | solution.py:460
  92.5 6.9 %collective-permute-start.31 = (bf16[256,256]{1,0:T(8,128)(2,1)S(1)}, bf16[256,256]{1,0:T(8,128)(2,1)S(1)}, u32[]{:S(2)}, u32[]{:S(2)}) collective-permute-start(bf16[256,256]{1,0:T(8,128)(2,1)S(1)} %get-tuple-element.43), channel_id=1, source_target_pairs={{0,1},{1,0},{2,3},{3,2},{4,5},{5,4},{6,7},{7,6},{8,9},{9,8},{10,11... | collective-permute-start | bytes 393224 | tf_op jit(solution)/shard_map/ppermute | solution.py:460
  94.0 2.2 %copy-start.8 = (bf16[128,1024]{1,0:T(8,128)(2,1)}, bf16[128,1024]{1,0:T(8,128)(2,1)S(1)}, u32[]{:S(2)}) copy-start(bf16[128,1024]{1,0:T(8,128)(2,1)S(1)} %collective-permute-done.3.refs_1_) | copy-start | bytes 786436
  94.0 5.9 %collective-permute-start.32 = (bf16[256,256]{1,0:T(8,128)(2,1)S(1)}, bf16[256,256]{1,0:T(8,128)(2,1)S(1)}, u32[]{:S(2)}, u32[]{:S(2)}) collective-permute-start(bf16[256,256]{1,0:T(8,128)(2,1)S(1)} %get-tuple-element.44), channel_id=1, source_target_pairs={{0,2},{1,3},{2,0},{3,1},{4,6},{5,7},{6,4},{7,5},{8,10},{9,11},{10,... | collective-permute-start | bytes 393224 | tf_op jit(solution)/shard_map/ppermute | solution.py:460
  96.0 0.7 copy-start.9
  96.0 5.9 %copy-start.2 = (f32[1024]{0:T(1024)S(1)}, f32[1024]{0:T(1024)}, u32[]{:S(2)}) copy-start(f32[1024]{0:T(1024)} %param.19) | copy-start | bytes 12292
  96.0 5.9 %copy-start.3 = (s32[2]{0:T(128)S(1)}, s32[2]{0:T(128)}, u32[]{:S(2)}) copy-start(s32[2]{0:T(128)} %live_ref.1) | copy-start | bytes 28
  96.1 5.9 %collective-permute-start.33 = (bf16[256,256]{1,0:T(8,128)(2,1)S(1)}, bf16[256,256]{1,0:T(8,128)(2,1)S(1)}, u32[]{:S(2)}, u32[]{:S(2)}) collective-permute-start(bf16[256,256]{1,0:T(8,128)(2,1)S(1)} %get-tuple-element.45), channel_id=1, source_target_pairs={{0,3},{1,2},{2,1},{3,0},{4,7},{5,6},{6,5},{7,4},{8,11},{9,10},{10,... | collective-permute-start | bytes 393224 | tf_op jit(solution)/shard_map/ppermute | solution.py:460
  96.1 0.7 copy-start.10
  96.9 0.7 copy-start.11

commit v3 on v2

--- a/solution.py
+++ b/solution.py
@@ -181,6 +181,17 @@
         [],
         [VMEM] * helpers,
     )(*in_hbm([users, keys, values]))
+
+
+def stack(pieces):
+    rows, width = pieces[0].shape
+
+    def body(*refs):
+        for at, ref in enumerate(refs[:-1]):
+            refs[-1][pl.ds(at * rows, rows)] = ref[...]
+
+    shape = jax.ShapeDtypeStruct((len(pieces) * rows, width), pieces[0].dtype)
+    return kernel_call(body, shape, [VMEM] * len(pieces), [])(*pieces)
 
 
 def normalise(values, gain):
@@ -279,14 +290,15 @@
             for rel in range(helpers)
             for block in range(blocks)
         ]
-        for copy in w_copies + c_copies:
+        late = [at for at, (rel, _, _) in enumerate(cands) if rel]
+        for copy in w_copies + [c_copies[at] for at in range(n_cands) if at not in late]:
             copy.wait()
         lane = lax.broadcasted_iota(jnp.int32, (rows_block, 128), 1)
         for rel in range(helpers):
             proj[...] = silu(jnp.dot(normed[rel], weight[...], preferred_element_type=jnp.float32))
             gate_ref[pl.ds(rel * count, count)] = proj[:, :feats]
             if rel == 0:
-                for copy in p_copies:
+                for copy in p_copies + [c_copies[at] for at in late]:
                     copy.wait()
             for block in range(blocks):
                 user = pl.multiple_of(owners[rel * blocks + block] * prefix, prefix)
@@ -315,7 +327,7 @@
                 average = total * (1.0 / feats)
                 off = sum(jnp.sum((piece - average) ** 2, axis=-1, keepdims=True) for piece in out)
                 both = jnp.where(lane == 0, average, jnp.where(lane == 1, off, 0.0))
-                stats_ref[rel * blocks + block] = both.T[:8]
+                stats_ref[pl.ds(2 * (rel * blocks + block), 2)] = both.T[:2]
                 for head in range(heads):
                     mixed_ref[
                         pl.ds(rel * count + block * rows_block, rows_block), pl.ds(head * head_dim, head_dim)
@@ -325,7 +337,7 @@
     shapes = [
         jax.ShapeDtypeStruct((total_rows, feats), jnp.float32),
         jax.ShapeDtypeStruct((total_rows, feats), jnp.float32),
-        jax.ShapeDtypeStruct((helpers * blocks, 8, rows_block), jnp.float32),
+        jax.ShapeDtypeStruct((2 * helpers * blocks, rows_block), jnp.float32),
     ]
     n_pieces = n_weights * helpers
     scratch = [
@@ -340,7 +352,8 @@
         pltpu.SemaphoreType.DMA((2 * helpers,)),
         pltpu.SemaphoreType.DMA((helpers,)),
     ]
-    arrays = in_hbm([array for _, _, array in cands] + list(weights) + list(prefixes))
+    arrays = in_hbm([array for _, _, array in cands] + list(weights)[:-CORES])
+    arrays += list(weights)[-CORES:] + in_hbm(prefixes)
     return kernel_call(body, shapes, [ANY] * len(arrays), scratch, flops=2 * total_rows * features * width)(*arrays)
 
 
@@ -356,7 +369,9 @@
         my_gain = gain_ref[:, pl.ds(pl.multiple_of(mine * feats, feats), feats)]
         for rel in range(helpers):
             for block in range(blocks):
-                parts = [stats_refs[peer][(rel ^ peer) * blocks + block] for peer in range(helpers)]
+                parts = [
+                    stats_refs[peer][pl.ds(2 * ((rel ^ peer) * blocks + block), 2)] for peer in range(helpers)
+                ]
                 average = sum(part[0:1] for part in parts) * (1.0 / helpers)
                 off = sum(
                     part[1:2] + feats * (part[0:1] - average) ** 2 for part in parts
@@ -463,7 +478,8 @@
 
     def everyone(rows_here, gain):
         near = to_peers([rows_here] * (3 if helpers == 4 else helpers))
-        normed = norm_rows(near, gain, 2)
+        normed = list(norm_rows(near[:1], gain, 2))
+        normed += norm_rows(near[1:], gain, 2)
         half = rows_here.shape[0] // 2
         out = [(at // 2, at % 2 * half, part) for at, part in enumerate(normed)]
         if helpers == 4:
@@ -501,7 +517,8 @@
     proj_shards = with_swaps(to_planes(w_shard))
     cands = everyone(cand_rows, gain)
     prefixes = to_peers(prefix_pieces)
-    o_shard = jnp.concatenate([w_out] + [to_plane(w_out, turn) for turn in range(1, planes)], axis=0)
+    o_parts = [w_out] + [to_plane(w_out, turn) for turn in range(1, planes)]
+    o_shard = stack(o_parts)
     out_shards = with_swaps(to_peers([o_shard] * helpers))
 
     mixed, gates, stats = attend(

time: 105 us -> 94.7 us (0.902)
  starting transfers between devices: 42 us -> 36 us
  waiting for transfers between devices: 40.7 us -> 35.9 us
    ppermute x5, waiting for transfers between devices: 11.1 us -> 6.28 us  [to_plane(): lax.ppermute(array, 'group', [(at, at ^ CORES * turn) for at in range(gro...]
    ppermute x2, starting transfers between devices: 4.36 us -> 1.96 us  [everyone(): out.append((3, at * half, lax.ppermute(part, 'helper', pairs)))]
    ppermute x17, starting transfers between devices: 25.6 us -> 23.9 us  [to_peers(): lax.ppermute(pieces[rel], 'helper', [(at, at ^ rel) for at in range(helpe...]
    pallas_call x1 -> x2, Pallas kernels: 2.63 us -> 4.01 us  [norm_rows(): kernel_call(body, shapes, [VMEM] * (1 + len(arrays)), [], specs)]
    ppermute x5, starting transfers between devices: 8.47 us -> 7.1 us  [to_plane(): lax.ppermute(array, 'group', [(at, at ^ CORES * turn) for at in range(gro...]
    unnamed x51 -> x42, local copies, waits for them, and re-layouts: 3.01 us -> 3.08 us
  transfers between devices with their start and end apart: 34 -> 34, of which waited for: 12 -> 14; matrix products, arithmetic and copies ran while one was open for 1% -> 0% of each run, Pallas kernels for 14% -> 15%
where the time goes in v3:
time: 94.7 us; the launch traced here: 94.2 us
  starting transfers between devices  36 us (38%)
  waiting for transfers between devices  35.9 us (38%)
  Pallas kernels  18.3 us (19%)
  local copies, waits for them, and re-layouts  3.08 us (3%)
    ppermute x17, waiting for transfers between devices, to_peers(): lax.ppermute(pieces[rel], 'helper', [(at, at ^ rel) for at in range(helpe...  26.1 us
    ppermute x17, starting transfers between devices, to_peers(): lax.ppermute(pieces[rel], 'helper', [(at, at ^ rel) for at in range(helpe...  23.9 us
    ppermute x5, starting transfers between devices, to_plane(): lax.ppermute(array, 'group', [(at, at ^ CORES * turn) for at in range(gro...  7.1 us
    pallas_call x1, Pallas kernels, attend(): kernel_call(body, shapes, [ANY] * len(arrays), scratch, flops=2 * total_r...  6.5 us
    ppermute x5, waiting for transfers between devices, to_plane(): lax.ppermute(array, 'group', [(at, at ^ CORES * turn) for at in range(gro...  6.28 us
    pallas_call x2, Pallas kernels, norm_rows(): kernel_call(body, shapes, [VMEM] * (1 + len(arrays)), [], specs)  4.01 us
    ppermute x2, waiting for transfers between devices, everyone(): out.append((3, at * half, lax.ppermute(part, 'helper', pairs)))  3.52 us
    unnamed x42, local copies, waits for them, and re-layouts  3.08 us
  transfers between devices with their start and end apart: 34, of which 14 were waited for; matrix products, arithmetic and copies ran while one was open for 0% of the time, Pallas kernels for 15%

profile of v3, /device:TPU:0, one launch (start us, length us, event | category | flops | bytes accessed | tf_op | source)
XLA Modules:
  0.0 94.2 jit_solution(13264172396043112208)
XLA Ops:
  0.6 0.0 copy-start
  0.6 2.1 %shard_map.118 = (bf16[528,256]{1,0:T(8,128)(2,1)}, bf16[528,256]{1,0:T(8,128)(2,1)S(1)}, bf16[528,256]{1,0:T(8,128)(2,1)S(1)}, bf16[528,256]{1,0:T(8,128)(2,1)S(1)}) custom-call(s32[2]{0:T(128)} %users_ref.1, bf16[256,1024]{1,0:T(8,128)(2,1)} %bitcast.21, bf16[256,1024]{1,0:T(8,128)(2,1)} %bitcast.22), custom_call_target="tpu_custom_call" | custom-call | bytes 1 | tf_op jit(solution)/shard_map/pallas_call | solution.py:177
  2.8 3.0 %collective-permute-start.25 = (bf16[528,256]{1,0:T(8,128)(2,1)S(1)}, bf16[528,256]{1,0:T(8,128)(2,1)S(1)}, u32[]{:S(2)}, u32[]{:S(2)}) collective-permute-start(bf16[528,256]{1,0:T(8,128)(2,1)S(1)} %get-tuple-element.36), channel_id=1, source_target_pairs={{0,1},{1,0},{2,3},{3,2},{4,5},{5,4},{6,7},{7,6},{8,9},{9,8},{10,11... | collective-permute-start | bytes 811016 | tf_op jit(solution)/shard_map/ppermute | solution.py:475
  5.7 1.5 %collective-permute-start.26 = (bf16[528,256]{1,0:T(8,128)(2,1)S(1)}, bf16[528,256]{1,0:T(8,128)(2,1)S(1)}, u32[]{:S(2)}, u32[]{:S(2)}) collective-permute-start(bf16[528,256]{1,0:T(8,128)(2,1)S(1)} %get-tuple-element.37), channel_id=1, source_target_pairs={{0,2},{1,3},{2,0},{3,1},{4,6},{5,7},{6,4},{7,5},{8,10},{9,11},{10,... | collective-permute-start | bytes 811016 | tf_op jit(solution)/shard_map/ppermute | solution.py:475
  7.2 1.0 %shard_map.117 = (bf16[1,32,1024]{2,1,0:T(8,128)(2,1)S(1)}, bf16[1,32,1024]{2,1,0:T(8,128)(2,1)S(1)}, bf16[1,32,1024]{2,1,0:T(8,128)(2,1)S(1)}, bf16[1,32,1024]{2,1,0:T(8,128)(2,1)S(1)}) custom-call(bf16[32,4096]{1,0:T(8,128)(2,1)} %refs_0_.3), custom_call_target="tpu_custom_call" | custom-call | bytes 1 | tf_op jit(solution)/shard_map/pallas_call | solution.py:151
  8.2 0.6 collective-permute-start.14
  8.8 0.1 collective-permute-start.15
  8.9 2.9 %collective-permute-start.16 = (bf16[32,1024]{1,0:T(8,128)(2,1)S(1)}, bf16[32,1024]{1,0:T(8,128)(2,1)S(1)}, u32[]{:S(2)}, u32[]{:S(2)}) collective-permute-start(bf16[32,1024]{1,0:T(8,128)(2,1)S(1)} %bitcast.18), channel_id=1, source_target_pairs={{0,3},{1,2},{2,1},{3,0},{4,7},{5,6},{6,5},{7,4},{8,11},{9,10},{10,... | collective-permute-start | bytes 196616 | tf_op jit(solution)/shard_map/ppermute | solution.py:475
  11.8 2.5 %collective-permute-done.14 = bf16[32,1024]{1,0:T(8,128)(2,1)S(1)} collective-permute-done((bf16[32,1024]{1,0:T(8,128)(2,1)S(1)}, bf16[32,1024]{1,0:T(8,128)(2,1)S(1)}, u32[]{:S(2)}, u32[]{:S(2)}) %collective-permute-start.14) | collective-permute-done | bytes 65568 | tf_op jit(solution)/shard_map/ppermute | solution.py:475
  14.3 1.8 %collective-permute-start = (bf16[32,1024]{1,0:T(8,128)(2,1)}, bf16[32,1024]{1,0:T(8,128)(2,1)S(1)}, u32[]{:S(2)}, u32[]{:S(2)}) collective-permute-start(bf16[32,1024]{1,0:T(8,128)(2,1)} %refs_0_.2), channel_id=1, source_target_pairs={{0,8},{4,12},{8,0},{12,4},{16,24},{20,28},{24,16},{28,20},{1,9},{5... | collective-permute-start | bytes 196616 | tf_op jit(solution)/shard_map/ppermute | solution.py:492
  16.1 0.3 collective-permute-done.15
  16.5 2.6 %collective-permute-start.1 = (bf16[32,1024]{1,0:T(8,128)(2,1)}, bf16[32,1024]{1,0:T(8,128)(2,1)S(1)}, u32[]{:S(2)}, u32[]{:S(2)}) collective-permute-start(bf16[32,1024]{1,0:T(8,128)(2,1)} %refs_0_.2), channel_id=1, source_target_pairs={{0,16},{4,20},{8,24},{12,28},{16,0},{20,4},{24,8},{28,12},{1,17},{... | collective-permute-start | bytes 196616 | tf_op jit(solution)/shard_map/ppermute | solution.py:492
  19.1 1.3 %collective-permute-start.2 = (bf16[32,1024]{1,0:T(8,128)(2,1)}, bf16[32,1024]{1,0:T(8,128)(2,1)S(1)}, u32[]{:S(2)}, u32[]{:S(2)}) collective-permute-start(bf16[32,1024]{1,0:T(8,128)(2,1)} %refs_0_.2), channel_id=1, source_target_pairs={{0,24},{4,28},{8,16},{12,20},{16,8},{20,12},{24,0},{28,4},{1,25},{... | collective-permute-start | bytes 196616 | tf_op jit(solution)/shard_map/ppermute | solution.py:492
  20.4 0.0 collective-permute-done.refs_1_
  20.4 0.9 collective-permute-start.10
  21.3 1.9 %collective-permute-done.1.refs_2_ = bf16[32,1024]{1,0:T(8,128)(2,1)S(1)} collective-permute-done((bf16[32,1024]{1,0:T(8,128)(2,1)}, bf16[32,1024]{1,0:T(8,128)(2,1)S(1)}, u32[]{:S(2)}, u32[]{:S(2)}) %collective-permute-start.1) | collective-permute-done | bytes 65568 | tf_op jit(solution)/shard_map/ppermute | solution.py:492
  23.2 1.8 %collective-permute-start.11 = (bf16[256,1024]{1,0:T(8,128)(2,1)}, bf16[256,1024]{1,0:T(8,128)(2,1)S(1)}, u32[]{:S(2)}, u32[]{:S(2)}) collective-permute-start(bf16[256,1024]{1,0:T(8,128)(2,1)} %bitcast.12), channel_id=1, source_target_pairs={{0,2},{1,3},{2,0},{3,1},{4,6},{5,7},{6,4},{7,5},{8,10},{9,11},{10,... | collective-permute-start | bytes 1572872 | tf_op jit(solution)/shard_map/ppermute | solution.py:475
  24.9 0.4 collective-permute-done.2.refs_3_
  25.3 2.1 %collective-permute-start.27 = (bf16[528,256]{1,0:T(8,128)(2,1)S(1)}, bf16[528,256]{1,0:T(8,128)(2,1)S(1)}, u32[]{:S(2)}, u32[]{:S(2)}) collective-permute-start(bf16[528,256]{1,0:T(8,128)(2,1)S(1)} %get-tuple-element.38), channel_id=1, source_target_pairs={{0,3},{1,2},{2,1},{3,0},{4,7},{5,6},{6,5},{7,4},{8,11},{9,10},{10,... | collective-permute-start | bytes 811016 | tf_op jit(solution)/shard_map/ppermute | solution.py:475
  27.5 0.8 collective-permute-start.20
  28.3 0.7 collective-permute-start.23
  28.9 9.8 %collective-permute-done.27.rest_19_ = bf16[528,256]{1,0:T(8,128)(2,1)S(1)} collective-permute-done((bf16[528,256]{1,0:T(8,128)(2,1)S(1)}, bf16[528,256]{1,0:T(8,128)(2,1)S(1)}, u32[]{:S(2)}, u32[]{:S(2)}) %collective-permute-start.27) | collective-permute-done | bytes 270368 | tf_op jit(solution)/shard_map/ppermute | solution.py:475
  38.8 0.6 collective-permute-start.18
  39.3 0.0 collective-permute-done.20.rest_12_
  39.3 0.0 collective-permute-start.17
  39.3 0.0 collective-permute-done.23
  39.3 0.1 copy-done.16
  39.5 1.3 %collective-permute-start.22 = (bf16[128,1024]{1,0:T(8,128)(2,1)}, bf16[128,1024]{1,0:T(8,128)(2,1)S(1)}, u32[]{:S(2)}, u32[]{:S(2)}) collective-permute-start(bf16[128,1024]{1,0:T(8,128)(2,1)} %collective-permute-done.20.rest_12_), channel_id=1, source_target_pairs={{8,0},{16,24},{12,4},{20,28},{9,1},{17,25},{13,5},{21,29},{10,2},{... | collective-permute-start | bytes 786440 | tf_op jit(solution)/shard_map/ppermute | solution.py:505
  40.7 0.0 copy-start.2
  40.8 0.8 copy-done.2
  41.6 4.0 %collective-permute-done.18.rest_10_ = bf16[128,1024]{1,0:T(8,128)(2,1)} collective-permute-done((bf16[128,1024]{1,0:T(8,128)(2,1)S(1)}, bf16[128,1024]{1,0:T(8,128)(2,1)}, u32[]{:S(2)}, u32[]{:S(2)}) %collective-permute-start.18) | collective-permute-done | bytes 262176 | tf_op jit(solution)/shard_map/ppermute | solution.py:492
  45.6 0.5 collective-permute-start.4
  46.1 0.0 collective-permute-done.10.refs_0_
  46.1 2.1 %collective-permute-start.6 = (bf16[128,1024]{1,0:T(8,128)(2,1)S(1)}, bf16[128,1024]{1,0:T(8,128)(2,1)S(1)}, u32[]{:S(2)}, u32[]{:S(2)}) collective-permute-start(bf16[128,1024]{1,0:T(8,128)(2,1)S(1)} %shard_map.113.refs_0_), channel_id=1, source_target_pairs={{0,2},{1,3},{2,0},{3,1},{4,6},{5,7},{6,4},{7,5},{8,10},{9,11},{10,... | collective-permute-start | bytes 786440 | tf_op jit(solution)/shard_map/ppermute | solution.py:475
  48.3 0.9 collective-permute-start.8
  49.1 2.2 %shard_map.116 = (bf16[128,1024]{1,0:T(8,128)(2,1)}, bf16[128,1024]{1,0:T(8,128)(2,1)}, bf16[128,1024]{1,0:T(8,128)(2,1)}, bf16[128,1024]{1,0:T(8,128)(2,1)}) custom-call(f32[1,1024]{1,0:T(1,128)} %bitcast.23, bf16[256,1024]{1,0:T(8,128)(2,1)S(1)} %collective-permute-done.10.refs_0_, bf16[256,1024]{1,0:T(8,128)(2,1)S(1)} %collective-permute-done.11.refs_1_), custom_call_target="tpu_custom_call" | custom-call | bytes 1 | tf_op jit(solution)/shard_map/pallas_call | solution.py:222
  51.3 0.0 collective-permute-done.17.rest_9_
  51.3 0.5 collective-permute-start.19
  51.9 1.3 %collective-permute-done.4.refs_2_ = bf16[128,1024]{1,0:T(8,128)(2,1)S(1)} collective-permute-done((bf16[128,1024]{1,0:T(8,128)(2,1)S(1)}, bf16[128,1024]{1,0:T(8,128)(2,1)S(1)}, u32[]{:S(2)}, u32[]{:S(2)}) %collective-permute-start.4) | collective-permute-done | bytes 262176 | tf_op jit(solution)/shard_map/ppermute | solution.py:475
  53.2 1.3 %collective-permute-start.12 = (bf16[128,1024]{1,0:T(8,128)(2,1)}, bf16[128,1024]{1,0:T(8,128)(2,1)S(1)}, u32[]{:S(2)}, u32[]{:S(2)}) collective-permute-start(bf16[128,1024]{1,0:T(8,128)(2,1)} %get-tuple-element.27.rest_2_), channel_id=1, source_target_pairs={{0,2},{1,3},{2,0},{3,1},{4,6},{5,7},{6,4},{7,5},{8,10},{9,11},{10,... | collective-permute-start | bytes 786440 | tf_op jit(solution)/shard_map/ppermute | solution.py:488
  54.5 2.6 %collective-permute-done.6.refs_4_ = bf16[128,1024]{1,0:T(8,128)(2,1)S(1)} collective-permute-done((bf16[128,1024]{1,0:T(8,128)(2,1)S(1)}, bf16[128,1024]{1,0:T(8,128)(2,1)S(1)}, u32[]{:S(2)}, u32[]{:S(2)}) %collective-permute-start.6) | collective-permute-done | bytes 262176 | tf_op jit(solution)/shard_map/ppermute | solution.py:475
  57.1 0.6 collective-permute-start.13
  57.7 0.5 collective-permute-start.3
  58.2 0.1 collective-permute-start.5
  58.3 1.8 %shard_map.115 = (bf16[128,1024]{1,0:T(8,128)(2,1)}, bf16[128,1024]{1,0:T(8,128)(2,1)}) custom-call(f32[1,1024]{1,0:T(1,128)} %bitcast.24, bf16[256,1024]{1,0:T(8,128)(2,1)S(1)} %bitcast.13), custom_call_target="tpu_custom_call" | custom-call | bytes 1 | tf_op jit(solution)/shard_map/pallas_call | solution.py:222
  60.1 2.6 %collective-permute-done.12.rest_6_ = bf16[128,1024]{1,0:T(8,128)(2,1)S(1)} collective-permute-done((bf16[128,1024]{1,0:T(8,128)(2,1)}, bf16[128,1024]{1,0:T(8,128)(2,1)S(1)}, u32[]{:S(2)}, u32[]{:S(2)}) %collective-permute-start.12) | collective-permute-done | bytes 262176 | tf_op jit(solution)/shard_map/ppermute | solution.py:488
  62.7 1.0 %collective-permute-done.13.rest_7_ = bf16[128,1024]{1,0:T(8,128)(2,1)S(1)} collective-permute-done((bf16[128,1024]{1,0:T(8,128)(2,1)}, bf16[128,1024]{1,0:T(8,128)(2,1)S(1)}, u32[]{:S(2)}, u32[]{:S(2)}) %collective-permute-start.13) | collective-permute-done | bytes 262176 | tf_op jit(solution)/shard_map/ppermute | solution.py:488
  63.7 0.7 copy-done.20
  64.4 6.5 %shard_map.119 = (f32[1024,256]{1,0:T(8,128)S(1)}, f32[1024,256]{1,0:T(8,128)S(1)}, f32[16,128]{1,0:T(8,128)S(1)}) custom-call(bf16[128,1024]{1,0:T(8,128)(2,1)} %get-tuple-element.25.rest_0_, bf16[128,1024]{1,0:T(8,128)(2,1)} %get-tuple-element.26.rest_1_, bf16[128,1024]{1,0:T(8,128)(2,1)} %get-tuple-element.27.rest_2_, ...), custom_call_target="tpu_custom_call" | custom-call | flops 2147483648 | bytes 1 | tf_op jit(solution)/shard_map/pallas_call | solution.py:357
  70.9 0.7 collective-permute-start.28
  71.6 3.0 %collective-permute-done.28.rest_1_ = f32[16,128]{1,0:T(8,128)S(1)} collective-permute-done((f32[16,128]{1,0:T(8,128)S(1)}, f32[16,128]{1,0:T(8,128)S(1)}, u32[]{:S(2)}, u32[]{:S(2)}) %collective-permute-start.28) | collective-permute-done | bytes 8224 | tf_op jit(solution)/shard_map/ppermute | solution.py:475
  74.6 1.4 %collective-permute-start.29 = (f32[16,128]{1,0:T(8,128)S(1)}, f32[16,128]{1,0:T(8,128)S(1)}, u32[]{:S(2)}, u32[]{:S(2)}) collective-permute-start(f32[16,128]{1,0:T(8,128)S(1)} %get-tuple-element.41.rest_0_), channel_id=1, source_target_pairs={{0,2},{1,3},{2,0},{3,1},{4,6},{5,7},{6,4},{7,5},{8,10},{9,11},{10,... | collective-permute-start | bytes 24584 | tf_op jit(solution)/shard_map/ppermute | solution.py:475
  76.1 2.2 %collective-permute-done.29.rest_2_ = f32[16,128]{1,0:T(8,128)S(1)} collective-permute-done((f32[16,128]{1,0:T(8,128)S(1)}, f32[16,128]{1,0:T(8,128)S(1)}, u32[]{:S(2)}, u32[]{:S(2)}) %collective-permute-start.29) | collective-permute-done | bytes 8224 | tf_op jit(solution)/shard_map/ppermute | solution.py:475
  78.3 1.8 %collective-permute-start.30 = (f32[16,128]{1,0:T(8,128)S(1)}, f32[16,128]{1,0:T(8,128)S(1)}, u32[]{:S(2)}, u32[]{:S(2)}) collective-permute-start(f32[16,128]{1,0:T(8,128)S(1)} %get-tuple-element.41.rest_0_), channel_id=1, source_target_pairs={{0,3},{1,2},{2,1},{3,0},{4,7},{5,6},{6,5},{7,4},{8,11},{9,10},{10,... | collective-permute-start | bytes 24584 | tf_op jit(solution)/shard_map/ppermute | solution.py:475
  80.1 2.7 %collective-permute-done.30.rest_3_ = f32[16,128]{1,0:T(8,128)S(1)} collective-permute-done((f32[16,128]{1,0:T(8,128)S(1)}, f32[16,128]{1,0:T(8,128)S(1)}, u32[]{:S(2)}, u32[]{:S(2)}) %collective-permute-start.30) | collective-permute-done | bytes 8224 | tf_op jit(solution)/shard_map/ppermute | solution.py:475
  82.9 0.6 shard_map.120
  83.5 0.7 collective-permute-start.31
  84.2 1.8 %collective-permute-start.32 = (bf16[256,256]{1,0:T(8,128)(2,1)S(1)}, bf16[256,256]{1,0:T(8,128)(2,1)S(1)}, u32[]{:S(2)}, u32[]{:S(2)}) collective-permute-start(bf16[256,256]{1,0:T(8,128)(2,1)S(1)} %get-tuple-element.44), channel_id=1, source_target_pairs={{0,2},{1,3},{2,0},{3,1},{4,6},{5,7},{6,4},{7,5},{8,10},{9,11},{10,... | collective-permute-start | bytes 393224 | tf_op jit(solution)/shard_map/ppermute | solution.py:475
  86.1 1.1 %collective-permute-start.33 = (bf16[256,256]{1,0:T(8,128)(2,1)S(1)}, bf16[256,256]{1,0:T(8,128)(2,1)S(1)}, u32[]{:S(2)}, u32[]{:S(2)}) collective-permute-start(bf16[256,256]{1,0:T(8,128)(2,1)S(1)} %get-tuple-element.45), channel_id=1, source_target_pairs={{0,3},{1,2},{2,1},{3,0},{4,7},{5,6},{6,5},{7,4},{8,11},{9,10},{10,... | collective-permute-start | bytes 393224 | tf_op jit(solution)/shard_map/ppermute | solution.py:475
  87.2 0.7 copy-done.11
  87.9 0.7 copy-done.12
  88.6 1.8 %shard_map.114.weight = bf16[1024,1024]{1,0:T(8,128)(2,1)S(1)} custom-call(bf16[128,1024]{1,0:T(8,128)(2,1)} %copy-done.1, bf16[128,1024]{1,0:T(8,128)(2,1)} %copy-done.9, bf16[128,1024]{1,0:T(8,128)(2,1)} %copy-done.6, bf16[128,1024]{1,0:T(8,128)(2,1)} %copy-done.10, bf16[128,1024]{1,0:T(8,128)(2,1)} %copy-done.7, bf16[128,1024]{1,0:T(8,128)(2,1)} %copy-done.11, ...), custom_call_target="tpu_custom_call" | custom-call | bytes 1 | tf_op jit(solution)/shard_map/pallas_call | solution.py:409
  90.4 1.6 %collective-permute-done.33.rest_3_ = bf16[256,256]{1,0:T(8,128)(2,1)S(1)} collective-permute-done((bf16[256,256]{1,0:T(8,128)(2,1)S(1)}, bf16[256,256]{1,0:T(8,128)(2,1)S(1)}, u32[]{:S(2)}, u32[]{:S(2)}) %collective-permute-start.33) | collective-permute-done | bytes 131104 | tf_op jit(solution)/shard_map/ppermute | solution.py:475
  92.0 2.2 %shard_map.121 = (bf16[256,1024]{1,0:T(8,128)(2,1)}, f32[2,128]{1,0:T(2,128)}) custom-call(s32[2]{0:T(128)S(1)} %copy-done.5, f32[1,1024]{1,0:T(1,128)S(1)} %bitcast.17, bf16[256,1024]{1,0:T(8,128)(2,1)S(1)} %bitcast.14, bf16[1024,1024]{1,0:T(8,128)(2,1)S(1)} %shard_map.114.weight, bf16[256,256]{1,0:T(8,128)(2,1)S(1)} %get-tuple-element.42.rest_0_, ...), custom_call_target="tpu_custom_call" | custom-call | flops 536870912 | bytes 1 | tf_op jit(solution)/shard_map/pallas_call | solution.py:451
  (57 shorter events, 0.2 us)
Async XLA Ops:
  0.6 57.7 %copy-start = (bf16[2,128,1024]{2,1,0:T(8,128)(2,1)S(1)}, bf16[2,128,1024]{2,1,0:T(8,128)(2,1)}, u32[]{:S(2)}) copy-start(bf16[2,128,1024]{2,1,0:T(8,128)(2,1)} %param.10) | copy-start | bytes 1572868
  2.8 24.7 %collective-permute-start.25 = (bf16[528,256]{1,0:T(8,128)(2,1)S(1)}, bf16[528,256]{1,0:T(8,128)(2,1)S(1)}, u32[]{:S(2)}, u32[]{:S(2)}) collective-permute-start(bf16[528,256]{1,0:T(8,128)(2,1)S(1)} %get-tuple-element.36), channel_id=1, source_target_pairs={{0,1},{1,0},{2,3},{3,2},{4,5},{5,4},{6,7},{7,6},{8,9},{9,8},{10,11... | collective-permute-start | bytes 811016 | tf_op jit(solution)/shard_map/ppermute | solution.py:475
  5.7 22.5 %collective-permute-start.26 = (bf16[528,256]{1,0:T(8,128)(2,1)S(1)}, bf16[528,256]{1,0:T(8,128)(2,1)S(1)}, u32[]{:S(2)}, u32[]{:S(2)}) collective-permute-start(bf16[528,256]{1,0:T(8,128)(2,1)S(1)} %get-tuple-element.37), channel_id=1, source_target_pairs={{0,2},{1,3},{2,0},{3,1},{4,6},{5,7},{6,4},{7,5},{8,10},{9,11},{10,... | collective-permute-start | bytes 811016 | tf_op jit(solution)/shard_map/ppermute | solution.py:475
  8.2 6.1 %collective-permute-start.14 = (bf16[32,1024]{1,0:T(8,128)(2,1)S(1)}, bf16[32,1024]{1,0:T(8,128)(2,1)S(1)}, u32[]{:S(2)}, u32[]{:S(2)}) collective-permute-start(bf16[32,1024]{1,0:T(8,128)(2,1)S(1)} %bitcast.20), channel_id=1, source_target_pairs={{0,1},{1,0},{2,3},{3,2},{4,5},{5,4},{6,7},{7,6},{8,9},{9,8},{10,11... | collective-permute-start | bytes 196616 | tf_op jit(solution)/shard_map/ppermute | solution.py:475
  8.8 7.6 %collective-permute-start.15 = (bf16[32,1024]{1,0:T(8,128)(2,1)S(1)}, bf16[32,1024]{1,0:T(8,128)(2,1)S(1)}, u32[]{:S(2)}, u32[]{:S(2)}) collective-permute-start(bf16[32,1024]{1,0:T(8,128)(2,1)S(1)} %bitcast.19), channel_id=1, source_target_pairs={{0,2},{1,3},{2,0},{3,1},{4,6},{5,7},{6,4},{7,5},{8,10},{9,11},{10,... | collective-permute-start | bytes 196616 | tf_op jit(solution)/shard_map/ppermute | solution.py:475
  8.9 10.2 %collective-permute-start.16 = (bf16[32,1024]{1,0:T(8,128)(2,1)S(1)}, bf16[32,1024]{1,0:T(8,128)(2,1)S(1)}, u32[]{:S(2)}, u32[]{:S(2)}) collective-permute-start(bf16[32,1024]{1,0:T(8,128)(2,1)S(1)} %bitcast.18), channel_id=1, source_target_pairs={{0,3},{1,2},{2,1},{3,0},{4,7},{5,6},{6,5},{7,4},{8,11},{9,10},{10,... | collective-permute-start | bytes 196616 | tf_op jit(solution)/shard_map/ppermute | solution.py:475
  14.3 6.1 %collective-permute-start = (bf16[32,1024]{1,0:T(8,128)(2,1)}, bf16[32,1024]{1,0:T(8,128)(2,1)S(1)}, u32[]{:S(2)}, u32[]{:S(2)}) collective-permute-start(bf16[32,1024]{1,0:T(8,128)(2,1)} %refs_0_.2), channel_id=1, source_target_pairs={{0,8},{4,12},{8,0},{12,4},{16,24},{20,28},{24,16},{28,20},{1,9},{5... | collective-permute-start | bytes 196616 | tf_op jit(solution)/shard_map/ppermute | solution.py:492
  16.5 6.7 %collective-permute-start.1 = (bf16[32,1024]{1,0:T(8,128)(2,1)}, bf16[32,1024]{1,0:T(8,128)(2,1)S(1)}, u32[]{:S(2)}, u32[]{:S(2)}) collective-permute-start(bf16[32,1024]{1,0:T(8,128)(2,1)} %refs_0_.2), channel_id=1, source_target_pairs={{0,16},{4,20},{8,24},{12,28},{16,0},{20,4},{24,8},{28,12},{1,17},{... | collective-permute-start | bytes 196616 | tf_op jit(solution)/shard_map/ppermute | solution.py:492
  19.1 6.3 %collective-permute-start.2 = (bf16[32,1024]{1,0:T(8,128)(2,1)}, bf16[32,1024]{1,0:T(8,128)(2,1)S(1)}, u32[]{:S(2)}, u32[]{:S(2)}) collective-permute-start(bf16[32,1024]{1,0:T(8,128)(2,1)} %refs_0_.2), channel_id=1, source_target_pairs={{0,24},{4,28},{8,16},{12,20},{16,8},{20,12},{24,0},{28,4},{1,25},{... | collective-permute-start | bytes 196616 | tf_op jit(solution)/shard_map/ppermute | solution.py:492
  20.4 25.7 %collective-permute-start.10 = (bf16[256,1024]{1,0:T(8,128)(2,1)}, bf16[256,1024]{1,0:T(8,128)(2,1)S(1)}, u32[]{:S(2)}, u32[]{:S(2)}) collective-permute-start(bf16[256,1024]{1,0:T(8,128)(2,1)} %bitcast.11), channel_id=1, source_target_pairs={{0,1},{1,0},{2,3},{3,2},{4,5},{5,4},{6,7},{7,6},{8,9},{9,8},{10,11... | collective-permute-start | bytes 1572872 | tf_op jit(solution)/shard_map/ppermute | solution.py:475
  23.2 25.1 %collective-permute-start.11 = (bf16[256,1024]{1,0:T(8,128)(2,1)}, bf16[256,1024]{1,0:T(8,128)(2,1)S(1)}, u32[]{:S(2)}, u32[]{:S(2)}) collective-permute-start(bf16[256,1024]{1,0:T(8,128)(2,1)} %bitcast.12), channel_id=1, source_target_pairs={{0,2},{1,3},{2,0},{3,1},{4,6},{5,7},{6,4},{7,5},{8,10},{9,11},{10,... | collective-permute-start | bytes 1572872 | tf_op jit(solution)/shard_map/ppermute | solution.py:475
  25.3 13.4 %collective-permute-start.27 = (bf16[528,256]{1,0:T(8,128)(2,1)S(1)}, bf16[528,256]{1,0:T(8,128)(2,1)S(1)}, u32[]{:S(2)}, u32[]{:S(2)}) collective-permute-start(bf16[528,256]{1,0:T(8,128)(2,1)S(1)} %get-tuple-element.38), channel_id=1, source_target_pairs={{0,3},{1,2},{2,1},{3,0},{4,7},{5,6},{6,5},{7,4},{8,11},{9,10},{10,... | collective-permute-start | bytes 811016 | tf_op jit(solution)/shard_map/ppermute | solution.py:475
  27.5 36.2 %copy-start.13 = (bf16[128,1024]{1,0:T(8,128)(2,1)}, bf16[128,1024]{1,0:T(8,128)(2,1)S(1)}, u32[]{:S(2)}) copy-start(bf16[128,1024]{1,0:T(8,128)(2,1)S(1)} %pad_maximum_fusion.rest_8_) | copy-start | bytes 786436
  27.5 14.1 %copy-start.14 = (bf16[528,256]{1,0:T(8,128)(2,1)}, bf16[528,256]{1,0:T(8,128)(2,1)S(1)}, u32[]{:S(2)}) copy-start(bf16[528,256]{1,0:T(8,128)(2,1)S(1)} %collective-permute-done.25.rest_17_) | copy-start | bytes 811012
  27.5 11.8 %collective-permute-start.20 = (bf16[128,1024]{1,0:T(8,128)(2,1)S(1)}, bf16[128,1024]{1,0:T(8,128)(2,1)}, u32[]{:S(2)}, u32[]{:S(2)}) collective-permute-start(bf16[128,1024]{1,0:T(8,128)(2,1)S(1)} %pad_maximum_fusion.rest_8_), channel_id=1, source_target_pairs={{0,16},{4,20},{8,24},{12,28},{16,0},{20,4},{24,8},{28,12},{1,17},{... | collective-permute-start | bytes 786440 | tf_op jit(solution)/shard_map/ppermute | solution.py:492
  28.3 17.8 %copy-start.15 = (bf16[528,256]{1,0:T(8,128)(2,1)}, bf16[528,256]{1,0:T(8,128)(2,1)S(1)}, u32[]{:S(2)}) copy-start(bf16[528,256]{1,0:T(8,128)(2,1)S(1)} %collective-permute-done.26.rest_18_) | copy-start | bytes 811012
  28.3 11.1 %collective-permute-start.23 = (bf16[128,1024]{1,0:T(8,128)(2,1)S(1)}, bf16[128,1024]{1,0:T(8,128)(2,1)S(1)}, u32[]{:S(2)}, u32[]{:S(2)}) collective-permute-start(bf16[128,1024]{1,0:T(8,128)(2,1)S(1)} %pad_maximum_fusion.rest_8_), channel_id=1, source_target_pairs={{8,16},{16,8},{12,20},{20,12},{9,17},{17,9},{13,21},{21,13},{10,18... | collective-permute-start | bytes 786440 | tf_op jit(solution)/shard_map/ppermute | solution.py:503
  38.7 0.7 copy-start.16
  38.8 6.9 %collective-permute-start.18 = (bf16[128,1024]{1,0:T(8,128)(2,1)S(1)}, bf16[128,1024]{1,0:T(8,128)(2,1)}, u32[]{:S(2)}, u32[]{:S(2)}) collective-permute-start(bf16[128,1024]{1,0:T(8,128)(2,1)S(1)} %pad_maximum_fusion.rest_8_), channel_id=1, source_target_pairs={{0,8},{4,12},{8,0},{12,4},{16,24},{20,28},{24,16},{28,20},{1,9},{5... | collective-permute-start | bytes 786440 | tf_op jit(solution)/shard_map/ppermute | solution.py:492
  39.3 12.0 %collective-permute-start.17 = (bf16[128,1024]{1,0:T(8,128)(2,1)S(1)}, bf16[128,1024]{1,0:T(8,128)(2,1)}, u32[]{:S(2)}, u32[]{:S(2)}) collective-permute-start(bf16[128,1024]{1,0:T(8,128)(2,1)S(1)} %pad_maximum_fusion.rest_8_), channel_id=1, source_target_pairs={{0,4},{4,0},{8,12},{12,8},{16,20},{20,16},{24,28},{28,24},{1,5},{5... | collective-permute-start | bytes 786440 | tf_op jit(solution)/shard_map/ppermute | solution.py:495
  39.5 11.9 %collective-permute-start.22 = (bf16[128,1024]{1,0:T(8,128)(2,1)}, bf16[128,1024]{1,0:T(8,128)(2,1)S(1)}, u32[]{:S(2)}, u32[]{:S(2)}) collective-permute-start(bf16[128,1024]{1,0:T(8,128)(2,1)} %collective-permute-done.20.rest_12_), channel_id=1, source_target_pairs={{8,0},{16,24},{12,4},{20,28},{9,1},{17,25},{13,5},{21,29},{10,2},{... | collective-permute-start | bytes 786440 | tf_op jit(solution)/shard_map/ppermute | solution.py:505
  40.7 0.8 copy-start.2
  41.6 29.3 %copy-start.1 = (bf16[128,1024]{1,0:T(8,128)(2,1)}, bf16[128,1024]{1,0:T(8,128)(2,1)S(1)}, u32[]{:S(2)}) copy-start(bf16[128,1024]{1,0:T(8,128)(2,1)S(1)} %shard_map.113.refs_0_) | copy-start | bytes 786436
  45.6 7.5 %collective-permute-start.4 = (bf16[128,1024]{1,0:T(8,128)(2,1)S(1)}, bf16[128,1024]{1,0:T(8,128)(2,1)S(1)}, u32[]{:S(2)}, u32[]{:S(2)}) collective-permute-start(bf16[128,1024]{1,0:T(8,128)(2,1)S(1)} %shard_map.113.refs_0_), channel_id=1, source_target_pairs={{0,1},{1,0},{2,3},{3,2},{4,5},{5,4},{6,7},{7,6},{8,9},{9,8},{10,11... | collective-permute-start | bytes 786440 | tf_op jit(solution)/shard_map/ppermute | solution.py:475
  46.1 10.9 %collective-permute-start.6 = (bf16[128,1024]{1,0:T(8,128)(2,1)S(1)}, bf16[128,1024]{1,0:T(8,128)(2,1)S(1)}, u32[]{:S(2)}, u32[]{:S(2)}) collective-permute-start(bf16[128,1024]{1,0:T(8,128)(2,1)S(1)} %shard_map.113.refs_0_), channel_id=1, source_target_pairs={{0,2},{1,3},{2,0},{3,1},{4,6},{5,7},{6,4},{7,5},{8,10},{9,11},{10,... | collective-permute-start | bytes 786440 | tf_op jit(solution)/shard_map/ppermute | solution.py:475
  48.3 9.4 %collective-permute-start.8 = (bf16[128,1024]{1,0:T(8,128)(2,1)S(1)}, bf16[128,1024]{1,0:T(8,128)(2,1)S(1)}, u32[]{:S(2)}, u32[]{:S(2)}) collective-permute-start(bf16[128,1024]{1,0:T(8,128)(2,1)S(1)} %shard_map.113.refs_0_), channel_id=1, source_target_pairs={{0,3},{1,2},{2,1},{3,0},{4,7},{5,6},{6,5},{7,4},{8,11},{9,10},{10,... | collective-permute-start | bytes 786440 | tf_op jit(solution)/shard_map/ppermute | solution.py:475
  51.3 6.4 %collective-permute-start.21 = (bf16[128,1024]{1,0:T(8,128)(2,1)}, bf16[128,1024]{1,0:T(8,128)(2,1)S(1)}, u32[]{:S(2)}, u32[]{:S(2)}) collective-permute-start(bf16[128,1024]{1,0:T(8,128)(2,1)} %collective-permute-done.20.rest_12_), channel_id=1, source_target_pairs={{0,4},{4,0},{8,12},{12,8},{16,20},{20,16},{24,28},{28,24},{1,5},{5... | collective-permute-start | bytes 786440 | tf_op jit(solution)/shard_map/ppermute | solution.py:495
  51.3 6.9 %collective-permute-start.19 = (bf16[128,1024]{1,0:T(8,128)(2,1)}, bf16[128,1024]{1,0:T(8,128)(2,1)S(1)}, u32[]{:S(2)}, u32[]{:S(2)}) collective-permute-start(bf16[128,1024]{1,0:T(8,128)(2,1)} %collective-permute-done.18.rest_10_), channel_id=1, source_target_pairs={{0,4},{4,0},{8,12},{12,8},{16,20},{20,16},{24,28},{28,24},{1,5},{5... | collective-permute-start | bytes 786440 | tf_op jit(solution)/shard_map/ppermute | solution.py:495
  53.2 17.7 %copy-start.6 = (bf16[128,1024]{1,0:T(8,128)(2,1)}, bf16[128,1024]{1,0:T(8,128)(2,1)S(1)}, u32[]{:S(2)}) copy-start(bf16[128,1024]{1,0:T(8,128)(2,1)S(1)} %collective-permute-done.4.refs_2_) | copy-start | bytes 786436
  53.2 9.5 %collective-permute-start.12 = (bf16[128,1024]{1,0:T(8,128)(2,1)}, bf16[128,1024]{1,0:T(8,128)(2,1)S(1)}, u32[]{:S(2)}, u32[]{:S(2)}) collective-permute-start(bf16[128,1024]{1,0:T(8,128)(2,1)} %get-tuple-element.27.rest_2_), channel_id=1, source_target_pairs={{0,2},{1,3},{2,0},{3,1},{4,6},{5,7},{6,4},{7,5},{8,10},{9,11},{10,... | collective-permute-start | bytes 786440 | tf_op jit(solution)/shard_map/ppermute | solution.py:488
  57.1 13.8 %copy-start.7 = (bf16[128,1024]{1,0:T(8,128)(2,1)}, bf16[128,1024]{1,0:T(8,128)(2,1)S(1)}, u32[]{:S(2)}) copy-start(bf16[128,1024]{1,0:T(8,128)(2,1)S(1)} %collective-permute-done.6.refs_4_) | copy-start | bytes 786436
  57.1 6.6 %collective-permute-start.13 = (bf16[128,1024]{1,0:T(8,128)(2,1)}, bf16[128,1024]{1,0:T(8,128)(2,1)S(1)}, u32[]{:S(2)}, u32[]{:S(2)}) collective-permute-start(bf16[128,1024]{1,0:T(8,128)(2,1)} %get-tuple-element.30.rest_5_), channel_id=1, source_target_pairs={{0,1},{1,0},{2,3},{3,2},{4,5},{5,4},{6,7},{7,6},{8,9},{9,8},{10,11... | collective-permute-start | bytes 786440 | tf_op jit(solution)/shard_map/ppermute | solution.py:488
  57.7 13.2 %copy-start.8 = (bf16[128,1024]{1,0:T(8,128)(2,1)}, bf16[128,1024]{1,0:T(8,128)(2,1)S(1)}, u32[]{:S(2)}) copy-start(bf16[128,1024]{1,0:T(8,128)(2,1)S(1)} %collective-permute-done.8.refs_6_) | copy-start | bytes 786436
  57.7 6.0 %collective-permute-start.24 = (bf16[128,1024]{1,0:T(8,128)(2,1)S(1)}, bf16[128,1024]{1,0:T(8,128)(2,1)S(1)}, u32[]{:S(2)}, u32[]{:S(2)}) collective-permute-start(bf16[128,1024]{1,0:T(8,128)(2,1)S(1)} %broadcast_select_fusion.rest_14_), channel_id=1, source_target_pairs={{0,4},{4,0},{8,12},{12,8},{16,20},{20,16},{24,28},{28,24},{1,5},{5... | collective-permute-start | bytes 786440 | tf_op jit(solution)/shard_map/ppermute | solution.py:495
  57.7 6.0 %copy-start.17 = (bf16[128,1024]{1,0:T(8,128)(2,1)}, bf16[128,1024]{1,0:T(8,128)(2,1)S(1)}, u32[]{:S(2)}) copy-start(bf16[128,1024]{1,0:T(8,128)(2,1)S(1)} %collective-permute-done.21.rest_13_) | copy-start | bytes 786436
  57.7 26.5 %collective-permute-start.3 = (bf16[128,1024]{1,0:T(8,128)(2,1)S(1)}, bf16[128,1024]{1,0:T(8,128)(2,1)S(1)}, u32[]{:S(2)}, u32[]{:S(2)}) collective-permute-start(bf16[128,1024]{1,0:T(8,128)(2,1)S(1)} %shard_map.113.refs_0_), channel_id=1, source_target_pairs={{0,4},{4,0},{8,12},{12,8},{16,20},{20,16},{24,28},{28,24},{1,5},{5... | collective-permute-start | bytes 786440 | tf_op jit(solution)/shard_map/ppermute | solution.py:495
  58.2 5.5 %copy-start.18 = (bf16[128,1024]{1,0:T(8,128)(2,1)}, bf16[128,1024]{1,0:T(8,128)(2,1)S(1)}, u32[]{:S(2)}) copy-start(bf16[128,1024]{1,0:T(8,128)(2,1)S(1)} %collective-permute-done.19.rest_11_) | copy-start | bytes 786436
  58.2 27.8 %collective-permute-start.5 = (bf16[128,1024]{1,0:T(8,128)(2,1)S(1)}, bf16[128,1024]{1,0:T(8,128)(2,1)S(1)}, u32[]{:S(2)}, u32[]{:S(2)}) collective-permute-start(bf16[128,1024]{1,0:T(8,128)(2,1)S(1)} %collective-permute-done.4.refs_2_), channel_id=1, source_target_pairs={{0,4},{4,0},{8,12},{12,8},{16,20},{20,16},{24,28},{28,24},{1,5},{5... | collective-permute-start | bytes 786440 | tf_op jit(solution)/shard_map/ppermute | solution.py:495
  62.7 1.0 %copy-start.19 = (bf16[128,1024]{1,0:T(8,128)(2,1)}, bf16[128,1024]{1,0:T(8,128)(2,1)S(1)}, u32[]{:S(2)}) copy-start(bf16[128,1024]{1,0:T(8,128)(2,1)S(1)} %collective-permute-done.12.rest_6_) | copy-start | bytes 786436
  62.7 24.4 %collective-permute-start.7 = (bf16[128,1024]{1,0:T(8,128)(2,1)S(1)}, bf16[128,1024]{1,0:T(8,128)(2,1)S(1)}, u32[]{:S(2)}, u32[]{:S(2)}) collective-permute-start(bf16[128,1024]{1,0:T(8,128)(2,1)S(1)} %collective-permute-done.6.refs_4_), channel_id=1, source_target_pairs={{0,4},{4,0},{8,12},{12,8},{16,20},{20,16},{24,28},{28,24},{1,5},{5... | collective-permute-start | bytes 786440 | tf_op jit(solution)/shard_map/ppermute | solution.py:495
  63.6 0.7 copy-start.20
  63.7 23.5 %collective-permute-start.9 = (bf16[128,1024]{1,0:T(8,128)(2,1)S(1)}, bf16[128,1024]{1,0:T(8,128)(2,1)S(1)}, u32[]{:S(2)}, u32[]{:S(2)}) collective-permute-start(bf16[128,1024]{1,0:T(8,128)(2,1)S(1)} %collective-permute-done.8.refs_6_), channel_id=1, source_target_pairs={{0,4},{4,0},{8,12},{12,8},{16,20},{20,16},{24,28},{28,24},{1,5},{5... | collective-permute-start | bytes 786440 | tf_op jit(solution)/shard_map/ppermute | solution.py:495
  64.4 18.5 %copy-start.3 = (f32[1024]{0:T(1024)S(1)}, f32[1024]{0:T(1024)}, u32[]{:S(2)}) copy-start(f32[1024]{0:T(1024)} %param.18) | copy-start | bytes 12292
  70.9 3.7 %collective-permute-start.28 = (f32[16,128]{1,0:T(8,128)S(1)}, f32[16,128]{1,0:T(8,128)S(1)}, u32[]{:S(2)}, u32[]{:S(2)}) collective-permute-start(f32[16,128]{1,0:T(8,128)S(1)} %get-tuple-element.41.rest_0_), channel_id=1, source_target_pairs={{0,1},{1,0},{2,3},{3,2},{4,5},{5,4},{6,7},{7,6},{8,9},{9,8},{10,11... | collective-permute-start | bytes 24584 | tf_op jit(solution)/shard_map/ppermute | solution.py:475
  74.6 3.7 %collective-permute-start.29 = (f32[16,128]{1,0:T(8,128)S(1)}, f32[16,128]{1,0:T(8,128)S(1)}, u32[]{:S(2)}, u32[]{:S(2)}) collective-permute-start(f32[16,128]{1,0:T(8,128)S(1)} %get-tuple-element.41.rest_0_), channel_id=1, source_target_pairs={{0,2},{1,3},{2,0},{3,1},{4,6},{5,7},{6,4},{7,5},{8,10},{9,11},{10,... | collective-permute-start | bytes 24584 | tf_op jit(solution)/shard_map/ppermute | solution.py:475
  78.3 4.5 %collective-permute-start.30 = (f32[16,128]{1,0:T(8,128)S(1)}, f32[16,128]{1,0:T(8,128)S(1)}, u32[]{:S(2)}, u32[]{:S(2)}) collective-permute-start(f32[16,128]{1,0:T(8,128)S(1)} %get-tuple-element.41.rest_0_), channel_id=1, source_target_pairs={{0,3},{1,2},{2,1},{3,0},{4,7},{5,6},{6,5},{7,4},{8,11},{9,10},{10,... | collective-permute-start | bytes 24584 | tf_op jit(solution)/shard_map/ppermute | solution.py:475
  83.5 6.9 %collective-permute-start.31 = (bf16[256,256]{1,0:T(8,128)(2,1)S(1)}, bf16[256,256]{1,0:T(8,128)(2,1)S(1)}, u32[]{:S(2)}, u32[]{:S(2)}) collective-permute-start(bf16[256,256]{1,0:T(8,128)(2,1)S(1)} %get-tuple-element.43), channel_id=1, source_target_pairs={{0,1},{1,0},{2,3},{3,2},{4,5},{5,4},{6,7},{7,6},{8,9},{9,8},{10,11... | collective-permute-start | bytes 393224 | tf_op jit(solution)/shard_map/ppermute | solution.py:475
  84.2 3.0 %copy-start.9 = (bf16[128,1024]{1,0:T(8,128)(2,1)}, bf16[128,1024]{1,0:T(8,128)(2,1)S(1)}, u32[]{:S(2)}) copy-start(bf16[128,1024]{1,0:T(8,128)(2,1)S(1)} %collective-permute-done.3.refs_1_) | copy-start | bytes 786436
  84.2 6.2 %collective-permute-start.32 = (bf16[256,256]{1,0:T(8,128)(2,1)S(1)}, bf16[256,256]{1,0:T(8,128)(2,1)S(1)}, u32[]{:S(2)}, u32[]{:S(2)}) collective-permute-start(bf16[256,256]{1,0:T(8,128)(2,1)S(1)} %get-tuple-element.44), channel_id=1, source_target_pairs={{0,2},{1,3},{2,0},{3,1},{4,6},{5,7},{6,4},{7,5},{8,10},{9,11},{10,... | collective-permute-start | bytes 393224 | tf_op jit(solution)/shard_map/ppermute | solution.py:475
  86.0 1.1 %copy-start.10 = (bf16[128,1024]{1,0:T(8,128)(2,1)}, bf16[128,1024]{1,0:T(8,128)(2,1)S(1)}, u32[]{:S(2)}) copy-start(bf16[128,1024]{1,0:T(8,128)(2,1)S(1)} %collective-permute-done.5.refs_3_) | copy-start | bytes 786436
  86.0 5.9 %copy-start.4 = (f32[1024]{0:T(1024)S(1)}, f32[1024]{0:T(1024)}, u32[]{:S(2)}) copy-start(f32[1024]{0:T(1024)} %param.19) | copy-start | bytes 12292
  86.0 5.9 %copy-start.5 = (s32[2]{0:T(128)S(1)}, s32[2]{0:T(128)}, u32[]{:S(2)}) copy-start(s32[2]{0:T(128)} %live_ref.1) | copy-start | bytes 28
  86.1 5.9 %collective-permute-start.33 = (bf16[256,256]{1,0:T(8,128)(2,1)S(1)}, bf16[256,256]{1,0:T(8,128)(2,1)S(1)}, u32[]{:S(2)}, u32[]{:S(2)}) collective-permute-start(bf16[256,256]{1,0:T(8,128)(2,1)S(1)} %get-tuple-element.45), channel_id=1, source_target_pairs={{0,3},{1,2},{2,1},{3,0},{4,7},{5,6},{6,5},{7,4},{8,11},{9,10},{10,... | collective-permute-start | bytes 393224 | tf_op jit(solution)/shard_map/ppermute | solution.py:475
  87.1 0.7 copy-start.11
  87.9 0.7 copy-start.12

commit v4 on v3

--- a/solution.py
+++ b/solution.py
@@ -352,7 +352,8 @@
         pltpu.SemaphoreType.DMA((2 * helpers,)),
         pltpu.SemaphoreType.DMA((helpers,)),
     ]
-    arrays = in_hbm([array for _, _, array in cands] + list(weights)[:-CORES])
+    arrays = [array if rel == helpers - 1 else in_hbm([array])[0] for rel, _, array in cands]
+    arrays += in_hbm(list(weights)[:-CORES])
     arrays += list(weights)[-CORES:] + in_hbm(prefixes)
     return kernel_call(body, shapes, [ANY] * len(arrays), scratch, flops=2 * total_rows * features * width)(*arrays)
 
@@ -411,7 +412,7 @@
         jax.ShapeDtypeStruct((features, width), weights[0].dtype),
         [ANY] * n_weights,
         [pltpu.SemaphoreType.DMA((n_weights * planes,))],
-    )(*in_hbm(weights))
+    )(*weights)
 
 
 def project_out(gated, weight, cands, live, vec, rows_block):

time: 94.7 us -> 93.8 us (level)
  local copies, waits for them, and re-layouts: 3.08 us -> 0.98 us
  Pallas kernels: 18.3 us -> 20.1 us
    unnamed x42 -> x24, local copies, waits for them, and re-layouts: 3.08 us -> 0.98 us
    pallas_call x1, Pallas kernels: 1.83 us -> 3.52 us  [assemble(): kernel_call(body, jax.ShapeDtypeStruct((features, width), weights[0].dtyp...]
  transfers between devices with their start and end apart: 34 -> 34, of which waited for: 14 -> 14; matrix products, arithmetic and copies ran while one was open for 0% -> 0% of each run, Pallas kernels for 15% -> 17%
where the time goes in v4:
time: 93.8 us; the launch traced here: 93.4 us
  waiting for transfers between devices  35.9 us (38%)
  starting transfers between devices  35.5 us (38%)
  Pallas kernels  20.1 us (21%)
  local copies, waits for them, and re-layouts  0.98 us (1%)
    ppermute x17, waiting for transfers between devices, to_peers(): lax.ppermute(pieces[rel], 'helper', [(at, at ^ rel) for at in range(helpe...  26 us
    ppermute x17, starting transfers between devices, to_peers(): lax.ppermute(pieces[rel], 'helper', [(at, at ^ rel) for at in range(helpe...  23.6 us
    ppermute x5, starting transfers between devices, to_plane(): lax.ppermute(array, 'group', [(at, at ^ CORES * turn) for at in range(gro...  7.1 us
    pallas_call x1, Pallas kernels, attend(): kernel_call(body, shapes, [ANY] * len(arrays), scratch, flops=2 * total_r...  6.52 us
    ppermute x5, waiting for transfers between devices, to_plane(): lax.ppermute(array, 'group', [(at, at ^ CORES * turn) for at in range(gro...  6.19 us
    pallas_call x2, Pallas kernels, norm_rows(): kernel_call(body, shapes, [VMEM] * (1 + len(arrays)), [], specs)  4.02 us
    ppermute x2, waiting for transfers between devices, everyone(): out.append((3, at * half, lax.ppermute(part, 'helper', pairs)))  3.67 us
    pallas_call x1, Pallas kernels, assemble(): kernel_call(body, jax.ShapeDtypeStruct((features, width), weights[0].dtyp...  3.52 us
  transfers between devices with their start and end apart: 34, of which 14 were waited for; matrix products, arithmetic and copies ran while one was open for 0% of the time, Pallas kernels for 17%

profile of v4, /device:TPU:0, one launch (start us, length us, event | category | flops | bytes accessed | tf_op | source)
XLA Modules:
  0.0 93.4 jit_solution(16782382091485662248)
XLA Ops:
  0.6 0.0 copy-start
  0.6 2.1 %shard_map.118 = (bf16[528,256]{1,0:T(8,128)(2,1)}, bf16[528,256]{1,0:T(8,128)(2,1)S(1)}, bf16[528,256]{1,0:T(8,128)(2,1)S(1)}, bf16[528,256]{1,0:T(8,128)(2,1)S(1)}) custom-call(s32[2]{0:T(128)} %users_ref.1, bf16[256,1024]{1,0:T(8,128)(2,1)} %bitcast.21, bf16[256,1024]{1,0:T(8,128)(2,1)} %bitcast.22), custom_call_target="tpu_custom_call" | custom-call | bytes 1 | tf_op jit(solution)/shard_map/pallas_call | solution.py:177
  2.8 3.0 %collective-permute-start.25 = (bf16[528,256]{1,0:T(8,128)(2,1)S(1)}, bf16[528,256]{1,0:T(8,128)(2,1)S(1)}, u32[]{:S(2)}, u32[]{:S(2)}) collective-permute-start(bf16[528,256]{1,0:T(8,128)(2,1)S(1)} %get-tuple-element.36), channel_id=1, source_target_pairs={{0,1},{1,0},{2,3},{3,2},{4,5},{5,4},{6,7},{7,6},{8,9},{9,8},{10,11... | collective-permute-start | bytes 811016 | tf_op jit(solution)/shard_map/ppermute | solution.py:476
  5.7 1.5 %collective-permute-start.26 = (bf16[528,256]{1,0:T(8,128)(2,1)S(1)}, bf16[528,256]{1,0:T(8,128)(2,1)S(1)}, u32[]{:S(2)}, u32[]{:S(2)}) collective-permute-start(bf16[528,256]{1,0:T(8,128)(2,1)S(1)} %get-tuple-element.37), channel_id=1, source_target_pairs={{0,2},{1,3},{2,0},{3,1},{4,6},{5,7},{6,4},{7,5},{8,10},{9,11},{10,... | collective-permute-start | bytes 811016 | tf_op jit(solution)/shard_map/ppermute | solution.py:476
  7.2 1.0 %shard_map.117 = (bf16[1,32,1024]{2,1,0:T(8,128)(2,1)S(1)}, bf16[1,32,1024]{2,1,0:T(8,128)(2,1)S(1)}, bf16[1,32,1024]{2,1,0:T(8,128)(2,1)S(1)}, bf16[1,32,1024]{2,1,0:T(8,128)(2,1)S(1)}) custom-call(bf16[32,4096]{1,0:T(8,128)(2,1)} %refs_0_.3), custom_call_target="tpu_custom_call" | custom-call | bytes 1 | tf_op jit(solution)/shard_map/pallas_call | solution.py:151
  8.2 0.6 collective-permute-start.14
  8.8 0.1 collective-permute-start.15
  8.9 2.9 %collective-permute-start.16 = (bf16[32,1024]{1,0:T(8,128)(2,1)S(1)}, bf16[32,1024]{1,0:T(8,128)(2,1)S(1)}, u32[]{:S(2)}, u32[]{:S(2)}) collective-permute-start(bf16[32,1024]{1,0:T(8,128)(2,1)S(1)} %bitcast.18), channel_id=1, source_target_pairs={{0,3},{1,2},{2,1},{3,0},{4,7},{5,6},{6,5},{7,4},{8,11},{9,10},{10,... | collective-permute-start | bytes 196616 | tf_op jit(solution)/shard_map/ppermute | solution.py:476
  11.8 2.5 %collective-permute-done.14 = bf16[32,1024]{1,0:T(8,128)(2,1)S(1)} collective-permute-done((bf16[32,1024]{1,0:T(8,128)(2,1)S(1)}, bf16[32,1024]{1,0:T(8,128)(2,1)S(1)}, u32[]{:S(2)}, u32[]{:S(2)}) %collective-permute-start.14) | collective-permute-done | bytes 65568 | tf_op jit(solution)/shard_map/ppermute | solution.py:476
  14.3 1.8 %collective-permute-start = (bf16[32,1024]{1,0:T(8,128)(2,1)}, bf16[32,1024]{1,0:T(8,128)(2,1)S(1)}, u32[]{:S(2)}, u32[]{:S(2)}) collective-permute-start(bf16[32,1024]{1,0:T(8,128)(2,1)} %refs_0_.2), channel_id=1, source_target_pairs={{0,8},{4,12},{8,0},{12,4},{16,24},{20,28},{24,16},{28,20},{1,9},{5... | collective-permute-start | bytes 196616 | tf_op jit(solution)/shard_map/ppermute | solution.py:493
  16.1 0.3 collective-permute-done.15
  16.5 2.6 %collective-permute-start.1 = (bf16[32,1024]{1,0:T(8,128)(2,1)}, bf16[32,1024]{1,0:T(8,128)(2,1)S(1)}, u32[]{:S(2)}, u32[]{:S(2)}) collective-permute-start(bf16[32,1024]{1,0:T(8,128)(2,1)} %refs_0_.2), channel_id=1, source_target_pairs={{0,16},{4,20},{8,24},{12,28},{16,0},{20,4},{24,8},{28,12},{1,17},{... | collective-permute-start | bytes 196616 | tf_op jit(solution)/shard_map/ppermute | solution.py:493
  19.1 1.3 %collective-permute-start.2 = (bf16[32,1024]{1,0:T(8,128)(2,1)}, bf16[32,1024]{1,0:T(8,128)(2,1)S(1)}, u32[]{:S(2)}, u32[]{:S(2)}) collective-permute-start(bf16[32,1024]{1,0:T(8,128)(2,1)} %refs_0_.2), channel_id=1, source_target_pairs={{0,24},{4,28},{8,16},{12,20},{16,8},{20,12},{24,0},{28,4},{1,25},{... | collective-permute-start | bytes 196616 | tf_op jit(solution)/shard_map/ppermute | solution.py:493
  20.4 0.0 collective-permute-done.refs_1_
  20.4 0.9 collective-permute-start.10
  21.3 1.9 %collective-permute-done.1.refs_2_ = bf16[32,1024]{1,0:T(8,128)(2,1)S(1)} collective-permute-done((bf16[32,1024]{1,0:T(8,128)(2,1)}, bf16[32,1024]{1,0:T(8,128)(2,1)S(1)}, u32[]{:S(2)}, u32[]{:S(2)}) %collective-permute-start.1) | collective-permute-done | bytes 65568 | tf_op jit(solution)/shard_map/ppermute | solution.py:493
  23.2 1.8 %collective-permute-start.11 = (bf16[256,1024]{1,0:T(8,128)(2,1)}, bf16[256,1024]{1,0:T(8,128)(2,1)S(1)}, u32[]{:S(2)}, u32[]{:S(2)}) collective-permute-start(bf16[256,1024]{1,0:T(8,128)(2,1)} %bitcast.12), channel_id=1, source_target_pairs={{0,2},{1,3},{2,0},{3,1},{4,6},{5,7},{6,4},{7,5},{8,10},{9,11},{10,... | collective-permute-start | bytes 1572872 | tf_op jit(solution)/shard_map/ppermute | solution.py:476
  24.9 0.4 collective-permute-done.2.refs_3_
  25.3 2.1 %collective-permute-start.27 = (bf16[528,256]{1,0:T(8,128)(2,1)S(1)}, bf16[528,256]{1,0:T(8,128)(2,1)S(1)}, u32[]{:S(2)}, u32[]{:S(2)}) collective-permute-start(bf16[528,256]{1,0:T(8,128)(2,1)S(1)} %get-tuple-element.38), channel_id=1, source_target_pairs={{0,3},{1,2},{2,1},{3,0},{4,7},{5,6},{6,5},{7,4},{8,11},{9,10},{10,... | collective-permute-start | bytes 811016 | tf_op jit(solution)/shard_map/ppermute | solution.py:476
  27.5 0.8 collective-permute-start.20
  28.3 0.7 collective-permute-start.23
  28.9 9.8 %collective-permute-done.27.rest_19_ = bf16[528,256]{1,0:T(8,128)(2,1)S(1)} collective-permute-done((bf16[528,256]{1,0:T(8,128)(2,1)S(1)}, bf16[528,256]{1,0:T(8,128)(2,1)S(1)}, u32[]{:S(2)}, u32[]{:S(2)}) %collective-permute-start.27) | collective-permute-done | bytes 270368 | tf_op jit(solution)/shard_map/ppermute | solution.py:476
  38.8 0.6 collective-permute-start.18
  39.3 0.0 collective-permute-done.20.rest_12_
  39.3 0.0 collective-permute-start.17
  39.3 0.0 collective-permute-done.23
  39.3 0.1 copy-done.8
  39.4 1.3 %collective-permute-start.22 = (bf16[128,1024]{1,0:T(8,128)(2,1)}, bf16[128,1024]{1,0:T(8,128)(2,1)S(1)}, u32[]{:S(2)}, u32[]{:S(2)}) collective-permute-start(bf16[128,1024]{1,0:T(8,128)(2,1)} %collective-permute-done.20.rest_12_), channel_id=1, source_target_pairs={{8,0},{16,24},{12,4},{20,28},{9,1},{17,25},{13,5},{21,29},{10,2},{... | collective-permute-start | bytes 786440 | tf_op jit(solution)/shard_map/ppermute | solution.py:506
  40.7 0.0 copy-start.1
  40.7 0.8 copy-done.1
  41.6 3.9 %collective-permute-done.18.rest_10_ = bf16[128,1024]{1,0:T(8,128)(2,1)S(1)} collective-permute-done((bf16[128,1024]{1,0:T(8,128)(2,1)S(1)}, bf16[128,1024]{1,0:T(8,128)(2,1)S(1)}, u32[]{:S(2)}, u32[]{:S(2)}) %collective-permute-start.18) | collective-permute-done | bytes 262176 | tf_op jit(solution)/shard_map/ppermute | solution.py:493
  45.5 0.5 collective-permute-start.4
  46.0 0.0 collective-permute-done.10.refs_0_
  46.0 2.1 %collective-permute-start.6 = (bf16[128,1024]{1,0:T(8,128)(2,1)S(1)}, bf16[128,1024]{1,0:T(8,128)(2,1)S(1)}, u32[]{:S(2)}, u32[]{:S(2)}) collective-permute-start(bf16[128,1024]{1,0:T(8,128)(2,1)S(1)} %shard_map.113.refs_0_), channel_id=1, source_target_pairs={{0,2},{1,3},{2,0},{3,1},{4,6},{5,7},{6,4},{7,5},{8,10},{9,11},{10,... | collective-permute-start | bytes 786440 | tf_op jit(solution)/shard_map/ppermute | solution.py:476
  48.2 0.9 collective-permute-start.8
  49.0 2.2 %shard_map.116 = (bf16[128,1024]{1,0:T(8,128)(2,1)}, bf16[128,1024]{1,0:T(8,128)(2,1)}, bf16[128,1024]{1,0:T(8,128)(2,1)}, bf16[128,1024]{1,0:T(8,128)(2,1)}) custom-call(f32[1,1024]{1,0:T(1,128)} %bitcast.23, bf16[256,1024]{1,0:T(8,128)(2,1)S(1)} %collective-permute-done.10.refs_0_, bf16[256,1024]{1,0:T(8,128)(2,1)S(1)} %collective-permute-done.11.refs_1_), custom_call_target="tpu_custom_call" | custom-call | bytes 1 | tf_op jit(solution)/shard_map/pallas_call | solution.py:222
  51.3 0.5 collective-permute-start.19
  51.8 1.4 %collective-permute-done.4.refs_2_ = bf16[128,1024]{1,0:T(8,128)(2,1)S(1)} collective-permute-done((bf16[128,1024]{1,0:T(8,128)(2,1)S(1)}, bf16[128,1024]{1,0:T(8,128)(2,1)S(1)}, u32[]{:S(2)}, u32[]{:S(2)}) %collective-permute-start.4) | collective-permute-done | bytes 262176 | tf_op jit(solution)/shard_map/ppermute | solution.py:476
  53.2 1.3 %collective-permute-start.12 = (bf16[128,1024]{1,0:T(8,128)(2,1)}, bf16[128,1024]{1,0:T(8,128)(2,1)S(1)}, u32[]{:S(2)}, u32[]{:S(2)}) collective-permute-start(bf16[128,1024]{1,0:T(8,128)(2,1)} %get-tuple-element.27.rest_2_), channel_id=1, source_target_pairs={{0,2},{1,3},{2,0},{3,1},{4,6},{5,7},{6,4},{7,5},{8,10},{9,11},{10,... | collective-permute-start | bytes 786440 | tf_op jit(solution)/shard_map/ppermute | solution.py:489
  54.5 2.6 %collective-permute-done.6.refs_4_ = bf16[128,1024]{1,0:T(8,128)(2,1)S(1)} collective-permute-done((bf16[128,1024]{1,0:T(8,128)(2,1)S(1)}, bf16[128,1024]{1,0:T(8,128)(2,1)S(1)}, u32[]{:S(2)}, u32[]{:S(2)}) %collective-permute-start.6) | collective-permute-done | bytes 262176 | tf_op jit(solution)/shard_map/ppermute | solution.py:476
  57.1 0.5 collective-permute-start.13
  57.6 0.0 collective-permute-done.8.refs_6_
  57.6 0.0 collective-permute-start.24
  57.6 0.0 collective-permute-done.21.rest_13_
  57.6 0.5 collective-permute-start.3
  58.1 0.1 collective-permute-start.5
  58.2 1.8 %shard_map.115 = (bf16[128,1024]{1,0:T(8,128)(2,1)}, bf16[128,1024]{1,0:T(8,128)(2,1)}) custom-call(f32[1,1024]{1,0:T(1,128)} %bitcast.24, bf16[256,1024]{1,0:T(8,128)(2,1)S(1)} %bitcast.13), custom_call_target="tpu_custom_call" | custom-call | bytes 1 | tf_op jit(solution)/shard_map/pallas_call | solution.py:222
  60.0 2.7 %collective-permute-done.12.rest_6_ = bf16[128,1024]{1,0:T(8,128)(2,1)S(1)} collective-permute-done((bf16[128,1024]{1,0:T(8,128)(2,1)}, bf16[128,1024]{1,0:T(8,128)(2,1)S(1)}, u32[]{:S(2)}, u32[]{:S(2)}) %collective-permute-start.12) | collective-permute-done | bytes 262176 | tf_op jit(solution)/shard_map/ppermute | solution.py:489
  62.7 1.0 %collective-permute-done.13.rest_7_ = bf16[128,1024]{1,0:T(8,128)(2,1)S(1)} collective-permute-done((bf16[128,1024]{1,0:T(8,128)(2,1)}, bf16[128,1024]{1,0:T(8,128)(2,1)S(1)}, u32[]{:S(2)}, u32[]{:S(2)}) %collective-permute-start.13) | collective-permute-done | bytes 262176 | tf_op jit(solution)/shard_map/ppermute | solution.py:489
  63.7 0.0 copy-start.2
  63.7 6.5 %shard_map.119 = (f32[1024,256]{1,0:T(8,128)S(1)}, f32[1024,256]{1,0:T(8,128)S(1)}, f32[16,128]{1,0:T(8,128)S(1)}) custom-call(bf16[128,1024]{1,0:T(8,128)(2,1)} %get-tuple-element.25.rest_0_, bf16[128,1024]{1,0:T(8,128)(2,1)} %get-tuple-element.26.rest_1_, bf16[128,1024]{1,0:T(8,128)(2,1)} %get-tuple-element.27.rest_2_, ...), custom_call_target="tpu_custom_call" | custom-call | flops 2147483648 | bytes 1 | tf_op jit(solution)/shard_map/pallas_call | solution.py:358
  70.2 0.6 collective-permute-start.28
  70.8 3.2 %collective-permute-done.28.rest_1_ = f32[16,128]{1,0:T(8,128)S(1)} collective-permute-done((f32[16,128]{1,0:T(8,128)S(1)}, f32[16,128]{1,0:T(8,128)S(1)}, u32[]{:S(2)}, u32[]{:S(2)}) %collective-permute-start.28) | collective-permute-done | bytes 8224 | tf_op jit(solution)/shard_map/ppermute | solution.py:476
  74.0 1.4 %collective-permute-start.29 = (f32[16,128]{1,0:T(8,128)S(1)}, f32[16,128]{1,0:T(8,128)S(1)}, u32[]{:S(2)}, u32[]{:S(2)}) collective-permute-start(f32[16,128]{1,0:T(8,128)S(1)} %get-tuple-element.41.rest_0_), channel_id=1, source_target_pairs={{0,2},{1,3},{2,0},{3,1},{4,6},{5,7},{6,4},{7,5},{8,10},{9,11},{10,... | collective-permute-start | bytes 24584 | tf_op jit(solution)/shard_map/ppermute | solution.py:476
  75.4 2.3 %collective-permute-done.29.rest_2_ = f32[16,128]{1,0:T(8,128)S(1)} collective-permute-done((f32[16,128]{1,0:T(8,128)S(1)}, f32[16,128]{1,0:T(8,128)S(1)}, u32[]{:S(2)}, u32[]{:S(2)}) %collective-permute-start.29) | collective-permute-done | bytes 8224 | tf_op jit(solution)/shard_map/ppermute | solution.py:476
  77.6 1.8 %collective-permute-start.30 = (f32[16,128]{1,0:T(8,128)S(1)}, f32[16,128]{1,0:T(8,128)S(1)}, u32[]{:S(2)}, u32[]{:S(2)}) collective-permute-start(f32[16,128]{1,0:T(8,128)S(1)} %get-tuple-element.41.rest_0_), channel_id=1, source_target_pairs={{0,3},{1,2},{2,1},{3,0},{4,7},{5,6},{6,5},{7,4},{8,11},{9,10},{10,... | collective-permute-start | bytes 24584 | tf_op jit(solution)/shard_map/ppermute | solution.py:476
  79.4 2.8 %collective-permute-done.30.rest_3_ = f32[16,128]{1,0:T(8,128)S(1)} collective-permute-done((f32[16,128]{1,0:T(8,128)S(1)}, f32[16,128]{1,0:T(8,128)S(1)}, u32[]{:S(2)}, u32[]{:S(2)}) %collective-permute-start.30) | collective-permute-done | bytes 8224 | tf_op jit(solution)/shard_map/ppermute | solution.py:476
  82.2 0.6 shard_map.120
  82.8 0.6 collective-permute-start.31
  83.4 1.9 %collective-permute-start.32 = (bf16[256,256]{1,0:T(8,128)(2,1)S(1)}, bf16[256,256]{1,0:T(8,128)(2,1)S(1)}, u32[]{:S(2)}, u32[]{:S(2)}) collective-permute-start(bf16[256,256]{1,0:T(8,128)(2,1)S(1)} %get-tuple-element.44), channel_id=1, source_target_pairs={{0,2},{1,3},{2,0},{3,1},{4,6},{5,7},{6,4},{7,5},{8,10},{9,11},{10,... | collective-permute-start | bytes 393224 | tf_op jit(solution)/shard_map/ppermute | solution.py:476
  85.2 1.1 %collective-permute-start.33 = (bf16[256,256]{1,0:T(8,128)(2,1)S(1)}, bf16[256,256]{1,0:T(8,128)(2,1)S(1)}, u32[]{:S(2)}, u32[]{:S(2)}) collective-permute-start(bf16[256,256]{1,0:T(8,128)(2,1)S(1)} %get-tuple-element.45), channel_id=1, source_target_pairs={{0,3},{1,2},{2,1},{3,0},{4,7},{5,6},{6,5},{7,4},{8,11},{9,10},{10,... | collective-permute-start | bytes 393224 | tf_op jit(solution)/shard_map/ppermute | solution.py:476
  86.4 3.5 %shard_map.114.weight = bf16[1024,1024]{1,0:T(8,128)(2,1)S(1)} custom-call(bf16[128,1024]{1,0:T(8,128)(2,1)S(1)} %shard_map.113.refs_0_, bf16[128,1024]{1,0:T(8,128)(2,1)S(1)} %collective-permute-done.3.refs_1_, bf16[128,1024]{1,0:T(8,128)(2,1)S(1)} %collective-permute-done.4.refs_2_, bf16[128,1024]{1,0:T(8,128)(2,1)S(1)} %collective-permute-done.5.refs_3_, ...), custom_call_target="tpu_custom_call" | custom-call | bytes 1 | tf_op jit(solution)/shard_map/pallas_call | solution.py:410
  89.9 1.2 %collective-permute-done.33.rest_3_ = bf16[256,256]{1,0:T(8,128)(2,1)S(1)} collective-permute-done((bf16[256,256]{1,0:T(8,128)(2,1)S(1)}, bf16[256,256]{1,0:T(8,128)(2,1)S(1)}, u32[]{:S(2)}, u32[]{:S(2)}) %collective-permute-start.33) | collective-permute-done | bytes 131104 | tf_op jit(solution)/shard_map/ppermute | solution.py:476
  91.1 2.3 %shard_map.121 = (bf16[256,1024]{1,0:T(8,128)(2,1)}, f32[2,128]{1,0:T(2,128)}) custom-call(s32[2]{0:T(128)S(1)} %copy-done.4, f32[1,1024]{1,0:T(1,128)S(1)} %bitcast.17, bf16[256,1024]{1,0:T(8,128)(2,1)S(1)} %bitcast.14, bf16[1024,1024]{1,0:T(8,128)(2,1)S(1)} %shard_map.114.weight, bf16[256,256]{1,0:T(8,128)(2,1)S(1)} %get-tuple-element.42.rest_0_, ...), custom_call_target="tpu_custom_call" | custom-call | flops 536870912 | bytes 1 | tf_op jit(solution)/shard_map/pallas_call | solution.py:452
  (39 shorter events, 0.1 us)
Async XLA Ops:
  0.6 57.6 %copy-start = (bf16[2,128,1024]{2,1,0:T(8,128)(2,1)S(1)}, bf16[2,128,1024]{2,1,0:T(8,128)(2,1)}, u32[]{:S(2)}) copy-start(bf16[2,128,1024]{2,1,0:T(8,128)(2,1)} %param.10) | copy-start | bytes 1572868
  2.8 24.7 %collective-permute-start.25 = (bf16[528,256]{1,0:T(8,128)(2,1)S(1)}, bf16[528,256]{1,0:T(8,128)(2,1)S(1)}, u32[]{:S(2)}, u32[]{:S(2)}) collective-permute-start(bf16[528,256]{1,0:T(8,128)(2,1)S(1)} %get-tuple-element.36), channel_id=1, source_target_pairs={{0,1},{1,0},{2,3},{3,2},{4,5},{5,4},{6,7},{7,6},{8,9},{9,8},{10,11... | collective-permute-start | bytes 811016 | tf_op jit(solution)/shard_map/ppermute | solution.py:476
  5.7 22.5 %collective-permute-start.26 = (bf16[528,256]{1,0:T(8,128)(2,1)S(1)}, bf16[528,256]{1,0:T(8,128)(2,1)S(1)}, u32[]{:S(2)}, u32[]{:S(2)}) collective-permute-start(bf16[528,256]{1,0:T(8,128)(2,1)S(1)} %get-tuple-element.37), channel_id=1, source_target_pairs={{0,2},{1,3},{2,0},{3,1},{4,6},{5,7},{6,4},{7,5},{8,10},{9,11},{10,... | collective-permute-start | bytes 811016 | tf_op jit(solution)/shard_map/ppermute | solution.py:476
  8.2 6.1 %collective-permute-start.14 = (bf16[32,1024]{1,0:T(8,128)(2,1)S(1)}, bf16[32,1024]{1,0:T(8,128)(2,1)S(1)}, u32[]{:S(2)}, u32[]{:S(2)}) collective-permute-start(bf16[32,1024]{1,0:T(8,128)(2,1)S(1)} %bitcast.20), channel_id=1, source_target_pairs={{0,1},{1,0},{2,3},{3,2},{4,5},{5,4},{6,7},{7,6},{8,9},{9,8},{10,11... | collective-permute-start | bytes 196616 | tf_op jit(solution)/shard_map/ppermute | solution.py:476
  8.8 7.6 %collective-permute-start.15 = (bf16[32,1024]{1,0:T(8,128)(2,1)S(1)}, bf16[32,1024]{1,0:T(8,128)(2,1)S(1)}, u32[]{:S(2)}, u32[]{:S(2)}) collective-permute-start(bf16[32,1024]{1,0:T(8,128)(2,1)S(1)} %bitcast.19), channel_id=1, source_target_pairs={{0,2},{1,3},{2,0},{3,1},{4,6},{5,7},{6,4},{7,5},{8,10},{9,11},{10,... | collective-permute-start | bytes 196616 | tf_op jit(solution)/shard_map/ppermute | solution.py:476
  8.9 10.2 %collective-permute-start.16 = (bf16[32,1024]{1,0:T(8,128)(2,1)S(1)}, bf16[32,1024]{1,0:T(8,128)(2,1)S(1)}, u32[]{:S(2)}, u32[]{:S(2)}) collective-permute-start(bf16[32,1024]{1,0:T(8,128)(2,1)S(1)} %bitcast.18), channel_id=1, source_target_pairs={{0,3},{1,2},{2,1},{3,0},{4,7},{5,6},{6,5},{7,4},{8,11},{9,10},{10,... | collective-permute-start | bytes 196616 | tf_op jit(solution)/shard_map/ppermute | solution.py:476
  14.3 6.1 %collective-permute-start = (bf16[32,1024]{1,0:T(8,128)(2,1)}, bf16[32,1024]{1,0:T(8,128)(2,1)S(1)}, u32[]{:S(2)}, u32[]{:S(2)}) collective-permute-start(bf16[32,1024]{1,0:T(8,128)(2,1)} %refs_0_.2), channel_id=1, source_target_pairs={{0,8},{4,12},{8,0},{12,4},{16,24},{20,28},{24,16},{28,20},{1,9},{5... | collective-permute-start | bytes 196616 | tf_op jit(solution)/shard_map/ppermute | solution.py:493
  16.5 6.7 %collective-permute-start.1 = (bf16[32,1024]{1,0:T(8,128)(2,1)}, bf16[32,1024]{1,0:T(8,128)(2,1)S(1)}, u32[]{:S(2)}, u32[]{:S(2)}) collective-permute-start(bf16[32,1024]{1,0:T(8,128)(2,1)} %refs_0_.2), channel_id=1, source_target_pairs={{0,16},{4,20},{8,24},{12,28},{16,0},{20,4},{24,8},{28,12},{1,17},{... | collective-permute-start | bytes 196616 | tf_op jit(solution)/shard_map/ppermute | solution.py:493
  19.1 6.3 %collective-permute-start.2 = (bf16[32,1024]{1,0:T(8,128)(2,1)}, bf16[32,1024]{1,0:T(8,128)(2,1)S(1)}, u32[]{:S(2)}, u32[]{:S(2)}) collective-permute-start(bf16[32,1024]{1,0:T(8,128)(2,1)} %refs_0_.2), channel_id=1, source_target_pairs={{0,24},{4,28},{8,16},{12,20},{16,8},{20,12},{24,0},{28,4},{1,25},{... | collective-permute-start | bytes 196616 | tf_op jit(solution)/shard_map/ppermute | solution.py:493
  20.4 25.6 %collective-permute-start.10 = (bf16[256,1024]{1,0:T(8,128)(2,1)}, bf16[256,1024]{1,0:T(8,128)(2,1)S(1)}, u32[]{:S(2)}, u32[]{:S(2)}) collective-permute-start(bf16[256,1024]{1,0:T(8,128)(2,1)} %bitcast.11), channel_id=1, source_target_pairs={{0,1},{1,0},{2,3},{3,2},{4,5},{5,4},{6,7},{7,6},{8,9},{9,8},{10,11... | collective-permute-start | bytes 1572872 | tf_op jit(solution)/shard_map/ppermute | solution.py:476
  23.2 25.0 %collective-permute-start.11 = (bf16[256,1024]{1,0:T(8,128)(2,1)}, bf16[256,1024]{1,0:T(8,128)(2,1)S(1)}, u32[]{:S(2)}, u32[]{:S(2)}) collective-permute-start(bf16[256,1024]{1,0:T(8,128)(2,1)} %bitcast.12), channel_id=1, source_target_pairs={{0,2},{1,3},{2,0},{3,1},{4,6},{5,7},{6,4},{7,5},{8,10},{9,11},{10,... | collective-permute-start | bytes 1572872 | tf_op jit(solution)/shard_map/ppermute | solution.py:476
  25.3 13.4 %collective-permute-start.27 = (bf16[528,256]{1,0:T(8,128)(2,1)S(1)}, bf16[528,256]{1,0:T(8,128)(2,1)S(1)}, u32[]{:S(2)}, u32[]{:S(2)}) collective-permute-start(bf16[528,256]{1,0:T(8,128)(2,1)S(1)} %get-tuple-element.38), channel_id=1, source_target_pairs={{0,3},{1,2},{2,1},{3,0},{4,7},{5,6},{6,5},{7,4},{8,11},{9,10},{10,... | collective-permute-start | bytes 811016 | tf_op jit(solution)/shard_map/ppermute | solution.py:476
  27.5 36.2 %copy-start.5 = (bf16[128,1024]{1,0:T(8,128)(2,1)}, bf16[128,1024]{1,0:T(8,128)(2,1)S(1)}, u32[]{:S(2)}) copy-start(bf16[128,1024]{1,0:T(8,128)(2,1)S(1)} %pad_maximum_fusion.rest_8_) | copy-start | bytes 786436
  27.5 14.1 %copy-start.6 = (bf16[528,256]{1,0:T(8,128)(2,1)}, bf16[528,256]{1,0:T(8,128)(2,1)S(1)}, u32[]{:S(2)}) copy-start(bf16[528,256]{1,0:T(8,128)(2,1)S(1)} %collective-permute-done.25.rest_17_) | copy-start | bytes 811012
  27.5 11.8 %collective-permute-start.20 = (bf16[128,1024]{1,0:T(8,128)(2,1)S(1)}, bf16[128,1024]{1,0:T(8,128)(2,1)}, u32[]{:S(2)}, u32[]{:S(2)}) collective-permute-start(bf16[128,1024]{1,0:T(8,128)(2,1)S(1)} %pad_maximum_fusion.rest_8_), channel_id=1, source_target_pairs={{0,16},{4,20},{8,24},{12,28},{16,0},{20,4},{24,8},{28,12},{1,17},{... | collective-permute-start | bytes 786440 | tf_op jit(solution)/shard_map/ppermute | solution.py:493
  28.3 17.7 %copy-start.7 = (bf16[528,256]{1,0:T(8,128)(2,1)}, bf16[528,256]{1,0:T(8,128)(2,1)S(1)}, u32[]{:S(2)}) copy-start(bf16[528,256]{1,0:T(8,128)(2,1)S(1)} %collective-permute-done.26.rest_18_) | copy-start | bytes 811012
  28.3 11.1 %collective-permute-start.23 = (bf16[128,1024]{1,0:T(8,128)(2,1)S(1)}, bf16[128,1024]{1,0:T(8,128)(2,1)S(1)}, u32[]{:S(2)}, u32[]{:S(2)}) collective-permute-start(bf16[128,1024]{1,0:T(8,128)(2,1)S(1)} %pad_maximum_fusion.rest_8_), channel_id=1, source_target_pairs={{8,16},{16,8},{12,20},{20,12},{9,17},{17,9},{13,21},{21,13},{10,18... | collective-permute-start | bytes 786440 | tf_op jit(solution)/shard_map/ppermute | solution.py:504
  38.7 0.7 copy-start.8
  38.8 6.8 %collective-permute-start.18 = (bf16[128,1024]{1,0:T(8,128)(2,1)S(1)}, bf16[128,1024]{1,0:T(8,128)(2,1)S(1)}, u32[]{:S(2)}, u32[]{:S(2)}) collective-permute-start(bf16[128,1024]{1,0:T(8,128)(2,1)S(1)} %pad_maximum_fusion.rest_8_), channel_id=1, source_target_pairs={{0,8},{4,12},{8,0},{12,4},{16,24},{20,28},{24,16},{28,20},{1,9},{5... | collective-permute-start | bytes 786440 | tf_op jit(solution)/shard_map/ppermute | solution.py:493
  39.3 11.9 %collective-permute-start.17 = (bf16[128,1024]{1,0:T(8,128)(2,1)S(1)}, bf16[128,1024]{1,0:T(8,128)(2,1)}, u32[]{:S(2)}, u32[]{:S(2)}) collective-permute-start(bf16[128,1024]{1,0:T(8,128)(2,1)S(1)} %pad_maximum_fusion.rest_8_), channel_id=1, source_target_pairs={{0,4},{4,0},{8,12},{12,8},{16,20},{20,16},{24,28},{28,24},{1,5},{5... | collective-permute-start | bytes 786440 | tf_op jit(solution)/shard_map/ppermute | solution.py:496
  39.4 11.8 %collective-permute-start.22 = (bf16[128,1024]{1,0:T(8,128)(2,1)}, bf16[128,1024]{1,0:T(8,128)(2,1)S(1)}, u32[]{:S(2)}, u32[]{:S(2)}) collective-permute-start(bf16[128,1024]{1,0:T(8,128)(2,1)} %collective-permute-done.20.rest_12_), channel_id=1, source_target_pairs={{8,0},{16,24},{12,4},{20,28},{9,1},{17,25},{13,5},{21,29},{10,2},{... | collective-permute-start | bytes 786440 | tf_op jit(solution)/shard_map/ppermute | solution.py:506
  40.7 0.8 copy-start.1
  45.5 2.6 %copy-start.9 = (bf16[128,1024]{1,0:T(8,128)(2,1)}, bf16[128,1024]{1,0:T(8,128)(2,1)S(1)}, u32[]{:S(2)}) copy-start(bf16[128,1024]{1,0:T(8,128)(2,1)S(1)} %collective-permute-done.18.rest_10_) | copy-start | bytes 786436
  45.5 7.6 %collective-permute-start.4 = (bf16[128,1024]{1,0:T(8,128)(2,1)S(1)}, bf16[128,1024]{1,0:T(8,128)(2,1)S(1)}, u32[]{:S(2)}, u32[]{:S(2)}) collective-permute-start(bf16[128,1024]{1,0:T(8,128)(2,1)S(1)} %shard_map.113.refs_0_), channel_id=1, source_target_pairs={{0,1},{1,0},{2,3},{3,2},{4,5},{5,4},{6,7},{7,6},{8,9},{9,8},{10,11... | collective-permute-start | bytes 786440 | tf_op jit(solution)/shard_map/ppermute | solution.py:476
  46.0 11.1 %collective-permute-start.6 = (bf16[128,1024]{1,0:T(8,128)(2,1)S(1)}, bf16[128,1024]{1,0:T(8,128)(2,1)S(1)}, u32[]{:S(2)}, u32[]{:S(2)}) collective-permute-start(bf16[128,1024]{1,0:T(8,128)(2,1)S(1)} %shard_map.113.refs_0_), channel_id=1, source_target_pairs={{0,2},{1,3},{2,0},{3,1},{4,6},{5,7},{6,4},{7,5},{8,10},{9,11},{10,... | collective-permute-start | bytes 786440 | tf_op jit(solution)/shard_map/ppermute | solution.py:476
  48.2 9.4 %collective-permute-start.8 = (bf16[128,1024]{1,0:T(8,128)(2,1)S(1)}, bf16[128,1024]{1,0:T(8,128)(2,1)S(1)}, u32[]{:S(2)}, u32[]{:S(2)}) collective-permute-start(bf16[128,1024]{1,0:T(8,128)(2,1)S(1)} %shard_map.113.refs_0_), channel_id=1, source_target_pairs={{0,3},{1,2},{2,1},{3,0},{4,7},{5,6},{6,5},{7,4},{8,11},{9,10},{10,... | collective-permute-start | bytes 786440 | tf_op jit(solution)/shard_map/ppermute | solution.py:476
  51.3 6.3 %collective-permute-start.21 = (bf16[128,1024]{1,0:T(8,128)(2,1)}, bf16[128,1024]{1,0:T(8,128)(2,1)S(1)}, u32[]{:S(2)}, u32[]{:S(2)}) collective-permute-start(bf16[128,1024]{1,0:T(8,128)(2,1)} %collective-permute-done.20.rest_12_), channel_id=1, source_target_pairs={{0,4},{4,0},{8,12},{12,8},{16,20},{20,16},{24,28},{28,24},{1,5},{5... | collective-permute-start | bytes 786440 | tf_op jit(solution)/shard_map/ppermute | solution.py:496
  51.3 6.8 %collective-permute-start.19 = (bf16[128,1024]{1,0:T(8,128)(2,1)}, bf16[128,1024]{1,0:T(8,128)(2,1)S(1)}, u32[]{:S(2)}, u32[]{:S(2)}) collective-permute-start(bf16[128,1024]{1,0:T(8,128)(2,1)} %copy-done.9), channel_id=1, source_target_pairs={{0,4},{4,0},{8,12},{12,8},{16,20},{20,16},{24,28},{28,24},{1,5},{5... | collective-permute-start | bytes 786440 | tf_op jit(solution)/shard_map/ppermute | solution.py:496
  53.2 9.5 %collective-permute-start.12 = (bf16[128,1024]{1,0:T(8,128)(2,1)}, bf16[128,1024]{1,0:T(8,128)(2,1)S(1)}, u32[]{:S(2)}, u32[]{:S(2)}) collective-permute-start(bf16[128,1024]{1,0:T(8,128)(2,1)} %get-tuple-element.27.rest_2_), channel_id=1, source_target_pairs={{0,2},{1,3},{2,0},{3,1},{4,6},{5,7},{6,4},{7,5},{8,10},{9,11},{10,... | collective-permute-start | bytes 786440 | tf_op jit(solution)/shard_map/ppermute | solution.py:489
  57.1 6.6 %collective-permute-start.13 = (bf16[128,1024]{1,0:T(8,128)(2,1)}, bf16[128,1024]{1,0:T(8,128)(2,1)S(1)}, u32[]{:S(2)}, u32[]{:S(2)}) collective-permute-start(bf16[128,1024]{1,0:T(8,128)(2,1)} %get-tuple-element.30.rest_5_), channel_id=1, source_target_pairs={{0,1},{1,0},{2,3},{3,2},{4,5},{5,4},{6,7},{7,6},{8,9},{9,8},{10,11... | collective-permute-start | bytes 786440 | tf_op jit(solution)/shard_map/ppermute | solution.py:489
  57.6 6.1 %collective-permute-start.24 = (bf16[128,1024]{1,0:T(8,128)(2,1)S(1)}, bf16[128,1024]{1,0:T(8,128)(2,1)S(1)}, u32[]{:S(2)}, u32[]{:S(2)}) collective-permute-start(bf16[128,1024]{1,0:T(8,128)(2,1)S(1)} %broadcast_select_fusion.rest_14_), channel_id=1, source_target_pairs={{0,4},{4,0},{8,12},{12,8},{16,20},{20,16},{24,28},{28,24},{1,5},{5... | collective-permute-start | bytes 786440 | tf_op jit(solution)/shard_map/ppermute | solution.py:496
  57.6 6.1 %copy-start.10 = (bf16[128,1024]{1,0:T(8,128)(2,1)}, bf16[128,1024]{1,0:T(8,128)(2,1)S(1)}, u32[]{:S(2)}) copy-start(bf16[128,1024]{1,0:T(8,128)(2,1)S(1)} %collective-permute-done.21.rest_13_) | copy-start | bytes 786436
  57.6 25.8 %collective-permute-start.3 = (bf16[128,1024]{1,0:T(8,128)(2,1)S(1)}, bf16[128,1024]{1,0:T(8,128)(2,1)S(1)}, u32[]{:S(2)}, u32[]{:S(2)}) collective-permute-start(bf16[128,1024]{1,0:T(8,128)(2,1)S(1)} %shard_map.113.refs_0_), channel_id=1, source_target_pairs={{0,4},{4,0},{8,12},{12,8},{16,20},{20,16},{24,28},{28,24},{1,5},{5... | collective-permute-start | bytes 786440 | tf_op jit(solution)/shard_map/ppermute | solution.py:496
  58.1 5.6 %copy-start.11 = (bf16[128,1024]{1,0:T(8,128)(2,1)}, bf16[128,1024]{1,0:T(8,128)(2,1)S(1)}, u32[]{:S(2)}) copy-start(bf16[128,1024]{1,0:T(8,128)(2,1)S(1)} %collective-permute-done.19.rest_11_) | copy-start | bytes 786436
  58.1 27.1 %collective-permute-start.5 = (bf16[128,1024]{1,0:T(8,128)(2,1)S(1)}, bf16[128,1024]{1,0:T(8,128)(2,1)S(1)}, u32[]{:S(2)}, u32[]{:S(2)}) collective-permute-start(bf16[128,1024]{1,0:T(8,128)(2,1)S(1)} %collective-permute-done.4.refs_2_), channel_id=1, source_target_pairs={{0,4},{4,0},{8,12},{12,8},{16,20},{20,16},{24,28},{28,24},{1,5},{5... | collective-permute-start | bytes 786440 | tf_op jit(solution)/shard_map/ppermute | solution.py:496
  62.7 23.7 %collective-permute-start.7 = (bf16[128,1024]{1,0:T(8,128)(2,1)S(1)}, bf16[128,1024]{1,0:T(8,128)(2,1)S(1)}, u32[]{:S(2)}, u32[]{:S(2)}) collective-permute-start(bf16[128,1024]{1,0:T(8,128)(2,1)S(1)} %collective-permute-done.6.refs_4_), channel_id=1, source_target_pairs={{0,4},{4,0},{8,12},{12,8},{16,20},{20,16},{24,28},{28,24},{1,5},{5... | collective-permute-start | bytes 786440 | tf_op jit(solution)/shard_map/ppermute | solution.py:496
  63.7 22.7 %collective-permute-start.9 = (bf16[128,1024]{1,0:T(8,128)(2,1)S(1)}, bf16[128,1024]{1,0:T(8,128)(2,1)S(1)}, u32[]{:S(2)}, u32[]{:S(2)}) collective-permute-start(bf16[128,1024]{1,0:T(8,128)(2,1)S(1)} %collective-permute-done.8.refs_6_), channel_id=1, source_target_pairs={{0,4},{4,0},{8,12},{12,8},{16,20},{20,16},{24,28},{28,24},{1,5},{5... | collective-permute-start | bytes 786440 | tf_op jit(solution)/shard_map/ppermute | solution.py:496
  63.7 18.5 %copy-start.2 = (f32[1024]{0:T(1024)S(1)}, f32[1024]{0:T(1024)}, u32[]{:S(2)}) copy-start(f32[1024]{0:T(1024)} %param.18) | copy-start | bytes 12292
  70.2 3.7 %collective-permute-start.28 = (f32[16,128]{1,0:T(8,128)S(1)}, f32[16,128]{1,0:T(8,128)S(1)}, u32[]{:S(2)}, u32[]{:S(2)}) collective-permute-start(f32[16,128]{1,0:T(8,128)S(1)} %get-tuple-element.41.rest_0_), channel_id=1, source_target_pairs={{0,1},{1,0},{2,3},{3,2},{4,5},{5,4},{6,7},{7,6},{8,9},{9,8},{10,11... | collective-permute-start | bytes 24584 | tf_op jit(solution)/shard_map/ppermute | solution.py:476
  74.0 3.7 %collective-permute-start.29 = (f32[16,128]{1,0:T(8,128)S(1)}, f32[16,128]{1,0:T(8,128)S(1)}, u32[]{:S(2)}, u32[]{:S(2)}) collective-permute-start(f32[16,128]{1,0:T(8,128)S(1)} %get-tuple-element.41.rest_0_), channel_id=1, source_target_pairs={{0,2},{1,3},{2,0},{3,1},{4,6},{5,7},{6,4},{7,5},{8,10},{9,11},{10,... | collective-permute-start | bytes 24584 | tf_op jit(solution)/shard_map/ppermute | solution.py:476
  77.6 4.5 %collective-permute-start.30 = (f32[16,128]{1,0:T(8,128)S(1)}, f32[16,128]{1,0:T(8,128)S(1)}, u32[]{:S(2)}, u32[]{:S(2)}) collective-permute-start(f32[16,128]{1,0:T(8,128)S(1)} %get-tuple-element.41.rest_0_), channel_id=1, source_target_pairs={{0,3},{1,2},{2,1},{3,0},{4,7},{5,6},{6,5},{7,4},{8,11},{9,10},{10,... | collective-permute-start | bytes 24584 | tf_op jit(solution)/shard_map/ppermute | solution.py:476
  82.8 7.1 %collective-permute-start.31 = (bf16[256,256]{1,0:T(8,128)(2,1)S(1)}, bf16[256,256]{1,0:T(8,128)(2,1)S(1)}, u32[]{:S(2)}, u32[]{:S(2)}) collective-permute-start(bf16[256,256]{1,0:T(8,128)(2,1)S(1)} %get-tuple-element.43), channel_id=1, source_target_pairs={{0,1},{1,0},{2,3},{3,2},{4,5},{5,4},{6,7},{7,6},{8,9},{9,8},{10,11... | collective-permute-start | bytes 393224 | tf_op jit(solution)/shard_map/ppermute | solution.py:476
  83.4 6.6 %collective-permute-start.32 = (bf16[256,256]{1,0:T(8,128)(2,1)S(1)}, bf16[256,256]{1,0:T(8,128)(2,1)S(1)}, u32[]{:S(2)}, u32[]{:S(2)}) collective-permute-start(bf16[256,256]{1,0:T(8,128)(2,1)S(1)} %get-tuple-element.44), channel_id=1, source_target_pairs={{0,2},{1,3},{2,0},{3,1},{4,6},{5,7},{6,4},{7,5},{8,10},{9,11},{10,... | collective-permute-start | bytes 393224 | tf_op jit(solution)/shard_map/ppermute | solution.py:476
  85.2 5.9 %copy-start.3 = (f32[1024]{0:T(1024)S(1)}, f32[1024]{0:T(1024)}, u32[]{:S(2)}) copy-start(f32[1024]{0:T(1024)} %param.19) | copy-start | bytes 12292
  85.2 5.9 %copy-start.4 = (s32[2]{0:T(128)S(1)}, s32[2]{0:T(128)}, u32[]{:S(2)}) copy-start(s32[2]{0:T(128)} %live_ref.1) | copy-start | bytes 28
  85.2 5.9 %collective-permute-start.33 = (bf16[256,256]{1,0:T(8,128)(2,1)S(1)}, bf16[256,256]{1,0:T(8,128)(2,1)S(1)}, u32[]{:S(2)}, u32[]{:S(2)}) collective-permute-start(bf16[256,256]{1,0:T(8,128)(2,1)S(1)} %get-tuple-element.45), channel_id=1, source_target_pairs={{0,3},{1,2},{2,1},{3,0},{4,7},{5,6},{6,5},{7,4},{8,11},{9,10},{10,... | collective-permute-start | bytes 393224 | tf_op jit(solution)/shard_map/ppermute | solution.py:476
